TPU v7x, 128 devices: a whole 4x4x4 slice. The times are simulated.
128 devices in a mesh: zg: 2 (over x_lo), xy: 64 (over x_hi, y, z, core).
Axes of the slice: x: 4 (x_hi: 2, x_lo: 2; x = x_hi * 2 + x_lo), y: 4, z: 4, core: 2. Of those that a mesh axis runs over, the one named last changes fastest.
Arguments:
- charges: float32 [262144], P(('zg', 'xy')), may hold values from -12 to 12
- cells: int32 [8, 262144], P(None, ('zg', 'xy')), may hold values from 0 to 786431
- splines: float32 [8, 262144], P(None, ('zg', 'xy')), may hold values from 0.05 to 1
- counts: int32 [128], P(('zg', 'xy')), may hold values from 1024 to 2048, as said below
- green: bfloat16 [512, 4, 384, 384], P(('zg', 'xy')), may hold values from -0.3125 to 0.3125
Outputs:
- potential: float32 [384, 512, 512], P(('zg', 'xy'))
Inputs may be any that keep to these rules, and one draw needn't show every extreme that they name: `counts`: some device has all 2048 slots live in every draw.
All inputs are finite; a program needn't handle non-finite values.
Results may differ from a plain program's by a relative error of at most 0.0041.
Values may be sent and summed in bfloat16 or wider, within the bound.
No kernel may reach another device: no remote copies, remote signals or barrier semaphores. Data moves between devices by JAX's collectives and lax.ppermute only.
A program may use at most 64 MiB of HBM per device.

v0:
```python
import math

import jax
import jax.numpy as jnp
from jax import lax
from jax.sharding import PartitionSpec as P

NX = 512
NY = 512
NZ = 384
KYB = 4


def tables(length):
    index = jnp.arange(length, dtype=jnp.int32)
    product = index[:, None] * index[None, :] % length
    angle = product.astype(jnp.float32) * (2.0 * math.pi / length)
    return (jnp.cos(angle), jnp.sin(angle))


def shards(charges, cells, splines, counts, green):
    groups = lax.axis_size("zg")
    rows = lax.axis_size("xy")
    slab = NZ // (groups * rows)
    slots = charges.shape[0]
    live = (jnp.arange(slots, dtype=jnp.int32) < counts[0]).astype(jnp.float32)
    values = splines * (charges * live)[None, :]
    density = (
        jnp.zeros((slab * NX * NY,), jnp.float32).at[cells.reshape(-1)].add(values.reshape(-1))
    )
    density = density.reshape(slab, NX, NY)
    cos_y, sin_y = tables(NY)
    cos_x, sin_x = tables(NX)
    scale = 1.0 / math.sqrt(NX * NY)
    forward_y = jnp.stack([cos_y, -sin_y], axis=1)
    along = jnp.einsum("zxy,yev->zxev", density, forward_y, precision=lax.Precision.HIGHEST)
    forward_x = jnp.stack(
        [jnp.stack([cos_x, sin_x], axis=1), jnp.stack([-sin_x, cos_x], axis=1)], axis=0
    )
    spectrum = (
        jnp.einsum("cuex,zxev->zcuv", forward_x, along, precision=lax.Precision.HIGHEST) * scale
    ).astype(jnp.bfloat16)
    pencil = lax.all_to_all(spectrum, ("zg", "xy"), split_axis=2, concat_axis=0, tiled=True)
    depth, parts, waves, width = pencil.shape
    blocks = pencil.reshape(depth, parts, waves, KYB, width // KYB)
    mixed = jnp.einsum("abzw,wcabj->zcabj", green, blocks, preferred_element_type=jnp.float32)
    returned = lax.all_to_all(
        mixed.reshape(depth, parts, waves, width).astype(jnp.bfloat16),
        ("zg", "xy"),
        split_axis=0,
        concat_axis=2,
        tiled=True,
    )
    inverse_x = jnp.stack(
        [jnp.stack([cos_x, -sin_x], axis=1), jnp.stack([sin_x, cos_x], axis=1)], axis=1
    )
    upper_x = inverse_x.astype(jnp.bfloat16)
    lower_x = (inverse_x - upper_x.astype(jnp.float32)).astype(jnp.bfloat16)
    middle = jnp.einsum("xceu,zeuv->zxcv", upper_x, returned, preferred_element_type=jnp.float32)
    middle = middle + jnp.einsum(
        "xceu,zeuv->zxcv", lower_x, returned, preferred_element_type=jnp.float32
    )
    inverse_y = jnp.stack([cos_y, -sin_y], axis=0)
    potential = (
        jnp.einsum("zxcv,cvy->zxy", middle, inverse_y, precision=lax.Precision.HIGHEST) * scale
    )
    return potential


def solution(mesh):
    in_specs = (
        P(("zg", "xy")),
        P(None, ("zg", "xy")),
        P(None, ("zg", "xy")),
        P(("zg", "xy")),
        P(("zg", "xy"), None, None, None),
    )
    out_specs = P(("zg", "xy"), None, None)
    return jax.shard_map(shards, mesh=mesh, in_specs=in_specs, out_specs=out_specs, check_vma=False)
```

profile of v0, /device:TPU:1, one launch (start us, length us, event | category | flops | bytes accessed | tf_op | source)
XLA Modules:
  0.0 296.6 jit_solution(15891612420639336365)
XLA Ops:
  0.0 0.0 copy-start.9
  0.0 0.0 copy-start.7
  0.0 0.0 copy-start.8
  0.0 5.0 %fusion.51 = (f32[512,1,512]{2,0,1:T(8,128)}, f32[512,1,512]{2,0,1:T(8,128)}) fusion(), kind=kLoop, calls=%fused_computation.61 | loop fusion | flops 3670016 | bytes 2097152 | tf_op jit(solution)/shard_map/sin | solution.py:18
  5.0 4.6 %fusion.53 = f32[512,1,512]{2,0,1:T(8,128)} fusion(), kind=kLoop, calls=%fused_computation.63 | loop fusion | flops 3932160 | bytes 1048576 | tf_op jit(solution)/shard_map/neg | solution.py:35
  10.2 0.0 copy-done.9
  10.3 0.0 copy-done.7
  10.3 0.0 copy-done.8
  10.3 0.1 copy.48
  10.4 0.1 compare_select_fusion
  10.5 86.7 %scatter_custom_fusion = f32[786432]{0:T(1024)S(1)} fusion(s32[16384]{0:T(1024)S(1)} %bitcast.109, f32[16384]{0:T(1024)S(1)} %bitcast.108, f32[]{:T(128)} %constant.24.clone.1), kind=kCustom, calls=%fused_computation.45 | custom fusion | flops 16384 | bytes 3145732 | tf_op jit(solution)/shard_map/scatter-add | solution.py:29
  97.2 2.3 reshape.202
  99.5 0.0 copy-start
  99.5 0.0 copy-start.1
  99.5 0.0 copy-start.2
  99.5 6.1 %fusion.35 = (f32[512,1,2,512]{3,0,2,1:T(8,128)}, f32[1,512,2,512]{3,1,2,0:T(8,128)S(1)}, f32[1,512,2,512]{3,1,2,0:T(8,128)S(1)}, f32[512,1,2,512]{3,0,2,1:T(8,128)}) fusion(f32[512,1,512]{2,0,1:T(8,128)} %fusion.53, f32[512,1,512]{2,0,1:T(8,128)} %get-tuple-element.12, f32[512,1,512]{2,0,1:T(8,128)} %get-tuple-element.11), kind=kLoop, calls=%fused_computation.38 | loop fusion | flops 2097152 | bytes 11534336 | tf_op jit(solution)/shard_map/stack | solution.py:54
  105.6 0.0 copy-done
  105.6 0.0 copy-done.1
  105.6 0.0 copy-done.2
  105.6 10.1 %fusion.12 = f32[3,512,2,512]{1,3,2,0:T(8,128)S(1)} fusion(f32[3,512,512,1]{2,1,0,3:T(8,128)S(1)} %copy-done, f32[512,1,512]{2,0,1:T(8,128)S(1)} %copy-done.1, f32[512,1,512]{2,0,1:T(8,128)S(1)} %copy-done.2), kind=kOutput, calls=%fused_computation.19 | convolution fusion | flops 9664200704 | bytes 11534336 | tf_op jit(solution)/shard_map/zxy,yev->zxev/dot_general | solution.py:36
  115.8 22.1 %fusion.11 = bf16[3,2,512,512]{2,3,1,0:T(8,128)(2,1)} fusion(f32[1,512,2,512]{3,1,2,0:T(8,128)S(1)} %get-tuple-element.6, f32[1,512,2,512]{3,1,2,0:T(8,128)S(1)} %get-tuple-element.9, f32[3,512,2,512]{1,3,2,0:T(8,128)S(1)} %fusion.12), kind=kOutput, calls=%fused_computation.17 | convolution fusion | flops 19331547136 | bytes 13631488 | tf_op jit(solution)/shard_map/cuex,zxev->zcuv/dot_general | solution.py:41
  137.8 7.3 %copy.22 = bf16[3,2,512,512]{3,1,0,2:T(2,128)(2,1)S(1)} copy(bf16[3,2,512,512]{2,3,1,0:T(8,128)(2,1)} %fusion.11) | data formatting | bytes 6291456 | tf_op jit(solution)/shard_map/convert_element_type | solution.py:42
  145.2 53.2 %all_to_all.33 = bf16[3,2,512,512]{3,1,0,2:T(2,128)(2,1)S(1)} all-to-all(bf16[3,2,512,512]{3,1,0,2:T(2,128)(2,1)S(1)} %copy.22), channel_id=1, replica_groups=mesh['zg'=2,'xy'=64] {'zg','xy'}, dimensions={2} | all-to-all | bytes 6291456 | tf_op jit(solution)/shard_map/all_to_all | solution.py:43
  198.4 3.3 %copy.24 = bf16[128,3,2,4,512]{4,3,2,1,0:T(4,128)(2,1)} copy(bf16[128,3,2,4,512]{4,2,1,3,0:T(2,128)(2,1)S(1)} %bitcast.103) | data formatting | bytes 6291456 | tf_op jit(solution)/shard_map/all_to_all | solution.py:43
  201.6 4.0 %reshape.193 = bf16[384,2,4,4,128]{4,3,2,1,0:T(4,128)(2,1)S(1)} reshape(bf16[128,3,2,4,512]{4,3,2,1,0:T(4,128)(2,1)} %copy.24) | data formatting | bytes 6291456 | tf_op jit(solution)/shard_map/reshape | solution.py:45
  205.7 5.4 %convert_bitcast_fusion = bf16[384,2,4,4,128]{0,4,1,3,2:T(8,128)(2,1)S(1)} fusion(bf16[4,4,384,384]{3,2,1,0:T(8,128)(2,1)} %param.9, bf16[384,2,4,4,128]{4,3,2,1,0:T(4,128)(2,1)S(1)} %reshape.193), kind=kOutput, calls=%fused_computation.22 | convolution fusion | flops 1209532416 | bytes 11010048 | tf_op jit(solution)/shard_map/abzw,wcabj->zcabj/dot_general | solution.py:46
  211.1 0.4 copy.26
  211.5 4.4 %copy.27 = bf16[384,2,4,512]{3,2,1,0:T(4,128)(2,1)} copy(bf16[384,2,4,512]{0,3,2,1:T(8,128)(2,1)S(1)} %bitcast.104) | data formatting | bytes 6291456 | tf_op jit(solution)/shard_map/convert_element_type | solution.py:48
  215.8 4.8 %all-to-all-start.1 = ((bf16[384,2,4,512]{3,2,1,0:T(4,128)(2,1)}), bf16[384,2,4,512]{3,2,1,0:T(4,128)(2,1)S(1)}, u32[]{:S(2)}, u32[]{:S(2)}) async-start(bf16[384,2,4,512]{3,2,1,0:T(4,128)(2,1)} %copy.27), calls=%async_computation.1 | async-start | bytes 6291456 | tf_op jit(solution)/shard_map/all_to_all | solution.py:47
  220.6 5.0 %sine_negate_fusion = (f32[1,512,512]{2,1,0:T(8,128)}, f32[1,512,512]{2,1,0:T(8,128)}) fusion(), kind=kLoop, calls=%fused_computation.53 | loop fusion | flops 3932160 | bytes 2097152 | tf_op jit(solution)/shard_map/neg | solution.py:35
  225.6 36.8 %all-to-all-done.1 = bf16[384,2,4,512]{3,2,1,0:T(4,128)(2,1)S(1)} async-done(((bf16[384,2,4,512]{3,2,1,0:T(4,128)(2,1)}), bf16[384,2,4,512]{3,2,1,0:T(4,128)(2,1)S(1)}, u32[]{:S(2)}, u32[]{:S(2)}) %all-to-all-start.1) | async-done | bytes 3145760 | tf_op jit(solution)/shard_map/all_to_all | solution.py:47
  262.4 4.9 %copy.28 = bf16[3,2,128,4,512]{4,1,3,2,0:T(2,128)(2,1)} copy(bf16[3,2,128,4,512]{4,3,1,0,2:T(4,128)(2,1)S(1)} %bitcast.102) | data formatting | bytes 6291456 | tf_op jit(solution)/shard_map/all_to_all | solution.py:47
  267.3 7.0 %copy.37 = bf16[3,2,512,512,1]{2,3,1,4,0:T(8,128)(2,1)S(1)} copy(bf16[3,2,512,512,1]{3,1,2,0,4:T(2,128)(2,1)} %bitcast.105) | data formatting | bytes 6291456 | tf_op jit(solution)/shard_map/all_to_all | solution.py:47
  274.3 0.0 copy-start.5
  274.3 0.0 copy-start.6
  274.3 6.5 %fusion.22 = f32[3,512,512,2,1]{2,1,4,3,0:T(8,128)S(1)} fusion(bf16[3,2,512,512,1]{2,3,1,4,0:T(8,128)(2,1)S(1)} %copy.37, f32[512,1,2,512]{3,0,2,1:T(8,128)} %get-tuple-element.10, f32[512,1,2,512]{3,0,2,1:T(8,128)} %get-tuple-element.5), kind=kOutput, calls=%fused_computation.28 | convolution fusion | flops 3225419776 | bytes 13631488 | tf_op jit(solution)/shard_map/xceu,zeuv->zxcv/dot_general | solution.py:59
  280.8 0.0 copy-done.5
  280.8 0.0 copy-done.6
  280.8 0.0 copy-start.3
  280.9 0.0 copy-start.4
  280.9 3.5 %fusion.28 = f32[3,512,512,2,1]{2,1,4,3,0:T(8,128)S(1)} fusion(bf16[3,2,512,512,1]{2,3,1,4,0:T(8,128)(2,1)S(1)} %copy.37, f32[512,1,2,512]{3,0,2,1:T(8,128)S(1)} %copy-done.6, f32[512,1,2,512]{3,0,2,1:T(8,128)S(1)} %copy-done.5), kind=kOutput, calls=%fused_computation.33 | convolution fusion | flops 3226468352 | bytes 13631488 | tf_op jit(solution)/shard_map/xceu,zeuv->zxcv/dot_general | solution.py:60
  284.3 0.0 copy-done.3
  284.4 0.0 copy-done.4
  284.4 12.0 %bitcast_multiply_fusion.1 = f32[3,512,512]{2,1,0:T(8,128)} fusion(f32[1,512,512]{2,1,0:T(8,128)S(1)} %copy-done.3, f32[1,512,512]{2,1,0:T(8,128)S(1)} %copy-done.4, f32[3,512,512,2,1]{2,1,4,3,0:T(8,128)S(1)} %fusion.28, f32[3,512,512,2,1]{2,1,4,3,0:T(8,128)S(1)} %fusion.22), kind=kOutput, calls=%fused_computation.18 | convolution fusion | flops 9666560000 | bytes 17825792 | tf_op jit(solution)/shard_map/zxcv,cvy->zxy/dot_general | solution.py:65
  (3 shorter events, 0.0 us)
Async XLA Ops:
  0.0 10.2 %copy-start.9 = (f32[2048]{0:T(1024)S(1)}, f32[2048]{0:T(1024)}, u32[]{:S(2)}) copy-start(f32[2048]{0:T(1024)} %param.5) | copy-start | bytes 24580
  0.0 10.3 %copy-start.7 = (f32[8,2048]{1,0:T(8,128)S(1)}, f32[8,2048]{1,0:T(8,128)}, u32[]{:S(2)}) copy-start(f32[8,2048]{1,0:T(8,128)} %param.7) | copy-start | bytes 196612
  0.0 10.3 %copy-start.8 = (s32[8,2048]{1,0:T(8,128)S(1)}, s32[8,2048]{1,0:T(8,128)}, u32[]{:S(2)}) copy-start(s32[8,2048]{1,0:T(8,128)} %param.6) | copy-start | bytes 196612
  99.5 6.1 %copy-start = (f32[3,512,512,1]{2,1,0,3:T(8,128)S(1)}, f32[3,512,512,1]{2,1,0,3:T(8,128)}, u32[]{:S(2)}) copy-start(f32[3,512,512,1]{2,1,0,3:T(8,128)} %reshape.202) | copy-start | bytes 9437188
  99.5 6.1 %copy-start.1 = (f32[512,1,512]{2,0,1:T(8,128)S(1)}, f32[512,1,512]{2,0,1:T(8,128)}, u32[]{:S(2)}) copy-start(f32[512,1,512]{2,0,1:T(8,128)} %get-tuple-element.12) | copy-start | bytes 3145732
  99.5 6.1 %copy-start.2 = (f32[512,1,512]{2,0,1:T(8,128)S(1)}, f32[512,1,512]{2,0,1:T(8,128)}, u32[]{:S(2)}) copy-start(f32[512,1,512]{2,0,1:T(8,128)} %fusion.53) | copy-start | bytes 3145732
  215.8 46.5 %all-to-all-start.1 = ((bf16[384,2,4,512]{3,2,1,0:T(4,128)(2,1)}), bf16[384,2,4,512]{3,2,1,0:T(4,128)(2,1)S(1)}, u32[]{:S(2)}, u32[]{:S(2)}) async-start(bf16[384,2,4,512]{3,2,1,0:T(4,128)(2,1)} %copy.27), calls=%async_computation.1 | async-start | bytes 6291456 | tf_op jit(solution)/shard_map/all_to_all | solution.py:47
  274.3 6.5 %copy-start.5 = (f32[512,1,2,512]{3,0,2,1:T(8,128)S(1)}, f32[512,1,2,512]{3,0,2,1:T(8,128)}, u32[]{:S(2)}) copy-start(f32[512,1,2,512]{3,0,2,1:T(8,128)} %get-tuple-element.5) | copy-start | bytes 6291460
  274.3 6.5 %copy-start.6 = (f32[512,1,2,512]{3,0,2,1:T(8,128)S(1)}, f32[512,1,2,512]{3,0,2,1:T(8,128)}, u32[]{:S(2)}) copy-start(f32[512,1,2,512]{3,0,2,1:T(8,128)} %get-tuple-element.10) | copy-start | bytes 6291460
  280.8 3.5 %copy-start.3 = (f32[1,512,512]{2,1,0:T(8,128)S(1)}, f32[1,512,512]{2,1,0:T(8,128)}, u32[]{:S(2)}) copy-start(f32[1,512,512]{2,1,0:T(8,128)} %get-tuple-element.13) | copy-start | bytes 3145732
  280.9 3.5 %copy-start.4 = (f32[1,512,512]{2,1,0:T(8,128)S(1)}, f32[1,512,512]{2,1,0:T(8,128)}, u32[]{:S(2)}) copy-start(f32[1,512,512]{2,1,0:T(8,128)} %get-tuple-element.14) | copy-start | bytes 3145732
where the time goes:
time: 301 us; the launch traced here: 297 us
  other arithmetic  108 us (36%)
  matrix products  59.6 us (20%)
  blocking collectives  53.2 us (18%)
  waiting for transfers between devices  36.8 us (12%)
  local copies, waits for them, and re-layouts  33.7 us (11%)
  starting transfers between devices  4.78 us (2%)
    scatter-add x1, other arithmetic, shards(): jnp.zeros((slab * NX * NY,), jnp.float32).at[cells.reshape(-1)]  86.7 us
    all_to_all x1, blocking collectives, shards(): lax.all_to_all(spectrum, ('zg', 'xy'), split_axis=2, concat_axis=0, tiled...  53.2 us
    all_to_all x1, waiting for transfers between devices, shards(): lax.all_to_all(mixed.reshape(depth, parts, waves, width).astype(jnp.bfloa...  36.8 us
    dot_general x1, matrix products, shards(): jnp.einsum('cuex,zxev->zcuv', forward_x, along, precision=lax.Precision.H...  22.1 us
    dot_general x1, matrix products, shards(): jnp.einsum('zxcv,cvy->zxy', middle, inverse_y, precision=lax.Precision.HI...  12 us
    all_to_all x2, local copies, waits for them, and re-layouts, shards(): lax.all_to_all(mixed.reshape(depth, parts, waves, width).astype(jnp.bfloa...  11.9 us
    dot_general x1, matrix products, shards(): jnp.einsum('zxy,yev->zxev', density, forward_y, precision=lax.Precision.H...  10.1 us
    neg x2, other arithmetic, shards(): forward_y = jnp.stack([cos_y, -sin_y], axis=1)  9.62 us
  transfers between devices with their start and end apart: 1, of which 1 were waited for; matrix products, arithmetic and copies ran while one was open for 2% of the time, Pallas kernels for 0%

commit v1 on v0

v1 whole, which is shorter than its diff:
```python
import jax
import jax.numpy as jnp
import numpy as np
from jax import lax
from jax.experimental import pallas as pl
from jax.experimental.pallas import tpu as pltpu
from jax.sharding import PartitionSpec as P

NX = 512
NY = 512
NZ = 384
KYB = 4
AXES = ("zg", "xy")
DEV = 128
ZD = 3
NU = NX // DEV
HALF = NY // 2
LANE = 128
SLOTS = 2048
SPREAD = 8
TILES = SLOTS // LANE
ROWS = ZD * NX * NY // LANE
F32 = jnp.float32
BF16 = jnp.bfloat16


def split(table):
    high = table.astype(BF16)
    return high, (table - high.astype(np.float64)).astype(BF16)


def angles(left, right):
    return (np.outer(left, right) % NX) * (2.0 * np.pi / NX)


def tables():
    y = np.arange(NY)
    v = np.arange(HALF)
    scale = 1.0 / 512.0
    alternating = np.where(y % 2 == 0, 1.0, -1.0)
    forward_y = np.concatenate([np.cos(angles(y, v)), -np.sin(angles(y, v))], axis=1)
    forward_y[:, HALF] = alternating
    inverse_y = np.concatenate([np.cos(angles(v, y)), np.sin(angles(v, y))], axis=0)
    inverse_y[HALF] = -alternating
    x = np.arange(NX)
    a = angles(np.arange(NX), x).reshape(DEV, NU, NX)
    cos, sin = np.cos(a), np.sin(a)
    plain = np.stack([cos, -sin], axis=1).reshape(2 * NX, NX)
    turned = np.stack([sin, cos], axis=1).reshape(2 * NX, NX)
    return (
        *split(forward_y * scale),
        *split(plain),
        *split(turned),
        plain.T.astype(BF16),
        (inverse_y * scale).astype(BF16),
    )


def dot(a, b):
    return jnp.dot(a, b, preferred_element_type=F32)


def front_kernel(
    rows_hbm, cells, splines, charges, counts, yh_hbm, yl_hbm, ph_hbm, pl_hbm, th_hbm, tl_hbm, out, *scratch
):
    bins = scratch[:SPREAD]
    spikes = scratch[8:10]
    lanes, values, dens_hi, dens_lo, along_hi, along_lo = scratch[10:16]
    tabs = scratch[16:22]
    row_sem, tab_sem = scratch[22:24]
    row_of = scratch[24:]
    row_copies = [
        pltpu.make_async_copy(rows_hbm.at[pl.ds(t * 1024, 1024)], row_of[t], row_sem.at[t]) for t in range(TILES)
    ]
    for copy in row_copies:
        copy.start()
    sources = (yh_hbm, yl_hbm, ph_hbm, pl_hbm, th_hbm, tl_hbm)
    tab_copies = [pltpu.make_async_copy(s, d, tab_sem.at[i]) for i, (s, d) in enumerate(zip(sources, tabs))]
    for copy in tab_copies:
        copy.start()
    slot = lax.broadcasted_iota(jnp.int32, (1, SLOTS), 1)
    live = (slot < counts[0]).astype(F32)
    value = splines[...] * (charges[...] * live)
    lane_of = cells[...] & (LANE - 1)
    for t in range(TILES):
        lanes[t] = lane_of[:, t * LANE : (t + 1) * LANE]
        values[t] = value[:, t * LANE : (t + 1) * LANE]
    zeros = jnp.zeros((256, LANE), F32)

    def clear(i, carry):
        for b in bins:
            b[pl.ds(i * 256, 256), :] = zeros
        return carry

    lax.fori_loop(0, ROWS // 256, clear, 0)
    lane = lax.broadcasted_iota(jnp.int32, (SPREAD, LANE), 1)

    def build(spike, g):
        pick = jnp.full((SPREAD, LANE), g, jnp.int32)
        for t in range(TILES):
            at = jnp.take_along_axis(lanes[t], pick, axis=1)
            amount = jnp.take_along_axis(values[t], pick, axis=1)
            spike[t * SPREAD : (t + 1) * SPREAD, :] = jnp.where(lane == at, amount, 0.0)

    def apply(spike, g):
        for t in range(TILES):
            rows = [row_of[t][g + k * LANE] for k in range(SPREAD)]
            sums = [bins[k][pl.ds(rows[k], 1), :] + spike[pl.ds(t * SPREAD + k, 1), :] for k in range(SPREAD)]
            for k in range(SPREAD):
                bins[k][pl.ds(rows[k], 1), :] = sums[k]

    build(spikes[0], 0)
    for copy in row_copies:
        copy.wait()

    def body(h, carry):
        build(spikes[1], 2 * h + 1)
        apply(spikes[0], 2 * h)
        build(spikes[0], jnp.minimum(2 * h + 2, LANE - 1))
        apply(spikes[1], 2 * h + 1)
        return carry

    lax.fori_loop(0, LANE // 2, body, 0)
    for copy in tab_copies:
        copy.wait()
    yh, yl, ph, plo, th, tl = tabs
    first = lax.broadcasted_iota(jnp.int32, (2 * NX, LANE), 1) == 0

    def plane(z, carry):
        for j in range(NY // LANE):
            for q in range(4):
                at = pl.ds(z * (NX * 4) + q * 512 + j, 128, stride=4)
                total = bins[0][at, :]
                for b in bins[1:]:
                    total = total + b[at, :]
                high = total.astype(BF16)
                dens_hi[q * 128 : (q + 1) * 128, j * LANE : (j + 1) * LANE] = high
                dens_lo[q * 128 : (q + 1) * 128, j * LANE : (j + 1) * LANE] = (total - high.astype(F32)).astype(BF16)
        along = dot(dens_hi[...], yh[...]) + dot(dens_lo[...], yh[...]) + dot(dens_hi[...], yl[...])
        high = along.astype(BF16)
        along_hi[...] = high
        along_lo[...] = (along - high.astype(F32)).astype(BF16)
        re_hi, re_lo = along_hi[:, :HALF], along_lo[:, :HALF]
        im_hi, im_lo = along_hi[:, HALF:], along_lo[:, HALF:]
        p = dot(ph[...], re_hi) + dot(ph[...], re_lo) + dot(plo[...], re_hi)
        q = dot(th[...], im_hi) + dot(th[...], im_lo) + dot(tl[...], im_hi)
        p0, p1, q0, q1 = p[:, :LANE], p[:, LANE:], q[:, :LANE], q[:, LANE:]
        minus0 = jnp.where(first, 0.0, p0) - q0
        minus1 = p1 - q1
        parts = (
            p0 + jnp.where(first, 0.0, q0),
            p1 + q1,
            jnp.where(first, minus1, minus0),
            jnp.where(first, minus0, minus1),
        )
        for j, part in enumerate(parts):
            out[:, z, :, j * LANE : (j + 1) * LANE] = part.astype(BF16).reshape(DEV, 2 * NU, LANE)
        return carry

    lax.fori_loop(0, ZD, plane, 0)


def front(charges, cells, splines, counts, tabs):
    vmem = pl.BlockSpec(memory_space=pltpu.VMEM)
    smem = pl.BlockSpec(memory_space=pltpu.SMEM)
    hbm = pl.BlockSpec(memory_space=pl.ANY)
    rows = lax.shift_right_logical(cells, 7).reshape(SPREAD, TILES, LANE).transpose(1, 0, 2).reshape(-1)
    return pl.pallas_call(
        front_kernel,
        out_shape=jax.ShapeDtypeStruct((DEV, ZD, 2 * NU, NY), BF16),
        in_specs=[hbm, vmem, vmem, vmem, smem] + [hbm] * 6,
        out_specs=vmem,
        scratch_shapes=[pltpu.VMEM((ROWS, LANE), F32)] * SPREAD
        + [pltpu.VMEM((LANE, LANE), F32)] * 2
        + [pltpu.VMEM((TILES, SPREAD, LANE), jnp.int32), pltpu.VMEM((TILES, SPREAD, LANE), F32)]
        + [pltpu.VMEM((NX, NY), BF16)] * 4
        + [pltpu.VMEM(t.shape, BF16) for t in tabs]
        + [pltpu.SemaphoreType.DMA((TILES,)), pltpu.SemaphoreType.DMA((6,))]
        + [pltpu.SMEM((SPREAD * LANE,), jnp.int32)] * TILES,
        name="front",
    )(rows, cells, splines, charges.reshape(1, SLOTS), counts, *tabs)


BLOCK = (0, 1, 3, 2)


def green_kernel(spectrum, green, out, flat, sums, *rhs):
    for j in range(KYB):
        flat[...] = spectrum[:, :, j * LANE : (j + 1) * LANE].astype(F32).reshape(NZ * 2 * NU, LANE)
        for ul in range(NU):
            for c in range(2):
                rows = flat[pl.ds(c * NU + ul, NZ, stride=2 * NU), :]
                rhs[ul][j, :, c * LANE : (c + 1) * LANE] = rows.astype(BF16)
    first = lax.broadcasted_iota(jnp.int32, (NZ, 2 * LANE), 1) % LANE == 0
    for ul in range(NU):
        m0, m1, m2, m3 = (dot(green[ul, BLOCK[j]], rhs[ul][j]) for j in range(KYB))
        s2 = jnp.where(first, m3, m2)
        s3 = jnp.where(first, m2, m3)
        t0 = m0 + jnp.where(first, 0.0, s2)
        d0 = jnp.where(first, 0.0, m0) - s2
        t1 = m1 + s3
        d1 = m1 - s3
        re = pl.ds(ul, NZ, stride=2 * NU)
        im = pl.ds(NU + ul, NZ, stride=2 * NU)
        sums[0, re, :] = t0[:, :LANE]
        sums[0, im, :] = t0[:, LANE:]
        sums[1, re, :] = t1[:, :LANE]
        sums[1, im, :] = t1[:, LANE:]
        sums[2, re, :] = -d0[:, LANE:]
        sums[2, im, :] = d0[:, :LANE]
        sums[3, re, :] = -d1[:, LANE:]
        sums[3, im, :] = d1[:, :LANE]
    for j in range(KYB):
        out[:, :, j * LANE : (j + 1) * LANE] = sums[j].astype(BF16).reshape(NZ, 2 * NU, LANE)


def mix(pencil, green):
    vmem = pl.BlockSpec(memory_space=pltpu.VMEM)
    return pl.pallas_call(
        green_kernel,
        out_shape=jax.ShapeDtypeStruct((NZ, 2 * NU, NY), BF16),
        in_specs=[vmem, vmem],
        out_specs=vmem,
        scratch_shapes=[pltpu.VMEM((NZ * 2 * NU, LANE), F32), pltpu.VMEM((KYB, NZ * 2 * NU, LANE), F32)]
        + [pltpu.VMEM((KYB, NZ, 2 * LANE), BF16)] * NU,
        name="mix",
    )(pencil.reshape(NZ, 2 * NU, NY), green)


def back_kernel(mixed, inverse_x, inverse_y, out):
    middle = dot(inverse_x[...], mixed[:, 0].reshape(2 * NX, NY))
    out[0] = dot(middle.astype(BF16), inverse_y[...])


def back(returned, inverse_x, inverse_y):
    return pl.pallas_call(
        back_kernel,
        grid=(ZD,),
        out_shape=jax.ShapeDtypeStruct((ZD, NX, NY), F32),
        in_specs=[
            pl.BlockSpec((DEV, 1, 2 * NU, NY), lambda z: (0, z, 0, 0)),
            pl.BlockSpec((NX, 2 * NX), lambda z: (0, 0)),
            pl.BlockSpec((NY, NY), lambda z: (0, 0)),
        ],
        out_specs=pl.BlockSpec((1, NX, NY), lambda z: (z, 0, 0)),
        name="back",
    )(returned, inverse_x, inverse_y)


def shards(charges, cells, splines, counts, green):
    *forward, inverse_x, inverse_y = (jnp.asarray(t) for t in tables())
    spectrum = front(charges, cells, splines, counts, forward)
    pencil = lax.all_to_all(spectrum, AXES, split_axis=0, concat_axis=0, tiled=True)
    mixed = mix(pencil, green).reshape(DEV, ZD, 2 * NU, NY)
    returned = lax.all_to_all(mixed, AXES, split_axis=0, concat_axis=0, tiled=True)
    return back(returned, inverse_x, inverse_y)


def solution(mesh):
    in_specs = (
        P(AXES),
        P(None, AXES),
        P(None, AXES),
        P(AXES),
        P(AXES, None, None, None),
    )
    return jax.shard_map(
        shards, mesh=mesh, in_specs=in_specs, out_specs=P(AXES, None, None), check_vma=False
    )
```

time: 301 us -> 144 us (0.48); the launches traced: 297 us -> 144 us
  other arithmetic: 108 us -> 1.47 us
  matrix products: 59.6 us -> 0 us
  blocking collectives: 53.2 us -> 101 us
  Pallas kernels: 0 us -> 41.1 us
  waiting for transfers between devices: 36.8 us -> 0 us
  local copies, waits for them, and re-layouts: 33.7 us -> 0 us
  starting transfers between devices: 4.78 us -> 0 us
    scatter-add x1 -> x0, other arithmetic: 86.7 us -> none  [shards(): jnp.zeros((slab * NX * NY,), jnp.float32).at[cells.reshape(-1)]]
    dot_general x6 -> x0, matrix products: 59.6 us -> none  [the longest x1 22.1 us: shards(): jnp.einsum('cuex,zxev->zcuv', forward_x, along, precision=lax.Precision.H...]
    all_to_all x1 -> x2, blocking collectives: 53.2 us -> 101 us  [the longest x1 53.4 us: shards(): lax.all_to_all(spectrum, AXES, split_axis=0, concat_axis=0, tiled=True)]
    pallas_call x0 -> x3, Pallas kernels: none -> 41.1 us  [the longest x1 25.4 us: front(): pl.pallas_call(front_kernel, out_shape=jax.ShapeDtypeStruct((DEV, ZD, 2 *...]
    all_to_all x1 -> x0, waiting for transfers between devices: 36.8 us -> none  [shards(): lax.all_to_all(mixed.reshape(depth, parts, waves, width).astype(jnp.bfloa...]
    all_to_all x3 -> x0, local copies, waits for them, and re-layouts: 15.2 us -> none  [the longest x2 11.9 us: shards(): lax.all_to_all(mixed.reshape(depth, parts, waves, width).astype(jnp.bfloa...]
    convert_element_type x3 -> x0, local copies, waits for them, and re-layouts: 12.1 us -> none  [the longest x1 7.3 us: shards(): spectrum = (jnp.einsum('cuex,zxev->zcuv', forward_x, along, precision=lax...]
    neg x2 -> x0, other arithmetic: 9.62 us -> none  [shards(): forward_y = jnp.stack([cos_y, -sin_y], axis=1)]
  transfers between devices with their start and end apart: 1 -> 0, of which waited for: 1 -> 0; matrix products, arithmetic and copies ran while one was open for 2% -> 0% of each run, Pallas kernels for 0% -> 0%
where the time goes in v1:
time: 144 us
  blocking collectives  101 us (70%)
  Pallas kernels  41.1 us (29%)
  other arithmetic  1.47 us (1%)
    all_to_all x1, blocking collectives, shards(): lax.all_to_all(spectrum, AXES, split_axis=0, concat_axis=0, tiled=True)  53.4 us
    all_to_all x1, blocking collectives, shards(): lax.all_to_all(mixed, AXES, split_axis=0, concat_axis=0, tiled=True)  47.2 us
    pallas_call x1, Pallas kernels, front(): pl.pallas_call(front_kernel, out_shape=jax.ShapeDtypeStruct((DEV, ZD, 2 *...  25.4 us
    pallas_call x1, Pallas kernels, mix(): pl.pallas_call(green_kernel, out_shape=jax.ShapeDtypeStruct((NZ, 2 * NU,...  9.46 us
    pallas_call x1, Pallas kernels, back(): pl.pallas_call(back_kernel, grid=(ZD,), out_shape=jax.ShapeDtypeStruct((Z...  6.23 us

profile of v1, /device:TPU:1, one launch (start us, length us, event | category | flops | bytes accessed | tf_op | source)
XLA Modules:
  0.0 143.8 jit_solution(955740205367210368)
XLA Ops:
  0.7 1.5 %shift-right-logical_bitcast_fusion.rows_hbm = s32[16384]{0:T(1024)} fusion(s32[8,2048]{1,0:T(8,128)} %cells.1), kind=kLoop, calls=%fused_computation | loop fusion | flops 16384 | bytes 131072 | tf_op jit(solution)/shard_map/reshape | solution.py:167
  2.1 25.4 %front.1 = bf16[128,3,8,512]{3,2,1,0:T(8,128)(2,1)} custom-call(s32[16384]{0:T(1024)} %shift-right-logical_bitcast_fusion.rows_hbm, s32[8,2048]{1,0:T(8,128)} %cells.1, f32[8,2048]{1,0:T(8,128)} %splines.1, f32[1,2048]{1,0:T(1,128)} %bitcast.11, s32[1]{0:T(128)S(6)} %copy.14.counts, bf16[512,512]{1,0:T(8,128)(2,1)} %constant.18.clone.yh_hbm, ...), custom_call_target="tpu_custom_call" | custom-call | tf_op jit(solution)/shard_map/front/pallas_call | solution.py:168
  27.5 53.4 %all_to_all.10 = bf16[128,3,8,512]{3,2,1,0:T(8,128)(2,1)} all-to-all(bf16[128,3,8,512]{3,2,1,0:T(8,128)(2,1)} %front.1), channel_id=1, replica_groups=mesh['zg'=2,'xy'=64] {'zg','xy'}, dimensions={0} | all-to-all | bytes 6291456 | tf_op jit(solution)/shard_map/all_to_all | solution.py:253
  80.9 9.5 %mix.1 = bf16[384,8,512]{2,1,0:T(8,128)(2,1)} custom-call(bf16[384,8,512]{2,1,0:T(8,128)(2,1)} %bitcast.9, bf16[4,4,384,384]{3,2,1,0:T(8,128)(2,1)} %green.1), custom_call_target="tpu_custom_call" | custom-call | tf_op jit(solution)/shard_map/mix/pallas_call | solution.py:219
  90.4 47.2 %all_to_all.11.mixed = bf16[128,3,8,512]{3,2,1,0:T(8,128)(2,1)} all-to-all(bf16[128,3,8,512]{3,2,1,0:T(8,128)(2,1)} %bitcast.10), channel_id=1, replica_groups=mesh['zg'=2,'xy'=64] {'zg','xy'}, dimensions={0} | all-to-all | bytes 6291456 | tf_op jit(solution)/shard_map/all_to_all | solution.py:255
  137.5 6.2 %back.1 = f32[3,512,512]{2,1,0:T(8,128)} custom-call(bf16[128,3,8,512]{3,2,1,0:T(8,128)(2,1)} %all_to_all.11.mixed, bf16[512,1024]{1,0:T(8,128)(2,1)} %constant.24.clone.inverse_x, bf16[512,512]{1,0:T(8,128)(2,1)} %constant.25.clone.inverse_y), custom_call_target="tpu_custom_call" | custom-call | tf_op jit(solution)/shard_map/back/pallas_call | solution.py:236

commit v2 on v1

v2 whole, which is shorter than its diff:
```python
import functools

import jax
import jax.numpy as jnp
import numpy as np
from jax import lax
from jax.experimental import pallas as pl
from jax.experimental.pallas import tpu as pltpu
from jax.sharding import PartitionSpec as P

NX = 512
NY = 512
NZ = 384
KYB = 4
AXES = ("zg", "xy")
DEV = 128
ZD = 3
NU = NX // DEV
HALF = NY // 2
LANE = 128
SLOTS = 2048
SPREAD = 8
TILES = SLOTS // LANE
ROWS = ZD * NX * NY // LANE
F32 = jnp.float32
BF16 = jnp.bfloat16


def split(table):
    high = table.astype(BF16)
    return high, (table - high.astype(np.float64)).astype(BF16)


def angles(left, right):
    return (np.outer(left, right) % NX) * (2.0 * np.pi / NX)


def tables():
    y = np.arange(NY)
    v = np.arange(HALF)
    scale = 1.0 / 512.0
    alternating = np.where(y % 2 == 0, 1.0, -1.0)
    forward_y = np.concatenate([np.cos(angles(y, v)), -np.sin(angles(y, v))], axis=1)
    forward_y[:, HALF] = alternating
    inverse_y = np.concatenate([np.cos(angles(v, y)), np.sin(angles(v, y))], axis=0)
    inverse_y[HALF] = -alternating
    x = np.arange(NX)
    a = angles(np.arange(NX), x).reshape(DEV, NU, NX)
    cos, sin = np.cos(a), np.sin(a)
    plain = np.stack([cos, -sin], axis=1).reshape(2 * NX, NX)
    return (
        *split(forward_y * scale),
        *split(plain),
        plain.T.astype(BF16),
        *((scale * inverse_y.reshape(2, 2, LANE, NY)[:, j].reshape(2 * LANE, NY)).astype(BF16) for j in range(2)),
    )


def dot(a, b):
    return jnp.dot(a, b, preferred_element_type=F32)


def turn(q):
    whole = q.reshape(DEV, 2 * NU, LANE)
    real = lax.broadcasted_iota(jnp.int32, whole.shape, 1) < NU
    swapped = pltpu.roll(whole, NU, 1)
    return jnp.where(real, -swapped, swapped).reshape(2 * NX, LANE)


def along_x(high, low, re, im):
    tab_hi, tab_lo = high[0], low[0]
    data_hi, data_lo = high[1], low[1]
    p, q = (
        dot(tab_hi[...], data_hi[:, c]) + dot(tab_hi[...], data_lo[:, c]) + dot(tab_lo[...], data_hi[:, c])
        for c in (re, im)
    )
    return p, turn(q)


def store(out, z, plus, minus):
    out[:, z, :, :LANE] = plus.astype(BF16).reshape(DEV, 2 * NU, LANE)
    out[:, z, :, LANE:] = minus.astype(BF16).reshape(DEV, 2 * NU, LANE)


def front_kernel(
    rows_hbm, cells, splines, charges, counts, yh_hbm, yl_hbm, ph_hbm, pl_hbm, out, rest_hi, rest_lo, *scratch
):
    bins = scratch[:SPREAD]
    spikes = scratch[8:10]
    lanes, values, dens_hi, dens_lo, along_hi, along_lo = scratch[10:16]
    tabs = scratch[16:20]
    row_sem, tab_sem = scratch[20:22]
    row_of = scratch[22:]
    row_copies = [
        pltpu.make_async_copy(rows_hbm.at[pl.ds(t * 1024, 1024)], row_of[t], row_sem.at[t]) for t in range(TILES)
    ]
    for copy in row_copies:
        copy.start()
    sources = (yh_hbm, yl_hbm, ph_hbm, pl_hbm)
    tab_copies = [pltpu.make_async_copy(s, d, tab_sem.at[i]) for i, (s, d) in enumerate(zip(sources, tabs))]
    for copy in tab_copies:
        copy.start()
    slot = lax.broadcasted_iota(jnp.int32, (1, SLOTS), 1)
    live = (slot < counts[0]).astype(F32)
    value = splines[...] * (charges[...] * live)
    lane_of = cells[...] & (LANE - 1)
    for t in range(TILES):
        lanes[t] = lane_of[:, t * LANE : (t + 1) * LANE]
        values[t] = value[:, t * LANE : (t + 1) * LANE]
    zeros = jnp.zeros((256, LANE), F32)

    def clear(i, carry):
        for b in bins:
            b[pl.ds(i * 256, 256), :] = zeros
        return carry

    lax.fori_loop(0, ROWS // 256, clear, 0)
    lane = lax.broadcasted_iota(jnp.int32, (SPREAD, LANE), 1)

    def build(spike, g):
        pick = jnp.full((SPREAD, LANE), g, jnp.int32)
        for t in range(TILES):
            at = jnp.take_along_axis(lanes[t], pick, axis=1)
            amount = jnp.take_along_axis(values[t], pick, axis=1)
            spike[t * SPREAD : (t + 1) * SPREAD, :] = jnp.where(lane == at, amount, 0.0)

    def apply(spike, g):
        for t in range(TILES):
            rows = [row_of[t][g + k * LANE] for k in range(SPREAD)]
            sums = [bins[k][pl.ds(rows[k], 1), :] + spike[pl.ds(t * SPREAD + k, 1), :] for k in range(SPREAD)]
            for k in range(SPREAD):
                bins[k][pl.ds(rows[k], 1), :] = sums[k]

    build(spikes[0], 0)
    for copy in row_copies:
        copy.wait()

    def body(h, carry):
        build(spikes[1], 2 * h + 1)
        apply(spikes[0], 2 * h)
        build(spikes[0], jnp.minimum(2 * h + 2, LANE - 1))
        apply(spikes[1], 2 * h + 1)
        return carry

    lax.fori_loop(0, LANE // 2, body, 0)
    for copy in tab_copies:
        copy.wait()
    yh, yl, ph, plo = tabs
    first = lax.broadcasted_iota(jnp.int32, (2 * NX, LANE), 1) == 0

    def plane(z, carry):
        for j in range(NY // LANE):
            for q in range(4):
                at = pl.ds(z * (NX * 4) + q * 512 + j, 128, stride=4)
                total = bins[0][at, :]
                for b in bins[1:]:
                    total = total + b[at, :]
                high = total.astype(BF16)
                dens_hi[q * 128 : (q + 1) * 128, j * LANE : (j + 1) * LANE] = high
                dens_lo[q * 128 : (q + 1) * 128, j * LANE : (j + 1) * LANE] = (total - high.astype(F32)).astype(BF16)
        along = dot(dens_hi[...], yh[...]) + dot(dens_lo[...], yh[...]) + dot(dens_hi[...], yl[...])
        high = along.astype(BF16)
        along_hi[...] = high
        along_lo[...] = (along - high.astype(F32)).astype(BF16)
        p, q = along_x((ph, along_hi), (plo, along_lo), slice(0, LANE), slice(HALF, HALF + LANE))
        store(out, z, p + jnp.where(first, 0.0, q), jnp.where(first, 0.0, p) - q)
        for c, at in enumerate((LANE, HALF + LANE)):
            rest_hi[z, :, c * LANE : (c + 1) * LANE] = along_hi[:, at : at + LANE]
            rest_lo[z, :, c * LANE : (c + 1) * LANE] = along_lo[:, at : at + LANE]
        return carry

    lax.fori_loop(0, ZD, plane, 0)


def rest_kernel(rest_hi, rest_lo, ph, plo, out):
    p, q = along_x((ph, rest_hi.at[0]), (plo, rest_lo.at[0]), slice(0, LANE), slice(LANE, 2 * LANE))
    store(out, 0, p + q, p - q)


def rest(rest_hi, rest_lo, ph, plo):
    plane = pl.BlockSpec((1, NX, 2 * LANE), lambda z: (z, 0, 0))
    table = pl.BlockSpec((2 * NX, NX), lambda z: (0, 0))
    return pl.pallas_call(
        rest_kernel,
        grid=(ZD,),
        out_shape=jax.ShapeDtypeStruct((DEV, ZD, 2 * NU, 2 * LANE), BF16),
        in_specs=[plane, plane, table, table],
        out_specs=pl.BlockSpec((DEV, 1, 2 * NU, 2 * LANE), lambda z: (0, z, 0, 0)),
        name="rest",
    )(rest_hi, rest_lo, ph, plo)


def front(charges, cells, splines, counts, tabs):
    vmem = pl.BlockSpec(memory_space=pltpu.VMEM)
    smem = pl.BlockSpec(memory_space=pltpu.SMEM)
    hbm = pl.BlockSpec(memory_space=pl.ANY)
    rows = lax.shift_right_logical(cells, 7).reshape(SPREAD, TILES, LANE).transpose(1, 0, 2).reshape(-1)
    return pl.pallas_call(
        front_kernel,
        out_shape=(
            jax.ShapeDtypeStruct((DEV, ZD, 2 * NU, 2 * LANE), BF16),
            jax.ShapeDtypeStruct((ZD, NX, 2 * LANE), BF16),
            jax.ShapeDtypeStruct((ZD, NX, 2 * LANE), BF16),
        ),
        in_specs=[hbm, vmem, vmem, vmem, smem] + [hbm] * 4,
        out_specs=(vmem, vmem, vmem),
        scratch_shapes=[pltpu.VMEM((ROWS, LANE), F32)] * SPREAD
        + [pltpu.VMEM((LANE, LANE), F32)] * 2
        + [pltpu.VMEM((TILES, SPREAD, LANE), jnp.int32), pltpu.VMEM((TILES, SPREAD, LANE), F32)]
        + [pltpu.VMEM((NX, NY), BF16)] * 4
        + [pltpu.VMEM(t.shape, BF16) for t in tabs]
        + [pltpu.SemaphoreType.DMA((TILES,)), pltpu.SemaphoreType.DMA((4,))]
        + [pltpu.SMEM((SPREAD * LANE,), jnp.int32)] * TILES,
        name="front",
    )(rows, cells, splines, charges.reshape(1, SLOTS), counts, *tabs)


def green_kernel(blocks, spectrum, green, out, flat, sums, *rhs):
    plus, minus, odd = blocks
    for j in range(2):
        flat[...] = spectrum[:, :, j * LANE : (j + 1) * LANE].astype(F32).reshape(NZ * 2 * NU, LANE)
        for ul in range(NU):
            for c in range(2):
                rows = flat[pl.ds(c * NU + ul, NZ, stride=2 * NU), :]
                rhs[ul][j, :, c * LANE : (c + 1) * LANE] = rows.astype(BF16)
    first = lax.broadcasted_iota(jnp.int32, (NZ, 2 * LANE), 1) % LANE == 0
    for ul in range(NU):
        m0 = dot(green[ul, plus], rhs[ul][0])
        m1 = jnp.where(first, dot(green[ul, odd], rhs[ul][1]), dot(green[ul, minus], rhs[ul][1]))
        if plus == 0:
            total = m0 + jnp.where(first, 0.0, m1)
            apart = jnp.where(first, 0.0, m0) - m1
        else:
            total = m0 + m1
            apart = m0 - m1
        re = pl.ds(ul, NZ, stride=2 * NU)
        im = pl.ds(NU + ul, NZ, stride=2 * NU)
        sums[0, re, :] = total[:, :LANE]
        sums[0, im, :] = total[:, LANE:]
        sums[1, re, :] = -apart[:, LANE:]
        sums[1, im, :] = apart[:, :LANE]
    for j in range(2):
        out[:, :, j * LANE : (j + 1) * LANE] = sums[j].astype(BF16).reshape(NZ, 2 * NU, LANE)


def mix(pencil, green, blocks):
    vmem = pl.BlockSpec(memory_space=pltpu.VMEM)
    return pl.pallas_call(
        functools.partial(green_kernel, blocks),
        out_shape=jax.ShapeDtypeStruct((NZ, 2 * NU, 2 * LANE), BF16),
        in_specs=[vmem, vmem],
        out_specs=vmem,
        scratch_shapes=[pltpu.VMEM((NZ * 2 * NU, LANE), F32), pltpu.VMEM((2, NZ * 2 * NU, LANE), F32)]
        + [pltpu.VMEM((2, NZ, 2 * LANE), BF16)] * NU,
        name=f"mix{blocks[0]}",
    )(pencil.reshape(NZ, 2 * NU, 2 * LANE), green).reshape(DEV, ZD, 2 * NU, 2 * LANE)


def back_kernel(mixed, inverse_x, inverse_y, *refs):
    middle = dot(inverse_x[...], mixed[:, 0].reshape(2 * NX, 2 * LANE))
    total = dot(middle.astype(BF16), inverse_y[...])
    refs[-1][0] = total if len(refs) == 1 else total + refs[0][0]


def back(returned, inverse_x, inverse_y, *before):
    plane = pl.BlockSpec((1, NX, NY), lambda z: (z, 0, 0))
    return pl.pallas_call(
        back_kernel,
        grid=(ZD,),
        out_shape=jax.ShapeDtypeStruct((ZD, NX, NY), F32),
        in_specs=[
            pl.BlockSpec((DEV, 1, 2 * NU, 2 * LANE), lambda z: (0, z, 0, 0)),
            pl.BlockSpec((NX, 2 * NX), lambda z: (0, 0)),
            pl.BlockSpec((2 * LANE, NY), lambda z: (0, 0)),
        ]
        + [plane] * len(before),
        out_specs=plane,
        name=f"back{len(before)}",
    )(returned, inverse_x, inverse_y, *before)


def exchange(chunk):
    return lax.all_to_all(chunk, AXES, split_axis=0, concat_axis=0, tiled=True)


def shards(charges, cells, splines, counts, green):
    yh, yl, ph, plo, inverse_x, inverse_a, inverse_b = (jnp.asarray(t) for t in tables())
    first, rest_hi, rest_lo = front(charges, cells, splines, counts, (yh, yl, ph, plo))
    pencil_a = exchange(first)
    pencil_b = exchange(rest(rest_hi, rest_lo, ph, plo))
    back_a = exchange(mix(pencil_a, green, (0, 3, 2)))
    back_b = exchange(mix(pencil_b, green, (1, 2, 3)))
    return back(back_b, inverse_x, inverse_b, back(back_a, inverse_x, inverse_a))


def solution(mesh):
    in_specs = (
        P(AXES),
        P(None, AXES),
        P(None, AXES),
        P(AXES),
        P(AXES, None, None, None),
    )
    return jax.shard_map(
        shards, mesh=mesh, in_specs=in_specs, out_specs=P(AXES, None, None), check_vma=False
    )
```

time: 144 us -> 163 us (1.13)
  blocking collectives: 101 us -> 0 us
  waiting for transfers between devices: 0 us -> 73.5 us
  starting transfers between devices: 0 us -> 24.2 us
  Pallas kernels: 41.1 us -> 58.1 us
  local copies, waits for them, and re-layouts: 0 us -> 4.57 us
    all_to_all x2 -> x0, blocking collectives: 101 us -> none  [the longest x1 53.4 us: shards(): lax.all_to_all(spectrum, AXES, split_axis=0, concat_axis=0, tiled=True)]
    all_to_all x0 -> x4, waiting for transfers between devices: none -> 73.5 us  [exchange(): return lax.all_to_all(chunk, AXES, split_axis=0, concat_axis=0, tiled=True)]
    all_to_all x0 -> x4, starting transfers between devices: none -> 24.2 us  [exchange(): return lax.all_to_all(chunk, AXES, split_axis=0, concat_axis=0, tiled=True)]
    pallas_call x2 -> x4, Pallas kernels: 34.9 us -> 46.3 us  [the longest x1 25.2 us: front(): pl.pallas_call(front_kernel, out_shape=(jax.ShapeDtypeStruct((DEV, ZD, 2...]
    pallas_call x1 -> x2, Pallas kernels: 6.23 us -> 11.7 us  [back(): pl.pallas_call(back_kernel, grid=(ZD,), out_shape=jax.ShapeDtypeStruct((Z...]
    unnamed x0 -> x8, local copies, waits for them, and re-layouts: none -> 4.57 us
  transfers between devices with their start and end apart: 0 -> 4, of which waited for: 0 -> 4; matrix products, arithmetic and copies ran while one was open for 0% -> 0% of each run, Pallas kernels for 0% -> 16%
where the time goes in v2:
time: 163 us
  waiting for transfers between devices  73.5 us (45%)
  Pallas kernels  58.1 us (36%)
  starting transfers between devices  24.2 us (15%)
  local copies, waits for them, and re-layouts  4.57 us (3%)
    all_to_all x4, waiting for transfers between devices, exchange(): return lax.all_to_all(chunk, AXES, split_axis=0, concat_axis=0, tiled=True)  73.5 us
    pallas_call x1, Pallas kernels, front(): pl.pallas_call(front_kernel, out_shape=(jax.ShapeDtypeStruct((DEV, ZD, 2...  25.2 us
    all_to_all x4, starting transfers between devices, exchange(): return lax.all_to_all(chunk, AXES, split_axis=0, concat_axis=0, tiled=True)  24.2 us
    pallas_call x2, Pallas kernels, mix(): pl.pallas_call(functools.partial(green_kernel, blocks), out_shape=jax.Sha...  13.1 us
    pallas_call x2, Pallas kernels, back(): pl.pallas_call(back_kernel, grid=(ZD,), out_shape=jax.ShapeDtypeStruct((Z...  11.7 us
    pallas_call x1, Pallas kernels, rest(): pl.pallas_call(rest_kernel, grid=(ZD,), out_shape=jax.ShapeDtypeStruct((D...  8.01 us
    unnamed x8, local copies, waits for them, and re-layouts  4.57 us
  transfers between devices with their start and end apart: 4, of which 4 were waited for; matrix products, arithmetic and copies ran while one was open for 0% of the time, Pallas kernels for 16%

profile of v2, /device:TPU:1, one launch (start us, length us, event | category | flops | bytes accessed | tf_op | source)
XLA Modules:
  0.0 162.5 jit_solution(15870165673397761252)
XLA Ops:
  0.7 1.5 shift-right-logical_bitcast_fusion.rows_hbm
  2.1 25.2 %front.1 = (bf16[128,3,8,256]{3,2,1,0:T(8,128)(2,1)}, bf16[3,512,256]{2,1,0:T(8,128)(2,1)}, bf16[3,512,256]{2,1,0:T(8,128)(2,1)}) custom-call(s32[16384]{0:T(1024)} %shift-right-logical_bitcast_fusion.rows_hbm, s32[8,2048]{1,0:T(8,128)} %cells.1, f32[8,2048]{1,0:T(8,128)} %splines.1, f32[1,2048]{1,0:T(1,128)} %bitcast.15, s32[1]{0:T(128)S(6)} %copy.13.counts, ...), custom_call_target="tpu_custom_call" | custom-call | tf_op jit(solution)/shard_map/front/pallas_call | solution.py:198
  27.4 11.5 %all-to-all-start.2 = ((bf16[128,3,8,256]{3,2,1,0:T(8,128)(2,1)}), bf16[128,3,8,256]{3,2,1,0:T(8,128)(2,1)S(1)}, u32[]{:S(2)}, u32[]{:S(2)}) async-start(bf16[128,3,8,256]{3,2,1,0:T(8,128)(2,1)} %get-tuple-element.10), calls=%async_computation.2 | async-start | bytes 3145728 | tf_op jit(solution)/shard_map/all_to_all | solution.py:283
  38.9 8.0 %rest.1 = bf16[128,3,8,256]{3,2,1,0:T(8,128)(2,1)} custom-call(bf16[3,512,256]{2,1,0:T(8,128)(2,1)} %get-tuple-element.8.rest_hi, bf16[3,512,256]{2,1,0:T(8,128)(2,1)} %get-tuple-element.9.rest_lo, bf16[1024,512]{1,0:T(8,128)(2,1)} %constant.18.clone.ph_hbm.ph, bf16[1024,512]{1,0:T(8,128)(2,1)} %constant.19.clone.pl_hbm.plo), custom_call_target="tpu_custom_call" | custom-call | tf_op jit(solution)/shard_map/rest/pallas_call | solution.py:183
  46.9 17.0 %all-to-all-done.2 = bf16[128,3,8,256]{3,2,1,0:T(8,128)(2,1)S(1)} async-done(((bf16[128,3,8,256]{3,2,1,0:T(8,128)(2,1)}), bf16[128,3,8,256]{3,2,1,0:T(8,128)(2,1)S(1)}, u32[]{:S(2)}, u32[]{:S(2)}) %all-to-all-start.2) | async-done | bytes 1572896 | tf_op jit(solution)/shard_map/all_to_all | solution.py:283
  63.9 0.0 copy-start.2
  63.9 1.1 copy-done.2
  65.1 4.2 %all-to-all-start = ((bf16[128,3,8,256]{3,2,1,0:T(8,128)(2,1)}), bf16[128,3,8,256]{3,2,1,0:T(8,128)(2,1)S(1)}, u32[]{:S(2)}, u32[]{:S(2)}) async-start(bf16[128,3,8,256]{3,2,1,0:T(8,128)(2,1)} %rest.1), calls=%async_computation | async-start | bytes 3145728 | tf_op jit(solution)/shard_map/all_to_all | solution.py:283
  69.3 6.6 %mix0.1 = bf16[384,8,256]{2,1,0:T(8,128)(2,1)} custom-call(bf16[384,8,256]{2,1,0:T(8,128)(2,1)} %bitcast.11, bf16[4,4,384,384]{3,2,1,0:T(8,128)(2,1)} %green.3), custom_call_target="tpu_custom_call" | custom-call | tf_op jit(solution)/shard_map/mix0/pallas_call | solution.py:248
  75.9 18.5 %all-to-all-done = bf16[128,3,8,256]{3,2,1,0:T(8,128)(2,1)S(1)} async-done(((bf16[128,3,8,256]{3,2,1,0:T(8,128)(2,1)}), bf16[128,3,8,256]{3,2,1,0:T(8,128)(2,1)S(1)}, u32[]{:S(2)}, u32[]{:S(2)}) %all-to-all-start) | async-done | bytes 1572896 | tf_op jit(solution)/shard_map/all_to_all | solution.py:283
  94.3 0.0 copy-start.3
  94.3 1.1 copy-done.3
  95.5 4.2 %all-to-all-start.3 = ((bf16[128,3,8,256]{3,2,1,0:T(8,128)(2,1)}), bf16[128,3,8,256]{3,2,1,0:T(8,128)(2,1)S(1)}, u32[]{:S(2)}, u32[]{:S(2)}) async-start(bf16[128,3,8,256]{3,2,1,0:T(8,128)(2,1)} %bitcast.14), calls=%async_computation.3 | async-start | bytes 3145728 | tf_op jit(solution)/shard_map/all_to_all | solution.py:283
  99.7 6.5 %mix1.1 = bf16[384,8,256]{2,1,0:T(8,128)(2,1)} custom-call(bf16[384,8,256]{2,1,0:T(8,128)(2,1)} %bitcast.12, bf16[4,4,384,384]{3,2,1,0:T(8,128)(2,1)} %green.3), custom_call_target="tpu_custom_call" | custom-call | tf_op jit(solution)/shard_map/mix1/pallas_call | solution.py:248
  106.2 18.5 %all-to-all-done.3.mixed = bf16[128,3,8,256]{3,2,1,0:T(8,128)(2,1)S(1)} async-done(((bf16[128,3,8,256]{3,2,1,0:T(8,128)(2,1)}), bf16[128,3,8,256]{3,2,1,0:T(8,128)(2,1)S(1)}, u32[]{:S(2)}, u32[]{:S(2)}) %all-to-all-start.3) | async-done | bytes 1572896 | tf_op jit(solution)/shard_map/all_to_all | solution.py:283
  124.7 0.0 copy-start.1
  124.7 1.1 copy-done.1
  125.9 4.2 %all-to-all-start.1 = ((bf16[128,3,8,256]{3,2,1,0:T(8,128)(2,1)}), bf16[128,3,8,256]{3,2,1,0:T(8,128)(2,1)S(1)}, u32[]{:S(2)}, u32[]{:S(2)}) async-start(bf16[128,3,8,256]{3,2,1,0:T(8,128)(2,1)} %bitcast.13), calls=%async_computation.1 | async-start | bytes 3145728 | tf_op jit(solution)/shard_map/all_to_all | solution.py:283
  130.1 5.5 %back0.1.refs_0_ = f32[3,512,512]{2,1,0:T(8,128)} custom-call(bf16[128,3,8,256]{3,2,1,0:T(8,128)(2,1)} %copy-done.1, bf16[512,1024]{1,0:T(8,128)(2,1)} %constant.20.clone.inverse_x, bf16[256,512]{1,0:T(8,128)(2,1)} %constant.21.clone.inverse_y), custom_call_target="tpu_custom_call" | custom-call | tf_op jit(solution)/shard_map/back0/pallas_call | solution.py:267
  135.6 19.5 %all-to-all-done.1.mixed = bf16[128,3,8,256]{3,2,1,0:T(8,128)(2,1)S(1)} async-done(((bf16[128,3,8,256]{3,2,1,0:T(8,128)(2,1)}), bf16[128,3,8,256]{3,2,1,0:T(8,128)(2,1)S(1)}, u32[]{:S(2)}, u32[]{:S(2)}) %all-to-all-start.1) | async-done | bytes 1572896 | tf_op jit(solution)/shard_map/all_to_all | solution.py:283
  155.1 0.0 copy-start
  155.1 1.1 copy-done
  156.3 6.2 %back1.1 = f32[3,512,512]{2,1,0:T(8,128)} custom-call(bf16[128,3,8,256]{3,2,1,0:T(8,128)(2,1)} %copy-done, bf16[512,1024]{1,0:T(8,128)(2,1)} %constant.20.clone.inverse_x, bf16[256,512]{1,0:T(8,128)(2,1)} %constant.22.clone.inverse_y, f32[3,512,512]{2,1,0:T(8,128)} %back0.1.refs_0_), custom_call_target="tpu_custom_call" | custom-call | tf_op jit(solution)/shard_map/back1/pallas_call | solution.py:267
Async XLA Ops:
  27.4 36.5 %all-to-all-start.2 = ((bf16[128,3,8,256]{3,2,1,0:T(8,128)(2,1)}), bf16[128,3,8,256]{3,2,1,0:T(8,128)(2,1)S(1)}, u32[]{:S(2)}, u32[]{:S(2)}) async-start(bf16[128,3,8,256]{3,2,1,0:T(8,128)(2,1)} %get-tuple-element.10), calls=%async_computation.2 | async-start | bytes 3145728 | tf_op jit(solution)/shard_map/all_to_all | solution.py:283
  63.9 1.1 copy-start.2
  65.1 29.3 %all-to-all-start = ((bf16[128,3,8,256]{3,2,1,0:T(8,128)(2,1)}), bf16[128,3,8,256]{3,2,1,0:T(8,128)(2,1)S(1)}, u32[]{:S(2)}, u32[]{:S(2)}) async-start(bf16[128,3,8,256]{3,2,1,0:T(8,128)(2,1)} %rest.1), calls=%async_computation | async-start | bytes 3145728 | tf_op jit(solution)/shard_map/all_to_all | solution.py:283
  94.3 1.1 copy-start.3
  95.5 29.3 %all-to-all-start.3 = ((bf16[128,3,8,256]{3,2,1,0:T(8,128)(2,1)}), bf16[128,3,8,256]{3,2,1,0:T(8,128)(2,1)S(1)}, u32[]{:S(2)}, u32[]{:S(2)}) async-start(bf16[128,3,8,256]{3,2,1,0:T(8,128)(2,1)} %bitcast.14), calls=%async_computation.3 | async-start | bytes 3145728 | tf_op jit(solution)/shard_map/all_to_all | solution.py:283
  124.7 1.1 copy-start.1
  125.9 29.3 %all-to-all-start.1 = ((bf16[128,3,8,256]{3,2,1,0:T(8,128)(2,1)}), bf16[128,3,8,256]{3,2,1,0:T(8,128)(2,1)S(1)}, u32[]{:S(2)}, u32[]{:S(2)}) async-start(bf16[128,3,8,256]{3,2,1,0:T(8,128)(2,1)} %bitcast.13), calls=%async_computation.1 | async-start | bytes 3145728 | tf_op jit(solution)/shard_map/all_to_all | solution.py:283
  155.1 1.1 copy-start

commit v3 on v1

v3 whole, which is shorter than its diff:
```python
import jax
import jax.numpy as jnp
import numpy as np
from jax import lax
from jax.experimental import pallas as pl
from jax.experimental.pallas import tpu as pltpu
from jax.sharding import PartitionSpec as P

NX = 512
NY = 512
NZ = 384
KYB = 4
AXES = ("zg", "xy")
DEV = 128
ZD = 3
NU = NX // DEV
HALF = NY // 2
LANE = 128
SLOTS = 2048
SPREAD = 8
TILES = SLOTS // LANE
ROWS = ZD * NX * NY // LANE
F32 = jnp.float32
BF16 = jnp.bfloat16


def split(table):
    high = table.astype(BF16)
    return high, (table - high.astype(np.float64)).astype(BF16)


def angles(left, right):
    return (np.outer(left, right) % NX) * (2.0 * np.pi / NX)


def waves():
    device = np.arange(DEV)[:, None, None]
    half = np.arange(2)[None, :, None]
    number = np.arange(NU // 2)[None, None, :]
    return device * NU + number * 2 + (half + device // (DEV // 2)) % 2


def forward_tables():
    y = np.arange(NY)
    v = np.arange(HALF)
    along_y = np.concatenate([np.cos(angles(y, v)), -np.sin(angles(y, v))], axis=1)
    along_y[:, HALF] = np.where(y % 2 == 0, 1.0, -1.0)
    x = np.arange(NX // 2)
    low = np.arange(DEV // 2)[:, None, None]
    number = np.arange(NU // 2)[None, None, :]
    out = [*split(along_y / 512.0)]
    for odd in range(2):
        which = (np.arange(2)[None, :, None] + odd) % 2
        a = angles(((low + which * (DEV // 2)) * NU + number * 2 + odd).reshape(-1), x).reshape(DEV // 2, NU, NX // 2)
        out += split(np.stack([np.cos(a), -np.sin(a)], axis=1).reshape(NX, NX // 2))
    return tuple(out)


def inverse_tables():
    wave = jnp.asarray(waves().reshape(DEV, 1, NU), jnp.int32)
    wave = jnp.broadcast_to(wave, (DEV, 2, NU)).reshape(1, 2 * NX)
    quarter = jnp.tile(jnp.repeat(jnp.arange(2, dtype=jnp.int32), NU), DEV)[None, :] * (NX // 4)
    x = lax.broadcasted_iota(jnp.int32, (NX, 2 * NX), 0)
    step = 2.0 * np.pi / NX
    along_x = jnp.cos(((x * wave + quarter) & (NX - 1)).astype(F32) * step)
    row = lax.broadcasted_iota(jnp.int32, (NY, NY), 0)
    y = lax.broadcasted_iota(jnp.int32, (NY, NY), 1)
    phase = (row & (HALF - 1)) * y - jnp.where(row < HALF, 0, NY // 4)
    phase = jnp.where(row == HALF, (y + 1) * (NY // 2), phase)
    along_y = jnp.cos((phase & (NY - 1)).astype(F32) * step) / 512.0
    return along_x.astype(BF16), along_y.astype(BF16)


def in_hbm(*arrays):
    return tuple(pltpu.with_memory_space_constraint(a, pltpu.HBM) for a in arrays)


def dot(a, b):
    return jnp.dot(a, b, preferred_element_type=F32)


def turn(q):
    whole = q.reshape(-1, 2 * NU, q.shape[1])
    real = lax.broadcasted_iota(jnp.int32, whole.shape, 1) < NU
    swapped = pltpu.roll(whole, NU, 1)
    return jnp.where(real, -swapped, swapped).reshape(q.shape)


def front_kernel(
    rows_hbm, cells_hbm, splines_hbm, charges_hbm, counts, yh_hbm, yl_hbm, eh_hbm, el_hbm, oh_hbm, ol_hbm, out_hbm, *scratch
):
    bins = scratch[:SPREAD]
    spikes = scratch[8:10]
    lanes, values, dens_hi, dens_lo, fold_hi, fold_lo = scratch[10:16]
    tabs = scratch[16:22]
    out, cells, splines, charges, row_sem, tab_sem, out_sem, slot_sem = scratch[22:30]
    row_of = scratch[30:]
    slot_copies = [
        pltpu.make_async_copy(s, d, slot_sem.at[i])
        for i, (s, d) in enumerate(((cells_hbm, cells), (splines_hbm, splines), (charges_hbm, charges)))
    ]
    for copy in slot_copies:
        copy.start()
    row_copies = [
        pltpu.make_async_copy(rows_hbm.at[pl.ds(t * 1024, 1024)], row_of[t], row_sem.at[t]) for t in range(TILES)
    ]
    for copy in row_copies:
        copy.start()
    sources = (yh_hbm, yl_hbm, eh_hbm, el_hbm, oh_hbm, ol_hbm)
    tab_copies = [pltpu.make_async_copy(s, d, tab_sem.at[i]) for i, (s, d) in enumerate(zip(sources, tabs))]
    for copy in tab_copies:
        copy.start()
    zeros = jnp.zeros((256, LANE), F32)

    def clear(i, carry):
        for b in bins:
            b[pl.ds(i * 256, 256), :] = zeros
        return carry

    lax.fori_loop(0, ROWS // 256, clear, 0)
    for copy in slot_copies:
        copy.wait()
    slot = lax.broadcasted_iota(jnp.int32, (1, SLOTS), 1)
    live = (slot < counts[0]).astype(F32)
    value = splines[...] * (charges[...] * live)
    lane_of = cells[...] & (LANE - 1)
    for t in range(TILES):
        lanes[t] = lane_of[:, t * LANE : (t + 1) * LANE]
        values[t] = value[:, t * LANE : (t + 1) * LANE]
    lane = lax.broadcasted_iota(jnp.int32, (SPREAD, LANE), 1)

    def build(spike, g):
        pick = jnp.full((SPREAD, LANE), g, jnp.int32)
        for t in range(TILES):
            at = jnp.take_along_axis(lanes[t], pick, axis=1)
            amount = jnp.take_along_axis(values[t], pick, axis=1)
            spike[t * SPREAD : (t + 1) * SPREAD, :] = jnp.where(lane == at, amount, 0.0)

    def apply(spike, g):
        for t in range(TILES):
            rows = [row_of[t][g + k * LANE] for k in range(SPREAD)]
            sums = [bins[k][pl.ds(rows[k], 1), :] + spike[pl.ds(t * SPREAD + k, 1), :] for k in range(SPREAD)]
            for k in range(SPREAD):
                bins[k][pl.ds(rows[k], 1), :] = sums[k]

    build(spikes[0], 0)
    for copy in row_copies:
        copy.wait()

    def body(h, carry):
        build(spikes[1], 2 * h + 1)
        apply(spikes[0], 2 * h)
        build(spikes[0], jnp.minimum(2 * h + 2, LANE - 1))
        apply(spikes[1], 2 * h + 1)
        return carry

    lax.fori_loop(0, LANE // 2, body, 0)
    for copy in tab_copies:
        copy.wait()
    yh, yl, *along_x = tabs
    first = lax.broadcasted_iota(jnp.int32, (NX, LANE), 1) == 0
    lower = lax.broadcasted_iota(jnp.int32, (NX, LANE), 0) % 4 < 2

    def plane(z, carry):
        for j in range(NY // LANE):
            for q in range(4):
                at = pl.ds(z * (NX * 4) + q * 512 + j, 128, stride=4)
                total = bins[0][at, :]
                for b in bins[1:]:
                    total = total + b[at, :]
                high = total.astype(BF16)
                dens_hi[q * 128 : (q + 1) * 128, j * LANE : (j + 1) * LANE] = high
                dens_lo[q * 128 : (q + 1) * 128, j * LANE : (j + 1) * LANE] = (total - high.astype(F32)).astype(BF16)
        along = dot(dens_hi[...], yh[...]) + dot(dens_lo[...], yh[...]) + dot(dens_hi[...], yl[...])
        near, far = along[: NX // 2], along[NX // 2 :]
        parts = []
        for h, folded in enumerate((near + far, near - far)):
            high = folded.astype(BF16)
            fold_hi[h] = high
            fold_lo[h] = (folded - high.astype(F32)).astype(BF16)
            tab_hi, tab_lo = along_x[2 * h], along_x[2 * h + 1]
            p, q = (
                dot(tab_hi[...], fold_hi[h, :, c]) + dot(tab_hi[...], fold_lo[h, :, c]) + dot(tab_lo[...], fold_hi[h, :, c])
                for c in (slice(0, HALF), slice(HALF, NY))
            )
            q = turn(q)
            p0, p1, q0, q1 = p[:, :LANE], p[:, LANE:], q[:, :LANE], q[:, LANE:]
            minus0 = jnp.where(first, 0.0, p0) - q0
            minus1 = p1 - q1
            parts.append(
                (
                    p0 + jnp.where(first, 0.0, q0),
                    p1 + q1,
                    jnp.where(first, minus1, minus0),
                    jnp.where(first, minus0, minus1),
                )
            )
        for j, (even, odd) in enumerate(zip(*parts)):
            at = slice(j * LANE, (j + 1) * LANE)
            shape = (DEV // 2, 2 * NU, LANE)
            out[z, : DEV // 2, :, at] = jnp.where(lower, even, odd).astype(BF16).reshape(shape)
            out[z, DEV // 2 :, :, at] = jnp.where(lower, odd, even).astype(BF16).reshape(shape)
        pltpu.make_async_copy(out.at[z], out_hbm.at[:, z], out_sem.at[z]).start()
        return carry

    lax.fori_loop(0, ZD, plane, 0)
    for z in range(ZD):
        pltpu.make_async_copy(out.at[z], out_hbm.at[:, z], out_sem.at[z]).wait()


def front(charges, cells, splines, counts, tabs):
    smem = pl.BlockSpec(memory_space=pltpu.SMEM)
    hbm = pl.BlockSpec(memory_space=pltpu.HBM)
    rows = lax.shift_right_logical(cells, 7).reshape(SPREAD, TILES, LANE).transpose(1, 0, 2).reshape(-1)
    return pl.pallas_call(
        front_kernel,
        out_shape=pltpu.HBM((DEV, ZD, 2 * NU, NY), BF16),
        in_specs=[hbm] * 4 + [smem] + [hbm] * 6,
        out_specs=hbm,
        scratch_shapes=[pltpu.VMEM((ROWS, LANE), F32)] * SPREAD
        + [pltpu.VMEM((LANE, LANE), F32)] * 2
        + [pltpu.VMEM((TILES, SPREAD, LANE), jnp.int32), pltpu.VMEM((TILES, SPREAD, LANE), F32)]
        + [pltpu.VMEM((NX, NY), BF16)] * 2
        + [pltpu.VMEM((2, NX // 2, NY), BF16)] * 2
        + [pltpu.VMEM(t.shape, BF16) for t in tabs]
        + [pltpu.VMEM((ZD, DEV, 2 * NU, NY), BF16)]
        + [pltpu.VMEM((SPREAD, SLOTS), jnp.int32), pltpu.VMEM((SPREAD, SLOTS), F32), pltpu.VMEM((1, SLOTS), F32)]
        + [pltpu.SemaphoreType.DMA((n,)) for n in (TILES, 6, ZD, 3)]
        + [pltpu.SMEM((SPREAD * LANE,), jnp.int32)] * TILES,
        compiler_params=pltpu.CompilerParams(vmem_limit_bytes=44 << 20),
        name="front",
    )(*in_hbm(rows, cells, splines, charges.reshape(1, SLOTS)), counts, *in_hbm(*tabs))


BLOCK = (0, 1, 3, 2)
PART = NZ // 2


def green_kernel(odd_first, spectrum, green_hbm, out_hbm, green, out, flat, sums, green_sem, out_sem, *rhs):
    waves_of = [2 * (ul % 2) + jnp.bitwise_xor(odd_first[0], ul // 2) for ul in range(NU)]
    fetches = [
        pltpu.make_async_copy(green_hbm.at[waves_of[ul]], green.at[ul], green_sem.at[ul]) for ul in range(NU)
    ]
    for fetch in fetches:
        fetch.start()
    for j in range(KYB):
        flat[...] = spectrum[:, :, j * LANE : (j + 1) * LANE].astype(F32).reshape(NZ * 2 * NU, LANE)
        for ul in range(NU):
            for c in range(2):
                rows = flat[pl.ds(c * NU + ul, NZ, stride=2 * NU), :]
                rhs[ul][j, :, c * LANE : (c + 1) * LANE] = rows.astype(BF16)
    first = lax.broadcasted_iota(jnp.int32, (PART, 2 * LANE), 1) % LANE == 0
    sends = []
    for part in range(2):
        planes = slice(part * PART, (part + 1) * PART)
        for ul in range(NU):
            if part == 0:
                fetches[ul].wait()
            m0, m1, m2, m3 = (dot(green[ul, BLOCK[j], planes, :], rhs[ul][j]) for j in range(KYB))
            s2 = jnp.where(first, m3, m2)
            s3 = jnp.where(first, m2, m3)
            t0 = m0 + jnp.where(first, 0.0, s2)
            d0 = jnp.where(first, 0.0, m0) - s2
            t1 = m1 + s3
            d1 = m1 - s3
            re = pl.ds(ul, PART, stride=2 * NU)
            im = pl.ds(NU + ul, PART, stride=2 * NU)
            sums[0, re, :] = t0[:, :LANE]
            sums[0, im, :] = t0[:, LANE:]
            sums[1, re, :] = t1[:, :LANE]
            sums[1, im, :] = t1[:, LANE:]
            sums[2, re, :] = -d0[:, LANE:]
            sums[2, im, :] = d0[:, :LANE]
            sums[3, re, :] = -d1[:, LANE:]
            sums[3, im, :] = d1[:, :LANE]
        for j in range(KYB):
            out[planes, :, j * LANE : (j + 1) * LANE] = sums[j].astype(BF16).reshape(PART, 2 * NU, LANE)
        send = pltpu.make_async_copy(out.at[planes], out_hbm.at[planes], out_sem.at[part])
        send.start()
        sends.append(send)
    for send in sends:
        send.wait()


def mix(pencil, green):
    vmem = pl.BlockSpec(memory_space=pltpu.VMEM)
    hbm = pl.BlockSpec(memory_space=pltpu.HBM)
    return pl.pallas_call(
        green_kernel,
        out_shape=pltpu.HBM((NZ, 2 * NU, NY), BF16),
        in_specs=[pl.BlockSpec(memory_space=pltpu.SMEM), vmem, hbm],
        out_specs=hbm,
        compiler_params=pltpu.CompilerParams(vmem_limit_bytes=36 << 20),
        scratch_shapes=[
            pltpu.VMEM((NU, KYB, NZ, NZ), BF16),
            pltpu.VMEM((NZ, 2 * NU, NY), BF16),
            pltpu.VMEM((NZ * 2 * NU, LANE), F32),
            pltpu.VMEM((KYB, PART * 2 * NU, LANE), F32),
            pltpu.SemaphoreType.DMA((NU,)),
            pltpu.SemaphoreType.DMA((2,)),
        ]
        + [pltpu.VMEM((KYB, NZ, 2 * LANE), BF16)] * NU,
        name="mix",
    )(lax.axis_index("zg").astype(jnp.int32).reshape(1), pencil.reshape(NZ, 2 * NU, NY), *in_hbm(green))


def back_kernel(mixed, x_hbm, y_hbm, out_hbm, along_x, along_y, out, tab_sem, out_sem):
    fetches = [
        pltpu.make_async_copy(x_hbm.at[pl.ds(0, HALF)], along_x.at[pl.ds(0, HALF)], tab_sem.at[0]),
        pltpu.make_async_copy(y_hbm, along_y, tab_sem.at[1]),
        pltpu.make_async_copy(x_hbm.at[pl.ds(HALF, HALF)], along_x.at[pl.ds(HALF, HALF)], tab_sem.at[2]),
    ]
    for fetch in fetches:
        fetch.start()
    sends = []
    for z in range(ZD):
        waves = mixed[:, z].reshape(2 * NX, NY)
        for h in range(2):
            rows = pl.ds(h * HALF, HALF)
            if z == 0:
                fetches[2 * h].wait()
            middle = dot(along_x[rows, :], waves).astype(BF16)
            if z == 0 and h == 0:
                fetches[1].wait()
            out[z, rows, :] = dot(middle, along_y[...])
            send = pltpu.make_async_copy(out.at[z, rows], out_hbm.at[z, rows], out_sem.at[2 * z + h])
            send.start()
            sends.append(send)
    for send in sends:
        send.wait()


def back(returned, inverse_x, inverse_y):
    vmem = pl.BlockSpec(memory_space=pltpu.VMEM)
    hbm = pl.BlockSpec(memory_space=pltpu.HBM)
    return pl.pallas_call(
        back_kernel,
        out_shape=jax.ShapeDtypeStruct((ZD, NX, NY), F32),
        in_specs=[vmem, hbm, hbm],
        out_specs=hbm,
        compiler_params=pltpu.CompilerParams(vmem_limit_bytes=24 << 20),
        scratch_shapes=[
            pltpu.VMEM((NX, 2 * NX), BF16),
            pltpu.VMEM((NY, NY), BF16),
            pltpu.VMEM((ZD, NX, NY), F32),
            pltpu.SemaphoreType.DMA((3,)),
            pltpu.SemaphoreType.DMA((2 * ZD,)),
        ],
        name="back",
    )(returned, *in_hbm(inverse_x, inverse_y))


def shards(charges, cells, splines, counts, green):
    forward = tuple(jnp.asarray(t) for t in forward_tables())
    inverse_x, inverse_y = inverse_tables()
    spectrum = front(charges, cells, splines, counts, forward)
    pencil = lax.all_to_all(spectrum, AXES, split_axis=0, concat_axis=0, tiled=True)
    mixed = mix(pencil, green).reshape(DEV, ZD, 2 * NU, NY)
    returned = lax.all_to_all(mixed, AXES, split_axis=0, concat_axis=0, tiled=True)
    return back(returned, inverse_x, inverse_y)


def solution(mesh):
    in_specs = (
        P(AXES),
        P(None, AXES),
        P(None, AXES),
        P(AXES),
        P(AXES, None, None, None),
    )
    return jax.shard_map(
        shards, mesh=mesh, in_specs=in_specs, out_specs=P(AXES, None, None), check_vma=False
    )
```

time: 144 us -> 137 us (0.951)
  blocking collectives: 101 us -> 0 us
  waiting for transfers between devices: 0 us -> 69.8 us
  starting transfers between devices: 0 us -> 16.5 us
  other arithmetic: 1.47 us -> 14.7 us
  Pallas kernels: 41.1 us -> 34.2 us
    all_to_all x2 -> x0, blocking collectives: 101 us -> none  [the longest x1 53.4 us: shards(): lax.all_to_all(spectrum, AXES, split_axis=0, concat_axis=0, tiled=True)]
    all_to_all x0 -> x2, waiting for transfers between devices: none -> 69.8 us  [the longest x1 41.8 us: shards(): lax.all_to_all(spectrum, AXES, split_axis=0, concat_axis=0, tiled=True)]
    all_to_all x0 -> x2, starting transfers between devices: none -> 16.5 us  [the longest x1 11.5 us: shards(): lax.all_to_all(spectrum, AXES, split_axis=0, concat_axis=0, tiled=True)]
    convert_element_type x0 -> x2, other arithmetic: none -> 13.3 us  [inverse_tables(): return (along_x.astype(BF16), along_y.astype(BF16))]
    pallas_call x3, Pallas kernels: 41.1 us -> 34.2 us  [the longest x1 22.3 us: front(): pl.pallas_call(front_kernel, out_shape=pltpu.HBM((DEV, ZD, 2 * NU, NY), B...]
  transfers between devices with their start and end apart: 0 -> 2, of which waited for: 0 -> 2; matrix products, arithmetic and copies ran while one was open for 0% -> 10% of each run, Pallas kernels for 0% -> 0%
where the time goes in v3:
time: 137 us
  waiting for transfers between devices  69.8 us (51%)
  Pallas kernels  34.2 us (25%)
  starting transfers between devices  16.5 us (12%)
  other arithmetic  14.7 us (11%)
    all_to_all x1, waiting for transfers between devices, shards(): lax.all_to_all(spectrum, AXES, split_axis=0, concat_axis=0, tiled=True)  41.8 us
    all_to_all x1, waiting for transfers between devices, shards(): lax.all_to_all(mixed, AXES, split_axis=0, concat_axis=0, tiled=True)  28 us
    pallas_call x1, Pallas kernels, front(): pl.pallas_call(front_kernel, out_shape=pltpu.HBM((DEV, ZD, 2 * NU, NY), B...  22.3 us
    convert_element_type x2, other arithmetic, inverse_tables(): return (along_x.astype(BF16), along_y.astype(BF16))  13.3 us
    all_to_all x1, starting transfers between devices, shards(): lax.all_to_all(spectrum, AXES, split_axis=0, concat_axis=0, tiled=True)  11.5 us
    pallas_call x1, Pallas kernels, mix(): pl.pallas_call(green_kernel, out_shape=pltpu.HBM((NZ, 2 * NU, NY), BF16),...  6.64 us
    pallas_call x1, Pallas kernels, back(): pl.pallas_call(back_kernel, out_shape=jax.ShapeDtypeStruct((ZD, NX, NY),...  5.25 us
    all_to_all x1, starting transfers between devices, shards(): lax.all_to_all(mixed, AXES, split_axis=0, concat_axis=0, tiled=True)  4.97 us
  transfers between devices with their start and end apart: 2, of which 2 were waited for; matrix products, arithmetic and copies ran while one was open for 10% of the time, Pallas kernels for 0%

profile of v3, /device:TPU:1, one launch (start us, length us, event | category | flops | bytes accessed | tf_op | source)
XLA Modules:
  0.0 136.5 jit_solution(18418581446155058961)
XLA Ops:
  0.0 1.5 %shift-right-logical_bitcast_fusion.rows_hbm = s32[16384]{0:T(1024)} fusion(s32[8,2048]{1,0:T(8,128)} %cells_hbm.1), kind=kLoop, calls=%fused_computation.2 | loop fusion | flops 16384 | bytes 131072 | tf_op jit(solution)/shard_map/reshape | solution.py:214
  2.1 22.3 %front.1 = bf16[128,3,8,512]{3,2,1,0:T(8,128)(2,1)} custom-call(s32[16384]{0:T(1024)} %shift-right-logical_bitcast_fusion.rows_hbm, s32[8,2048]{1,0:T(8,128)} %cells_hbm.1, f32[8,2048]{1,0:T(8,128)} %splines_hbm.1, f32[1,2048]{1,0:T(1,128)} %bitcast.12, s32[1]{0:T(128)S(6)} %copy.13.counts, bf16[512,512]{1,0:T(8,128)(2,1)} %constant.42.clone.yh_hbm, ...), custom_call_target="tpu_custom_call" | custom-call | tf_op jit(solution)/shard_map/front/pallas_call | solution.py:215
  24.5 11.5 %all-to-all-start = ((bf16[128,3,8,512]{3,2,1,0:T(8,128)(2,1)}), bf16[128,3,8,512]{3,2,1,0:T(8,128)(2,1)S(1)}, u32[]{:S(2)}, u32[]{:S(2)}) async-start(bf16[128,3,8,512]{3,2,1,0:T(8,128)(2,1)} %front.1), calls=%async_computation | async-start | bytes 6291456 | tf_op jit(solution)/shard_map/all_to_all | solution.py:357
  36.0 41.8 %all-to-all-done = bf16[128,3,8,512]{3,2,1,0:T(8,128)(2,1)S(1)} async-done(((bf16[128,3,8,512]{3,2,1,0:T(8,128)(2,1)}), bf16[128,3,8,512]{3,2,1,0:T(8,128)(2,1)S(1)}, u32[]{:S(2)}, u32[]{:S(2)}) %all-to-all-start) | async-done | bytes 3145760 | tf_op jit(solution)/shard_map/all_to_all | solution.py:357
  77.7 6.6 %mix.1 = bf16[384,8,512]{2,1,0:T(8,128)(2,1)} custom-call(s32[1]{0:T(128)} %bitcast.odd_first, bf16[384,8,512]{2,1,0:T(8,128)(2,1)S(1)} %bitcast.10, bf16[4,4,384,384]{3,2,1,0:T(8,128)(2,1)} %green_hbm.1), custom_call_target="tpu_custom_call" | custom-call | tf_op jit(solution)/shard_map/mix/pallas_call | solution.py:288
  84.4 0.0 copy-start
  84.4 5.0 %all-to-all-start.1 = ((bf16[128,3,8,512]{3,2,1,0:T(8,128)(2,1)}), bf16[128,3,8,512]{3,2,1,0:T(8,128)(2,1)S(1)}, u32[]{:S(2)}, u32[]{:S(2)}) async-start(bf16[128,3,8,512]{3,2,1,0:T(8,128)(2,1)} %bitcast.11), calls=%async_computation.1 | async-start | bytes 6291456 | tf_op jit(solution)/shard_map/all_to_all | solution.py:359
  89.3 0.0 copy-done
  89.4 0.2 mul.47
  89.6 0.1 mul.52
  89.7 0.1 mul.53
  89.8 5.1 %multiply_convert_fusion.y_hbm = bf16[512,512]{1,0:T(8,128)(2,1)} fusion(s32[512]{0:T(512)S(1)} %fusion, s32[512]{0:T(512)S(1)} %get-tuple-element.5, s32[512]{0:T(512)S(1)} %get-tuple-element.6, pred[512]{0:T(512)(128)(4,1)S(1)} %iota_compare_fusion.1), kind=kLoop, calls=%fused_computation.1 | loop fusion | flops 2097152 | bytes 530944 | tf_op jit(solution)/shard_map/convert_element_type | solution.py:71
  94.9 8.2 %cosine_convert_fusion.x_hbm = bf16[512,1024]{1,0:T(8,128)(2,1)} fusion(s32[1024]{0:T(1024)S(1)} %mul.53, s32[1024]{0:T(1024)S(1)} %mul.47), kind=kLoop, calls=%fused_computation | loop fusion | flops 3145728 | bytes 1056768 | tf_op jit(solution)/shard_map/convert_element_type | solution.py:71
  103.1 28.0 %all-to-all-done.1.mixed = bf16[128,3,8,512]{3,2,1,0:T(8,128)(2,1)S(1)} async-done(((bf16[128,3,8,512]{3,2,1,0:T(8,128)(2,1)}), bf16[128,3,8,512]{3,2,1,0:T(8,128)(2,1)S(1)}, u32[]{:S(2)}, u32[]{:S(2)}) %all-to-all-start.1) | async-done | bytes 3145760 | tf_op jit(solution)/shard_map/all_to_all | solution.py:359
  131.1 5.3 %back.1 = f32[3,512,512]{2,1,0:T(8,128)} custom-call(bf16[128,3,8,512]{3,2,1,0:T(8,128)(2,1)S(1)} %all-to-all-done.1.mixed, bf16[512,1024]{1,0:T(8,128)(2,1)} %cosine_convert_fusion.x_hbm, bf16[512,512]{1,0:T(8,128)(2,1)} %multiply_convert_fusion.y_hbm), custom_call_target="tpu_custom_call" | custom-call | tf_op jit(solution)/shard_map/back/pallas_call | solution.py:336
  (6 shorter events, 0.1 us)
Async XLA Ops:
  24.5 53.3 %all-to-all-start = ((bf16[128,3,8,512]{3,2,1,0:T(8,128)(2,1)}), bf16[128,3,8,512]{3,2,1,0:T(8,128)(2,1)S(1)}, u32[]{:S(2)}, u32[]{:S(2)}) async-start(bf16[128,3,8,512]{3,2,1,0:T(8,128)(2,1)} %front.1), calls=%async_computation | async-start | bytes 6291456 | tf_op jit(solution)/shard_map/all_to_all | solution.py:357
  84.4 5.0 %copy-start = (s32[128,4]{1,0:T(8,128)S(1)}, s32[128,4]{1,0:T(8,128)}, u32[]{:S(2)}) copy-start(s32[128,4]{1,0:T(8,128)} %constant.51) | copy-start | bytes 6148
  84.4 46.7 %all-to-all-start.1 = ((bf16[128,3,8,512]{3,2,1,0:T(8,128)(2,1)}), bf16[128,3,8,512]{3,2,1,0:T(8,128)(2,1)S(1)}, u32[]{:S(2)}, u32[]{:S(2)}) async-start(bf16[128,3,8,512]{3,2,1,0:T(8,128)(2,1)} %bitcast.11), calls=%async_computation.1 | async-start | bytes 6291456 | tf_op jit(solution)/shard_map/all_to_all | solution.py:359

commit v4 on v3

--- a/solution.py
+++ b/solution.py
@@ -16,6 +16,7 @@
 NU = NX // DEV
 HALF = NY // 2
 LANE = 128
+WIDE = 3 * LANE
 SLOTS = 2048
 SPREAD = 8
 TILES = SLOTS // LANE
@@ -34,10 +35,9 @@
 
 
 def waves():
-    device = np.arange(DEV)[:, None, None]
-    half = np.arange(2)[None, :, None]
-    number = np.arange(NU // 2)[None, None, :]
-    return device * NU + number * 2 + (half + device // (DEV // 2)) % 2
+    device = np.arange(DEV)[:, None]
+    offset = np.array([[0, 2, 1, -1], [1, -1, 0, 2]])[device[:, 0] // (DEV // 2)]
+    return np.where(offset < 0, -1, device * NU + offset)
 
 
 def forward_tables():
@@ -46,23 +46,23 @@
     along_y = np.concatenate([np.cos(angles(y, v)), -np.sin(angles(y, v))], axis=1)
     along_y[:, HALF] = np.where(y % 2 == 0, 1.0, -1.0)
     x = np.arange(NX // 2)
-    low = np.arange(DEV // 2)[:, None, None]
-    number = np.arange(NU // 2)[None, None, :]
+    near, far = waves()[: DEV // 2], waves()[DEV // 2 :]
     out = [*split(along_y / 512.0)]
-    for odd in range(2):
-        which = (np.arange(2)[None, :, None] + odd) % 2
-        a = angles(((low + which * (DEV // 2)) * NU + number * 2 + odd).reshape(-1), x).reshape(DEV // 2, NU, NX // 2)
-        out += split(np.stack([np.cos(a), -np.sin(a)], axis=1).reshape(NX, NX // 2))
+    for wave in (np.concatenate([near[:, :2], far[:, 2:]], axis=1), np.concatenate([far[:, :2], near[:, 2:]], axis=1)):
+        a = angles(wave.reshape(-1), x).reshape(DEV // 2, NU, NX // 2)
+        used = (wave >= 0)[:, :, None]
+        out += split(np.stack([np.cos(a) * used, -np.sin(a) * used], axis=1).reshape(NX, NX // 2))
     return tuple(out)
 
 
 def inverse_tables():
-    wave = jnp.asarray(waves().reshape(DEV, 1, NU), jnp.int32)
-    wave = jnp.broadcast_to(wave, (DEV, 2, NU)).reshape(1, 2 * NX)
+    wave = waves().reshape(DEV, 1, NU).repeat(2, axis=1).reshape(1, 2 * NX)
+    used = jnp.asarray(wave >= 0, F32)
+    wave = jnp.asarray(wave, jnp.int32)
     quarter = jnp.tile(jnp.repeat(jnp.arange(2, dtype=jnp.int32), NU), DEV)[None, :] * (NX // 4)
     x = lax.broadcasted_iota(jnp.int32, (NX, 2 * NX), 0)
     step = 2.0 * np.pi / NX
-    along_x = jnp.cos(((x * wave + quarter) & (NX - 1)).astype(F32) * step)
+    along_x = jnp.cos(((x * wave + quarter) & (NX - 1)).astype(F32) * step) * used
     row = lax.broadcasted_iota(jnp.int32, (NY, NY), 0)
     y = lax.broadcasted_iota(jnp.int32, (NY, NY), 1)
     phase = (row & (HALF - 1)) * y - jnp.where(row < HALF, 0, NY // 4)
@@ -159,7 +159,8 @@
         copy.wait()
     yh, yl, *along_x = tabs
     first = lax.broadcasted_iota(jnp.int32, (NX, LANE), 1) == 0
-    lower = lax.broadcasted_iota(jnp.int32, (NX, LANE), 0) % 4 < 2
+    lower = lax.broadcasted_iota(jnp.int32, (NX, LANE), 0) % NU < 2
+    row_of_tile = lax.broadcasted_iota(jnp.int32, (DEV // 2, 2 * NU, LANE), 1) % NU
 
     def plane(z, carry):
         for j in range(NY // LANE):
@@ -195,11 +196,16 @@
                     jnp.where(first, minus0, minus1),
                 )
             )
-        for j, (even, odd) in enumerate(zip(*parts)):
-            at = slice(j * LANE, (j + 1) * LANE)
+        near = [jnp.where(lower, even, odd) for even, odd in zip(*parts)]
+        far = [jnp.where(lower, odd, even) for even, odd in zip(*parts)]
+        for side, (groups, spare) in enumerate(((near, 3), (far, 1))):
             shape = (DEV // 2, 2 * NU, LANE)
-            out[z, : DEV // 2, :, at] = jnp.where(lower, even, odd).astype(BF16).reshape(shape)
-            out[z, DEV // 2 :, :, at] = jnp.where(lower, odd, even).astype(BF16).reshape(shape)
+            last = groups[3].reshape(shape)
+            for j in range(3):
+                moved = pltpu.roll(last, (spare - (j ^ 2 * side)) % 8, 1)
+                out[z, side * (DEV // 2) : (side + 1) * (DEV // 2), :, j * LANE : (j + 1) * LANE] = jnp.where(
+                    row_of_tile == spare, moved, groups[j].reshape(shape)
+                ).astype(BF16)
         pltpu.make_async_copy(out.at[z], out_hbm.at[:, z], out_sem.at[z]).start()
         return carry
 
@@ -214,7 +220,7 @@
     rows = lax.shift_right_logical(cells, 7).reshape(SPREAD, TILES, LANE).transpose(1, 0, 2).reshape(-1)
     return pl.pallas_call(
         front_kernel,
-        out_shape=pltpu.HBM((DEV, ZD, 2 * NU, NY), BF16),
+        out_shape=pltpu.HBM((DEV, ZD, 2 * NU, WIDE), BF16),
         in_specs=[hbm] * 4 + [smem] + [hbm] * 6,
         out_specs=hbm,
         scratch_shapes=[pltpu.VMEM((ROWS, LANE), F32)] * SPREAD
@@ -223,7 +229,7 @@
         + [pltpu.VMEM((NX, NY), BF16)] * 2
         + [pltpu.VMEM((2, NX // 2, NY), BF16)] * 2
         + [pltpu.VMEM(t.shape, BF16) for t in tabs]
-        + [pltpu.VMEM((ZD, DEV, 2 * NU, NY), BF16)]
+        + [pltpu.VMEM((ZD, DEV, 2 * NU, WIDE), BF16)]
         + [pltpu.VMEM((SPREAD, SLOTS), jnp.int32), pltpu.VMEM((SPREAD, SLOTS), F32), pltpu.VMEM((1, SLOTS), F32)]
         + [pltpu.SemaphoreType.DMA((n,)) for n in (TILES, 6, ZD, 3)]
         + [pltpu.SMEM((SPREAD * LANE,), jnp.int32)] * TILES,
@@ -232,48 +238,59 @@
     )(*in_hbm(rows, cells, splines, charges.reshape(1, SLOTS)), counts, *in_hbm(*tabs))
 
 
+WAVE = (0, 2, 1)
 BLOCK = (0, 1, 3, 2)
+MIRROR = (3, 2, 0, 1)
+SWAP = (1, 3, 0, 2)
 PART = NZ // 2
 
 
-def green_kernel(odd_first, spectrum, green_hbm, out_hbm, green, out, flat, sums, green_sem, out_sem, *rhs):
-    waves_of = [2 * (ul % 2) + jnp.bitwise_xor(odd_first[0], ul // 2) for ul in range(NU)]
-    fetches = [
-        pltpu.make_async_copy(green_hbm.at[waves_of[ul]], green.at[ul], green_sem.at[ul]) for ul in range(NU)
-    ]
+def green_kernel(far, spectrum, green_hbm, mirror_hbm, out_hbm, green, out, flat, sums, swapped, green_sem, out_sem, *rhs):
+    sources = [green_hbm.at[w] for w in WAVE] + [mirror_hbm]
+    fetches = [pltpu.make_async_copy(s, green.at[i], green_sem.at[i]) for i, s in enumerate(sources)]
     for fetch in fetches:
         fetch.start()
+    at = [jnp.bitwise_xor(row, 2 * far[0]) for row in range(NU)]
+    for j in range(3):
+        flat[...] = spectrum[:, :, j * LANE : (j + 1) * LANE].astype(F32).reshape(NZ * 2 * NU, LANE)
+        for row in range(NU):
+            for c in range(2):
+                values = flat[pl.ds(c * NU + at[row], NZ, stride=2 * NU), :].astype(BF16)
+                to, group = (rhs[row], j) if row < 3 else (rhs[j], 3)
+                to[group, :, c * LANE : (c + 1) * LANE] = values
+    first = lax.broadcasted_iota(jnp.int32, (NZ, 2 * LANE), 1) % LANE == 0
     for j in range(KYB):
-        flat[...] = spectrum[:, :, j * LANE : (j + 1) * LANE].astype(F32).reshape(NZ * 2 * NU, LANE)
-        for ul in range(NU):
-            for c in range(2):
-                rows = flat[pl.ds(c * NU + ul, NZ, stride=2 * NU), :]
-                rhs[ul][j, :, c * LANE : (c + 1) * LANE] = rows.astype(BF16)
-    first = lax.broadcasted_iota(jnp.int32, (PART, 2 * LANE), 1) % LANE == 0
+        swapped[j] = jnp.where(first, rhs[2][SWAP[j]], rhs[2][j])
+    first = first[:PART]
     sends = []
     for part in range(2):
         planes = slice(part * PART, (part + 1) * PART)
-        for ul in range(NU):
+        for row in range(3):
             if part == 0:
-                fetches[ul].wait()
-            m0, m1, m2, m3 = (dot(green[ul, BLOCK[j], planes, :], rhs[ul][j]) for j in range(KYB))
-            s2 = jnp.where(first, m3, m2)
-            s3 = jnp.where(first, m2, m3)
-            t0 = m0 + jnp.where(first, 0.0, s2)
-            d0 = jnp.where(first, 0.0, m0) - s2
-            t1 = m1 + s3
-            d1 = m1 - s3
-            re = pl.ds(ul, PART, stride=2 * NU)
-            im = pl.ds(NU + ul, PART, stride=2 * NU)
-            sums[0, re, :] = t0[:, :LANE]
-            sums[0, im, :] = t0[:, LANE:]
-            sums[1, re, :] = t1[:, :LANE]
-            sums[1, im, :] = t1[:, LANE:]
-            sums[2, re, :] = -d0[:, LANE:]
-            sums[2, im, :] = d0[:, :LANE]
-            sums[3, re, :] = -d1[:, LANE:]
-            sums[3, im, :] = d1[:, :LANE]
-        for j in range(KYB):
+                fetches[row].wait()
+            m = [dot(green[row, BLOCK[j], planes, :], rhs[row][j]) for j in range(KYB)]
+            if row == 2:
+                if part == 0:
+                    fetches[3].wait()
+                other = [dot(green[3, MIRROR[j], planes, :], swapped[j]) for j in range(KYB)]
+                m = [m[j] + jnp.where(first, other[SWAP.index(j)], other[j]) for j in range(KYB)]
+            s2 = jnp.where(first, m[3], m[2])
+            s3 = jnp.where(first, m[2], m[3])
+            t0 = m[0] + jnp.where(first, 0.0, s2)
+            d0 = jnp.where(first, 0.0, m[0]) - s2
+            t1 = m[1] + s3
+            d1 = m[1] - s3
+            groups = (
+                (t0[:, :LANE], t0[:, LANE:]),
+                (t1[:, :LANE], t1[:, LANE:]),
+                (-d0[:, LANE:], d0[:, :LANE]),
+                (-d1[:, LANE:], d1[:, :LANE]),
+            )
+            for j, group in enumerate(groups):
+                for c in range(2):
+                    to, slot = (j, row) if j < 3 else (row, 3)
+                    sums[to, pl.ds(c * NU + at[slot], PART, stride=2 * NU), :] = group[c]
+        for j in range(3):
             out[planes, :, j * LANE : (j + 1) * LANE] = sums[j].astype(BF16).reshape(PART, 2 * NU, LANE)
         send = pltpu.make_async_copy(out.at[planes], out_hbm.at[planes], out_sem.at[part])
         send.start()
@@ -282,29 +299,30 @@
         send.wait()
 
 
-def mix(pencil, green):
+def mix(pencil, green, mirror):
     vmem = pl.BlockSpec(memory_space=pltpu.VMEM)
     hbm = pl.BlockSpec(memory_space=pltpu.HBM)
     return pl.pallas_call(
         green_kernel,
-        out_shape=pltpu.HBM((NZ, 2 * NU, NY), BF16),
-        in_specs=[pl.BlockSpec(memory_space=pltpu.SMEM), vmem, hbm],
+        out_shape=pltpu.HBM((NZ, 2 * NU, WIDE), BF16),
+        in_specs=[pl.BlockSpec(memory_space=pltpu.SMEM), vmem, hbm, hbm],
         out_specs=hbm,
         compiler_params=pltpu.CompilerParams(vmem_limit_bytes=36 << 20),
         scratch_shapes=[
             pltpu.VMEM((NU, KYB, NZ, NZ), BF16),
-            pltpu.VMEM((NZ, 2 * NU, NY), BF16),
+            pltpu.VMEM((NZ, 2 * NU, WIDE), BF16),
             pltpu.VMEM((NZ * 2 * NU, LANE), F32),
-            pltpu.VMEM((KYB, PART * 2 * NU, LANE), F32),
+            pltpu.VMEM((3, PART * 2 * NU, LANE), F32),
+            pltpu.VMEM((KYB, NZ, 2 * LANE), BF16),
             pltpu.SemaphoreType.DMA((NU,)),
             pltpu.SemaphoreType.DMA((2,)),
         ]
-        + [pltpu.VMEM((KYB, NZ, 2 * LANE), BF16)] * NU,
+        + [pltpu.VMEM((KYB, NZ, 2 * LANE), BF16)] * 3,
         name="mix",
-    )(lax.axis_index("zg").astype(jnp.int32).reshape(1), pencil.reshape(NZ, 2 * NU, NY), *in_hbm(green))
-
-
-def back_kernel(mixed, x_hbm, y_hbm, out_hbm, along_x, along_y, out, tab_sem, out_sem):
+    )(lax.axis_index("zg").astype(jnp.int32).reshape(1), pencil.reshape(NZ, 2 * NU, WIDE), *in_hbm(green, mirror))
+
+
+def back_kernel(mixed, x_hbm, y_hbm, out_hbm, along_x, along_y, out, rest, tab_sem, out_sem):
     fetches = [
         pltpu.make_async_copy(x_hbm.at[pl.ds(0, HALF)], along_x.at[pl.ds(0, HALF)], tab_sem.at[0]),
         pltpu.make_async_copy(y_hbm, along_y, tab_sem.at[1]),
@@ -312,17 +330,28 @@
     ]
     for fetch in fetches:
         fetch.start()
+    row_of_tile = lax.broadcasted_iota(jnp.int32, (DEV // 2, 2 * NU, LANE), 1) % NU
     sends = []
     for z in range(ZD):
-        waves = mixed[:, z].reshape(2 * NX, NY)
+        for side in range(2):
+            devices = slice(side * (DEV // 2), (side + 1) * (DEV // 2))
+            spare = 3 - 2 * side
+            last = None
+            for j in range(3):
+                group = mixed[devices, z, :, j * LANE : (j + 1) * LANE].astype(F32)
+                moved = pltpu.roll(group, ((j ^ 2 * side) - spare) % 8, 1)
+                last = moved if last is None else jnp.where(row_of_tile == (j ^ 2 * side), moved, last)
+            rest[devices, :, LANE:] = last.astype(BF16)
+        rest[:, :, :LANE] = mixed[:, z, :, 2 * LANE :]
         for h in range(2):
             rows = pl.ds(h * HALF, HALF)
             if z == 0:
                 fetches[2 * h].wait()
-            middle = dot(along_x[rows, :], waves).astype(BF16)
+            front = dot(along_x[rows, :], mixed[:, z, :, : 2 * LANE].reshape(2 * NX, 2 * LANE)).astype(BF16)
+            tail = dot(along_x[rows, :], rest[...].reshape(2 * NX, 2 * LANE)).astype(BF16)
             if z == 0 and h == 0:
                 fetches[1].wait()
-            out[z, rows, :] = dot(middle, along_y[...])
+            out[z, rows, :] = dot(front, along_y[: 2 * LANE, :]) + dot(tail, along_y[2 * LANE :, :])
             send = pltpu.make_async_copy(out.at[z, rows], out_hbm.at[z, rows], out_sem.at[2 * z + h])
             send.start()
             sends.append(send)
@@ -343,6 +372,7 @@
             pltpu.VMEM((NX, 2 * NX), BF16),
             pltpu.VMEM((NY, NY), BF16),
             pltpu.VMEM((ZD, NX, NY), F32),
+            pltpu.VMEM((DEV, 2 * NU, 2 * LANE), BF16),
             pltpu.SemaphoreType.DMA((3,)),
             pltpu.SemaphoreType.DMA((2 * ZD,)),
         ],
@@ -350,12 +380,13 @@
     )(returned, *in_hbm(inverse_x, inverse_y))
 
 
-def shards(charges, cells, splines, counts, green):
+def steps(charges, cells, splines, counts, green):
     forward = tuple(jnp.asarray(t) for t in forward_tables())
     inverse_x, inverse_y = inverse_tables()
+    mirror = lax.ppermute(green[NU - 1], AXES, [(d, DEV - 1 - d) for d in range(DEV)])
     spectrum = front(charges, cells, splines, counts, forward)
     pencil = lax.all_to_all(spectrum, AXES, split_axis=0, concat_axis=0, tiled=True)
-    mixed = mix(pencil, green).reshape(DEV, ZD, 2 * NU, NY)
+    mixed = mix(pencil, green, mirror).reshape(DEV, ZD, 2 * NU, WIDE)
     returned = lax.all_to_all(mixed, AXES, split_axis=0, concat_axis=0, tiled=True)
     return back(returned, inverse_x, inverse_y)
 
@@ -368,6 +399,4 @@
         P(AXES),
         P(AXES, None, None, None),
     )
-    return jax.shard_map(
-        shards, mesh=mesh, in_specs=in_specs, out_specs=P(AXES, None, None), check_vma=False
-    )
+    return jax.shard_map(steps, mesh=mesh, in_specs=in_specs, out_specs=P(AXES, None, None), check_vma=False)

time: 137 us -> 144 us (1.051)
  starting transfers between devices: 16.5 us -> 23.4 us
    all_to_all x2, waiting for transfers between devices: 69.8 us -> 20.2 us  [the longest x1 20.2 us: steps(): lax.all_to_all(mixed, AXES, split_axis=0, concat_axis=0, tiled=True)]
    ppermute x0 -> x1, waiting for transfers between devices: none -> 49.5 us  [steps(): lax.ppermute(green[NU - 1], AXES, [(d, DEV - 1 - d) for d in range(DEV)])]
    ppermute x0 -> x1, starting transfers between devices: none -> 8.05 us  [steps(): lax.ppermute(green[NU - 1], AXES, [(d, DEV - 1 - d) for d in range(DEV)])]
  transfers between devices with their start and end apart: 2 -> 3, of which waited for: 2 -> 2; matrix products, arithmetic and copies ran while one was open for 10% -> 10% of each run, Pallas kernels for 0% -> 0%
where the time goes in v4:
time: 144 us
  waiting for transfers between devices  69.7 us (48%)
  Pallas kernels  33.9 us (24%)
  starting transfers between devices  23.4 us (16%)
  other arithmetic  14.6 us (10%)
  local copies, waits for them, and re-layouts  1.59 us (1%)
    ppermute x1, waiting for transfers between devices, steps(): lax.ppermute(green[NU - 1], AXES, [(d, DEV - 1 - d) for d in range(DEV)])  49.5 us
    pallas_call x1, Pallas kernels, front(): pl.pallas_call(front_kernel, out_shape=pltpu.HBM((DEV, ZD, 2 * NU, WIDE),...  22.8 us
    all_to_all x1, waiting for transfers between devices, steps(): lax.all_to_all(mixed, AXES, split_axis=0, concat_axis=0, tiled=True)  20.2 us
    convert_element_type x2, other arithmetic, inverse_tables(): return (along_x.astype(BF16), along_y.astype(BF16))  13.1 us
    all_to_all x1, starting transfers between devices, steps(): lax.all_to_all(spectrum, AXES, split_axis=0, concat_axis=0, tiled=True)  11.5 us
    ppermute x1, starting transfers between devices, steps(): lax.ppermute(green[NU - 1], AXES, [(d, DEV - 1 - d) for d in range(DEV)])  8.05 us
    pallas_call x1, Pallas kernels, mix(): pl.pallas_call(green_kernel, out_shape=pltpu.HBM((NZ, 2 * NU, WIDE), BF16...  5.82 us
    pallas_call x1, Pallas kernels, back(): pl.pallas_call(back_kernel, out_shape=jax.ShapeDtypeStruct((ZD, NX, NY),...  5.28 us
  transfers between devices with their start and end apart: 3, of which 2 were waited for; matrix products, arithmetic and copies ran while one was open for 10% of the time, Pallas kernels for 0%

profile of v4, /device:TPU:1, one launch (start us, length us, event | category | flops | bytes accessed | tf_op | source)
XLA Modules:
  0.0 144.0 jit_solution(16148422766832620904)
XLA Ops:
  0.0 1.5 %shift-right-logical_bitcast_fusion.rows_hbm = s32[16384]{0:T(1024)} fusion(s32[8,2048]{1,0:T(8,128)} %cells_hbm.1), kind=kLoop, calls=%fused_computation.3 | loop fusion | flops 16384 | bytes 131072 | tf_op jit(solution)/shard_map/reshape | solution.py:220
  2.1 22.8 %front.1 = bf16[128,3,8,384]{3,2,1,0:T(8,128)(2,1)} custom-call(s32[16384]{0:T(1024)} %shift-right-logical_bitcast_fusion.rows_hbm, s32[8,2048]{1,0:T(8,128)} %cells_hbm.1, f32[8,2048]{1,0:T(8,128)} %splines_hbm.1, f32[1,2048]{1,0:T(1,128)} %bitcast.14, s32[1]{0:T(128)S(6)} %copy.14.counts, bf16[512,512]{1,0:T(8,128)(2,1)} %constant.44.clone.yh_hbm, ...), custom_call_target="tpu_custom_call" | custom-call | tf_op jit(solution)/shard_map/front/pallas_call | solution.py:221
  24.9 11.5 %all-to-all-start = ((bf16[128,3,8,384]{3,2,1,0:T(8,128)(2,1)}), bf16[128,3,8,384]{3,2,1,0:T(8,128)(2,1)S(1)}, u32[]{:S(2)}, u32[]{:S(2)}) async-start(bf16[128,3,8,384]{3,2,1,0:T(8,128)(2,1)} %front.1), calls=%async_computation | async-start | bytes 4718592 | tf_op jit(solution)/shard_map/all_to_all | solution.py:388
  36.4 1.4 slice_bitcast_fusion
  37.8 8.1 %collective-permute-start = (bf16[4,384,384]{2,1,0:T(8,128)(2,1)S(1)}, bf16[4,384,384]{2,1,0:T(8,128)(2,1)}, u32[]{:S(2)}, u32[]{:S(2)}) collective-permute-start(bf16[4,384,384]{2,1,0:T(8,128)(2,1)S(1)} %slice_bitcast_fusion), channel_id=1, source_target_pairs={{0,127},{1,126},{2,125},{3,124},{4,123},{5,122},{6,121},{7,120},{8... | collective-permute-start | bytes 3538952 | tf_op jit(solution)/shard_map/ppermute | solution.py:386
  45.9 49.5 %collective-permute-done.mirror_hbm = bf16[4,384,384]{2,1,0:T(8,128)(2,1)} collective-permute-done((bf16[4,384,384]{2,1,0:T(8,128)(2,1)S(1)}, bf16[4,384,384]{2,1,0:T(8,128)(2,1)}, u32[]{:S(2)}, u32[]{:S(2)}) %collective-permute-start) | collective-permute-done | bytes 1179680 | tf_op jit(solution)/shard_map/ppermute | solution.py:386
  95.4 0.0 all-to-all-done
  95.4 5.8 %mix.1 = bf16[384,8,384]{2,1,0:T(8,128)(2,1)} custom-call(s32[1]{0:T(128)} %bitcast.far, bf16[384,8,384]{2,1,0:T(8,128)(2,1)S(1)} %bitcast.12, bf16[4,4,384,384]{3,2,1,0:T(8,128)(2,1)} %green_hbm.1, bf16[4,384,384]{2,1,0:T(8,128)(2,1)} %collective-permute-done.mirror_hbm), custom_call_target="tpu_custom_call" | custom-call | tf_op jit(solution)/shard_map/mix/pallas_call | solution.py:305
  101.2 0.0 copy-start
  101.2 0.0 copy-start.1
  101.2 3.8 %all-to-all-start.1 = ((bf16[128,3,8,384]{3,2,1,0:T(8,128)(2,1)}), bf16[128,3,8,384]{3,2,1,0:T(8,128)(2,1)S(1)}, u32[]{:S(2)}, u32[]{:S(2)}) async-start(bf16[128,3,8,384]{3,2,1,0:T(8,128)(2,1)} %bitcast.13), calls=%async_computation.1 | async-start | bytes 4718592 | tf_op jit(solution)/shard_map/all_to_all | solution.py:390
  105.0 0.1 mul.62
  105.1 0.1 mul.63
  105.3 5.1 %multiply_convert_fusion.1.y_hbm = bf16[512,512]{1,0:T(8,128)(2,1)} fusion(s32[512]{0:T(512)S(1)} %fusion, s32[512]{0:T(512)S(1)} %get-tuple-element.5, s32[512]{0:T(512)S(1)} %get-tuple-element.6, pred[512]{0:T(512)(128)(4,1)S(1)} %iota_compare_fusion.1), kind=kLoop, calls=%fused_computation.2 | loop fusion | flops 2097152 | bytes 530944 | tf_op jit(solution)/shard_map/convert_element_type | solution.py:71
  110.4 0.0 copy-done
  110.4 0.0 copy-done.1
  110.4 8.0 %multiply_convert_fusion.x_hbm = bf16[512,1024]{1,0:T(8,128)(2,1)} fusion(f32[1024]{0:T(1024)S(1)} %copy-done.1, s32[1024]{0:T(1024)S(1)} %mul.63, s32[1024]{0:T(1024)S(1)} %copy-done), kind=kLoop, calls=%fused_computation | loop fusion | flops 3670016 | bytes 1060864 | tf_op jit(solution)/shard_map/convert_element_type | solution.py:71
  118.4 20.2 %all-to-all-done.1.mixed = bf16[128,3,8,384]{3,2,1,0:T(8,128)(2,1)S(1)} async-done(((bf16[128,3,8,384]{3,2,1,0:T(8,128)(2,1)}), bf16[128,3,8,384]{3,2,1,0:T(8,128)(2,1)S(1)}, u32[]{:S(2)}, u32[]{:S(2)}) %all-to-all-start.1) | async-done | bytes 2359328 | tf_op jit(solution)/shard_map/all_to_all | solution.py:390
  138.6 5.3 %back.1 = f32[3,512,512]{2,1,0:T(8,128)} custom-call(bf16[128,3,8,384]{3,2,1,0:T(8,128)(2,1)S(1)} %all-to-all-done.1.mixed, bf16[512,1024]{1,0:T(8,128)(2,1)} %multiply_convert_fusion.x_hbm, bf16[512,512]{1,0:T(8,128)(2,1)} %multiply_convert_fusion.1.y_hbm), custom_call_target="tpu_custom_call" | custom-call | tf_op jit(solution)/shard_map/back/pallas_call | solution.py:365
  (5 shorter events, 0.0 us)
Async XLA Ops:
  24.9 70.5 %all-to-all-start = ((bf16[128,3,8,384]{3,2,1,0:T(8,128)(2,1)}), bf16[128,3,8,384]{3,2,1,0:T(8,128)(2,1)S(1)}, u32[]{:S(2)}, u32[]{:S(2)}) async-start(bf16[128,3,8,384]{3,2,1,0:T(8,128)(2,1)} %front.1), calls=%async_computation | async-start | bytes 4718592 | tf_op jit(solution)/shard_map/all_to_all | solution.py:388
  37.8 57.6 %collective-permute-start = (bf16[4,384,384]{2,1,0:T(8,128)(2,1)S(1)}, bf16[4,384,384]{2,1,0:T(8,128)(2,1)}, u32[]{:S(2)}, u32[]{:S(2)}) collective-permute-start(bf16[4,384,384]{2,1,0:T(8,128)(2,1)S(1)} %slice_bitcast_fusion), channel_id=1, source_target_pairs={{0,127},{1,126},{2,125},{3,124},{4,123},{5,122},{6,121},{7,120},{8... | collective-permute-start | bytes 3538952 | tf_op jit(solution)/shard_map/ppermute | solution.py:386
  101.2 9.2 %copy-start = (s32[1024]{0:T(1024)S(1)}, s32[1024]{0:T(1024)}, u32[]{:S(2)}) copy-start(s32[1024]{0:T(1024)} %constant.54) | copy-start | bytes 12292
  101.2 9.1 %copy-start.1 = (f32[1024]{0:T(1024)S(1)}, f32[1024]{0:T(1024)}, u32[]{:S(2)}) copy-start(f32[1024]{0:T(1024)} %constant.55) | copy-start | bytes 12292
  101.2 37.4 %all-to-all-start.1 = ((bf16[128,3,8,384]{3,2,1,0:T(8,128)(2,1)}), bf16[128,3,8,384]{3,2,1,0:T(8,128)(2,1)S(1)}, u32[]{:S(2)}, u32[]{:S(2)}) async-start(bf16[128,3,8,384]{3,2,1,0:T(8,128)(2,1)} %bitcast.13), calls=%async_computation.1 | async-start | bytes 4718592 | tf_op jit(solution)/shard_map/all_to_all | solution.py:390

commit v5 on v4

--- a/solution.py
+++ b/solution.py
@@ -87,25 +87,20 @@
 
 
 def front_kernel(
-    rows_hbm, cells_hbm, splines_hbm, charges_hbm, counts, yh_hbm, yl_hbm, eh_hbm, el_hbm, oh_hbm, ol_hbm, out_hbm, *scratch
+    cells_hbm, splines_hbm, charges_hbm, counts, yh_hbm, yl_hbm, eh_hbm, el_hbm, oh_hbm, ol_hbm, out_hbm, *scratch
 ):
     bins = scratch[:SPREAD]
     spikes = scratch[8:10]
     lanes, values, dens_hi, dens_lo, fold_hi, fold_lo = scratch[10:16]
     tabs = scratch[16:22]
-    out, cells, splines, charges, row_sem, tab_sem, out_sem, slot_sem = scratch[22:30]
-    row_of = scratch[30:]
+    out, cells, splines, charges, row_table, row_sem, tab_sem, out_sem, slot_sem = scratch[22:31]
+    row_of = scratch[31:]
     slot_copies = [
         pltpu.make_async_copy(s, d, slot_sem.at[i])
         for i, (s, d) in enumerate(((cells_hbm, cells), (splines_hbm, splines), (charges_hbm, charges)))
     ]
     for copy in slot_copies:
         copy.start()
-    row_copies = [
-        pltpu.make_async_copy(rows_hbm.at[pl.ds(t * 1024, 1024)], row_of[t], row_sem.at[t]) for t in range(TILES)
-    ]
-    for copy in row_copies:
-        copy.start()
     sources = (yh_hbm, yl_hbm, eh_hbm, el_hbm, oh_hbm, ol_hbm)
     tab_copies = [pltpu.make_async_copy(s, d, tab_sem.at[i]) for i, (s, d) in enumerate(zip(sources, tabs))]
     for copy in tab_copies:
@@ -117,8 +112,15 @@
             b[pl.ds(i * 256, 256), :] = zeros
         return carry
 
-    lax.fori_loop(0, ROWS // 256, clear, 0)
-    for copy in slot_copies:
+    lax.fori_loop(0, ROWS // 512, clear, 0)
+    slot_copies[0].wait()
+    for t in range(TILES):
+        row_table[t] = lax.shift_right_logical(cells[:, t * LANE : (t + 1) * LANE], 7)
+    row_copies = [pltpu.make_async_copy(row_table.at[t], row_of[t], row_sem.at[t]) for t in range(TILES)]
+    for copy in row_copies:
+        copy.start()
+    lax.fori_loop(ROWS // 512, ROWS // 256, clear, 0)
+    for copy in slot_copies[1:]:
         copy.wait()
     slot = lax.broadcasted_iota(jnp.int32, (1, SLOTS), 1)
     live = (slot < counts[0]).astype(F32)
@@ -138,7 +140,7 @@
 
     def apply(spike, g):
         for t in range(TILES):
-            rows = [row_of[t][g + k * LANE] for k in range(SPREAD)]
+            rows = [row_of[t][k, g] for k in range(SPREAD)]
             sums = [bins[k][pl.ds(rows[k], 1), :] + spike[pl.ds(t * SPREAD + k, 1), :] for k in range(SPREAD)]
             for k in range(SPREAD):
                 bins[k][pl.ds(rows[k], 1), :] = sums[k]
@@ -217,11 +219,10 @@
 def front(charges, cells, splines, counts, tabs):
     smem = pl.BlockSpec(memory_space=pltpu.SMEM)
     hbm = pl.BlockSpec(memory_space=pltpu.HBM)
-    rows = lax.shift_right_logical(cells, 7).reshape(SPREAD, TILES, LANE).transpose(1, 0, 2).reshape(-1)
     return pl.pallas_call(
         front_kernel,
         out_shape=pltpu.HBM((DEV, ZD, 2 * NU, WIDE), BF16),
-        in_specs=[hbm] * 4 + [smem] + [hbm] * 6,
+        in_specs=[hbm] * 3 + [smem] + [hbm] * 6,
         out_specs=hbm,
         scratch_shapes=[pltpu.VMEM((ROWS, LANE), F32)] * SPREAD
         + [pltpu.VMEM((LANE, LANE), F32)] * 2
@@ -231,11 +232,12 @@
         + [pltpu.VMEM(t.shape, BF16) for t in tabs]
         + [pltpu.VMEM((ZD, DEV, 2 * NU, WIDE), BF16)]
         + [pltpu.VMEM((SPREAD, SLOTS), jnp.int32), pltpu.VMEM((SPREAD, SLOTS), F32), pltpu.VMEM((1, SLOTS), F32)]
+        + [pltpu.VMEM((TILES, SPREAD, LANE), jnp.int32)]
         + [pltpu.SemaphoreType.DMA((n,)) for n in (TILES, 6, ZD, 3)]
-        + [pltpu.SMEM((SPREAD * LANE,), jnp.int32)] * TILES,
+        + [pltpu.SMEM((SPREAD, LANE), jnp.int32)] * TILES,
         compiler_params=pltpu.CompilerParams(vmem_limit_bytes=44 << 20),
         name="front",
-    )(*in_hbm(rows, cells, splines, charges.reshape(1, SLOTS)), counts, *in_hbm(*tabs))
+    )(*in_hbm(cells, splines, charges.reshape(1, SLOTS)), counts, *in_hbm(*tabs))
 
 
 WAVE = (0, 2, 1)
@@ -245,19 +247,25 @@
 PART = NZ // 2
 
 
-def green_kernel(far, spectrum, green_hbm, mirror_hbm, out_hbm, green, out, flat, sums, swapped, green_sem, out_sem, *rhs):
+def green_kernel(far, spectrum, green_hbm, mirror_hbm, out_hbm, green, out, sums, swapped, green_sem, out_sem, *rhs):
     sources = [green_hbm.at[w] for w in WAVE] + [mirror_hbm]
     fetches = [pltpu.make_async_copy(s, green.at[i], green_sem.at[i]) for i, s in enumerate(sources)]
     for fetch in fetches:
         fetch.start()
     at = [jnp.bitwise_xor(row, 2 * far[0]) for row in range(NU)]
-    for j in range(3):
-        flat[...] = spectrum[:, :, j * LANE : (j + 1) * LANE].astype(F32).reshape(NZ * 2 * NU, LANE)
-        for row in range(NU):
-            for c in range(2):
-                values = flat[pl.ds(c * NU + at[row], NZ, stride=2 * NU), :].astype(BF16)
-                to, group = (rhs[row], j) if row < 3 else (rhs[j], 3)
-                to[group, :, c * LANE : (c + 1) * LANE] = values
+    to = lax.broadcasted_iota(jnp.int32, (256, 256), 0)
+    of = lax.broadcasted_iota(jnp.int32, (256, 256), 1)
+    wanted = (to % 32) * (2 * NU) + jnp.bitwise_xor(to // 32, 2 * far[0])
+    regroup = jnp.where(of == wanted, 1.0, 0.0).astype(BF16)
+    for block in range(NZ // 32):
+        planes = slice(block * 32, (block + 1) * 32)
+        values = dot(regroup, spectrum[planes].reshape(256, WIDE)).astype(BF16)
+        for c in range(2):
+            for row in range(NU):
+                start = (c * NU + row) * 32
+                for j in range(3):
+                    to, group = (rhs[row], j) if row < 3 else (rhs[j], 3)
+                    to[group, planes, c * LANE : (c + 1) * LANE] = values[start : start + 32, j * LANE : (j + 1) * LANE]
     first = lax.broadcasted_iota(jnp.int32, (NZ, 2 * LANE), 1) % LANE == 0
     for j in range(KYB):
         swapped[j] = jnp.where(first, rhs[2][SWAP[j]], rhs[2][j])
@@ -311,7 +319,6 @@
         scratch_shapes=[
             pltpu.VMEM((NU, KYB, NZ, NZ), BF16),
             pltpu.VMEM((NZ, 2 * NU, WIDE), BF16),
-            pltpu.VMEM((NZ * 2 * NU, LANE), F32),
             pltpu.VMEM((3, PART * 2 * NU, LANE), F32),
             pltpu.VMEM((KYB, NZ, 2 * LANE), BF16),
             pltpu.SemaphoreType.DMA((NU,)),

time: 144 us -> 145 us (level)
  Pallas kernels: 33.9 us -> 36 us
  other arithmetic: 14.6 us -> 13.1 us
    pallas_call x1, Pallas kernels: 22.8 us -> 24.2 us  [front(): pl.pallas_call(front_kernel, out_shape=pltpu.HBM((DEV, ZD, 2 * NU, WIDE),...]
    reshape x1 -> x0, other arithmetic: 1.46 us -> none  [front(): lax.shift_right_logical(cells, 7).reshape(SPREAD, TILES, LANE)]
where the time goes in v5:
time: 145 us
  waiting for transfers between devices  69.7 us (48%)
  Pallas kernels  36 us (25%)
  starting transfers between devices  23.3 us (16%)
  other arithmetic  13.1 us (9%)
  local copies, waits for them, and re-layouts  1.59 us (1%)
    ppermute x1, waiting for transfers between devices, steps(): lax.ppermute(green[NU - 1], AXES, [(d, DEV - 1 - d) for d in range(DEV)])  49.5 us
    pallas_call x1, Pallas kernels, front(): pl.pallas_call(front_kernel, out_shape=pltpu.HBM((DEV, ZD, 2 * NU, WIDE),...  24.2 us
    all_to_all x1, waiting for transfers between devices, steps(): lax.all_to_all(mixed, AXES, split_axis=0, concat_axis=0, tiled=True)  20.2 us
    convert_element_type x2, other arithmetic, inverse_tables(): return (along_x.astype(BF16), along_y.astype(BF16))  13.1 us
    all_to_all x1, starting transfers between devices, steps(): lax.all_to_all(spectrum, AXES, split_axis=0, concat_axis=0, tiled=True)  11.5 us
    ppermute x1, starting transfers between devices, steps(): lax.ppermute(green[NU - 1], AXES, [(d, DEV - 1 - d) for d in range(DEV)])  8.05 us
    pallas_call x1, Pallas kernels, mix(): pl.pallas_call(green_kernel, out_shape=pltpu.HBM((NZ, 2 * NU, WIDE), BF16...  6.49 us
    pallas_call x1, Pallas kernels, back(): pl.pallas_call(back_kernel, out_shape=jax.ShapeDtypeStruct((ZD, NX, NY),...  5.28 us
  transfers between devices with their start and end apart: 3, of which 2 were waited for; matrix products, arithmetic and copies ran while one was open for 10% of the time, Pallas kernels for 0%

profile of v5, /device:TPU:1, one launch (start us, length us, event | category | flops | bytes accessed | tf_op | source)
XLA Modules:
  0.0 144.7 jit_solution(18008530785230819824)
XLA Ops:
  0.7 24.2 %front.1 = bf16[128,3,8,384]{3,2,1,0:T(8,128)(2,1)} custom-call(s32[8,2048]{1,0:T(8,128)} %cells_hbm.1, f32[8,2048]{1,0:T(8,128)} %splines_hbm.1, f32[1,2048]{1,0:T(1,128)} %bitcast.8, s32[1]{0:T(128)S(6)} %copy.14.counts, bf16[512,512]{1,0:T(8,128)(2,1)} %constant.42.clone.yh_hbm, bf16[512,512]{1,0:T(8,128)(2,1)} %constant.43.clone.yl_hbm, ...), custom_call_target="tpu_custom_call" | custom-call | tf_op jit(solution)/shard_map/front/pallas_call | solution.py:222
  24.9 11.5 %all-to-all-start = ((bf16[128,3,8,384]{3,2,1,0:T(8,128)(2,1)}), bf16[128,3,8,384]{3,2,1,0:T(8,128)(2,1)S(1)}, u32[]{:S(2)}, u32[]{:S(2)}) async-start(bf16[128,3,8,384]{3,2,1,0:T(8,128)(2,1)} %front.1), calls=%async_computation | async-start | bytes 4718592 | tf_op jit(solution)/shard_map/all_to_all | solution.py:395
  36.4 1.4 slice_bitcast_fusion
  37.8 8.1 %collective-permute-start = (bf16[4,384,384]{2,1,0:T(8,128)(2,1)S(1)}, bf16[4,384,384]{2,1,0:T(8,128)(2,1)}, u32[]{:S(2)}, u32[]{:S(2)}) collective-permute-start(bf16[4,384,384]{2,1,0:T(8,128)(2,1)S(1)} %slice_bitcast_fusion), channel_id=1, source_target_pairs={{0,127},{1,126},{2,125},{3,124},{4,123},{5,122},{6,121},{7,120},{8... | collective-permute-start | bytes 3538952 | tf_op jit(solution)/shard_map/ppermute | solution.py:393
  45.8 49.5 %collective-permute-done.mirror_hbm = bf16[4,384,384]{2,1,0:T(8,128)(2,1)} collective-permute-done((bf16[4,384,384]{2,1,0:T(8,128)(2,1)S(1)}, bf16[4,384,384]{2,1,0:T(8,128)(2,1)}, u32[]{:S(2)}, u32[]{:S(2)}) %collective-permute-start) | collective-permute-done | bytes 1179680 | tf_op jit(solution)/shard_map/ppermute | solution.py:393
  95.3 0.0 all-to-all-done
  95.3 6.5 %mix.1 = bf16[384,8,384]{2,1,0:T(8,128)(2,1)} custom-call(s32[1]{0:T(128)} %bitcast.far, bf16[384,8,384]{2,1,0:T(8,128)(2,1)S(1)} %bitcast.6, bf16[4,4,384,384]{3,2,1,0:T(8,128)(2,1)} %green_hbm.1, bf16[4,384,384]{2,1,0:T(8,128)(2,1)} %collective-permute-done.mirror_hbm), custom_call_target="tpu_custom_call" | custom-call | tf_op jit(solution)/shard_map/mix/pallas_call | solution.py:313
  101.8 0.0 copy-start
  101.9 0.0 copy-start.1
  101.9 3.8 %all-to-all-start.1 = ((bf16[128,3,8,384]{3,2,1,0:T(8,128)(2,1)}), bf16[128,3,8,384]{3,2,1,0:T(8,128)(2,1)S(1)}, u32[]{:S(2)}, u32[]{:S(2)}) async-start(bf16[128,3,8,384]{3,2,1,0:T(8,128)(2,1)} %bitcast.7), calls=%async_computation.1 | async-start | bytes 4718592 | tf_op jit(solution)/shard_map/all_to_all | solution.py:397
  105.7 0.1 mul.62
  105.8 0.1 mul.63
  105.9 5.1 %multiply_convert_fusion.1.y_hbm = bf16[512,512]{1,0:T(8,128)(2,1)} fusion(s32[512]{0:T(512)S(1)} %fusion, s32[512]{0:T(512)S(1)} %get-tuple-element.5, s32[512]{0:T(512)S(1)} %get-tuple-element.6, pred[512]{0:T(512)(128)(4,1)S(1)} %iota_compare_fusion.1), kind=kLoop, calls=%fused_computation.2 | loop fusion | flops 2097152 | bytes 530944 | tf_op jit(solution)/shard_map/convert_element_type | solution.py:71
  111.0 0.0 copy-done
  111.0 0.0 copy-done.1
  111.0 8.0 %multiply_convert_fusion.x_hbm = bf16[512,1024]{1,0:T(8,128)(2,1)} fusion(f32[1024]{0:T(1024)S(1)} %copy-done.1, s32[1024]{0:T(1024)S(1)} %mul.63, s32[1024]{0:T(1024)S(1)} %copy-done), kind=kLoop, calls=%fused_computation | loop fusion | flops 3670016 | bytes 1060864 | tf_op jit(solution)/shard_map/convert_element_type | solution.py:71
  119.0 20.2 %all-to-all-done.1.mixed = bf16[128,3,8,384]{3,2,1,0:T(8,128)(2,1)S(1)} async-done(((bf16[128,3,8,384]{3,2,1,0:T(8,128)(2,1)}), bf16[128,3,8,384]{3,2,1,0:T(8,128)(2,1)S(1)}, u32[]{:S(2)}, u32[]{:S(2)}) %all-to-all-start.1) | async-done | bytes 2359328 | tf_op jit(solution)/shard_map/all_to_all | solution.py:397
  139.2 5.3 %back.1 = f32[3,512,512]{2,1,0:T(8,128)} custom-call(bf16[128,3,8,384]{3,2,1,0:T(8,128)(2,1)S(1)} %all-to-all-done.1.mixed, bf16[512,1024]{1,0:T(8,128)(2,1)} %multiply_convert_fusion.x_hbm, bf16[512,512]{1,0:T(8,128)(2,1)} %multiply_convert_fusion.1.y_hbm), custom_call_target="tpu_custom_call" | custom-call | tf_op jit(solution)/shard_map/back/pallas_call | solution.py:372
  (5 shorter events, 0.0 us)
Async XLA Ops:
  24.9 70.4 %all-to-all-start = ((bf16[128,3,8,384]{3,2,1,0:T(8,128)(2,1)}), bf16[128,3,8,384]{3,2,1,0:T(8,128)(2,1)S(1)}, u32[]{:S(2)}, u32[]{:S(2)}) async-start(bf16[128,3,8,384]{3,2,1,0:T(8,128)(2,1)} %front.1), calls=%async_computation | async-start | bytes 4718592 | tf_op jit(solution)/shard_map/all_to_all | solution.py:395
  37.8 57.6 %collective-permute-start = (bf16[4,384,384]{2,1,0:T(8,128)(2,1)S(1)}, bf16[4,384,384]{2,1,0:T(8,128)(2,1)}, u32[]{:S(2)}, u32[]{:S(2)}) collective-permute-start(bf16[4,384,384]{2,1,0:T(8,128)(2,1)S(1)} %slice_bitcast_fusion), channel_id=1, source_target_pairs={{0,127},{1,126},{2,125},{3,124},{4,123},{5,122},{6,121},{7,120},{8... | collective-permute-start | bytes 3538952 | tf_op jit(solution)/shard_map/ppermute | solution.py:393
  101.8 9.2 %copy-start = (s32[1024]{0:T(1024)S(1)}, s32[1024]{0:T(1024)}, u32[]{:S(2)}) copy-start(s32[1024]{0:T(1024)} %constant.52) | copy-start | bytes 12292
  101.9 9.1 %copy-start.1 = (f32[1024]{0:T(1024)S(1)}, f32[1024]{0:T(1024)}, u32[]{:S(2)}) copy-start(f32[1024]{0:T(1024)} %constant.53) | copy-start | bytes 12292
  101.9 37.4 %all-to-all-start.1 = ((bf16[128,3,8,384]{3,2,1,0:T(8,128)(2,1)}), bf16[128,3,8,384]{3,2,1,0:T(8,128)(2,1)S(1)}, u32[]{:S(2)}, u32[]{:S(2)}) async-start(bf16[128,3,8,384]{3,2,1,0:T(8,128)(2,1)} %bitcast.7), calls=%async_computation.1 | async-start | bytes 4718592 | tf_op jit(solution)/shard_map/all_to_all | solution.py:397

commit v6 on v4

--- a/solution.py
+++ b/solution.py
@@ -55,20 +55,11 @@
     return tuple(out)
 
 
-def inverse_tables():
-    wave = waves().reshape(DEV, 1, NU).repeat(2, axis=1).reshape(1, 2 * NX)
-    used = jnp.asarray(wave >= 0, F32)
-    wave = jnp.asarray(wave, jnp.int32)
-    quarter = jnp.tile(jnp.repeat(jnp.arange(2, dtype=jnp.int32), NU), DEV)[None, :] * (NX // 4)
-    x = lax.broadcasted_iota(jnp.int32, (NX, 2 * NX), 0)
-    step = 2.0 * np.pi / NX
-    along_x = jnp.cos(((x * wave + quarter) & (NX - 1)).astype(F32) * step) * used
-    row = lax.broadcasted_iota(jnp.int32, (NY, NY), 0)
-    y = lax.broadcasted_iota(jnp.int32, (NY, NY), 1)
-    phase = (row & (HALF - 1)) * y - jnp.where(row < HALF, 0, NY // 4)
-    phase = jnp.where(row == HALF, (y + 1) * (NY // 2), phase)
-    along_y = jnp.cos((phase & (NY - 1)).astype(F32) * step) / 512.0
-    return along_x.astype(BF16), along_y.astype(BF16)
+def inverse_table():
+    wave = waves()[:, None, :]
+    a = angles(np.arange(NX // 2), wave.reshape(-1)).reshape(NX // 2, DEV, 1, NU)
+    table = np.concatenate([np.cos(a), -np.sin(a)], axis=2) * (wave >= 0)
+    return table.reshape(NX // 2, 2 * NX).astype(BF16)
 
 
 def in_hbm(*arrays):
@@ -77,6 +68,10 @@
 
 def dot(a, b):
     return jnp.dot(a, b, preferred_element_type=F32)
+
+
+def dot_nt(a, b):
+    return lax.dot_general(a, b, (((1,), (1,)), ((), ())), preferred_element_type=F32)
 
 
 def turn(q):
@@ -245,7 +240,7 @@
 PART = NZ // 2
 
 
-def green_kernel(far, spectrum, green_hbm, mirror_hbm, out_hbm, green, out, flat, sums, swapped, green_sem, out_sem, *rhs):
+def green_kernel(far, spectrum, green_hbm, mirror_hbm, out, green, flat, sums, swapped, green_sem, *rhs):
     sources = [green_hbm.at[w] for w in WAVE] + [mirror_hbm]
     fetches = [pltpu.make_async_copy(s, green.at[i], green_sem.at[i]) for i, s in enumerate(sources)]
     for fetch in fetches:
@@ -262,7 +257,6 @@
     for j in range(KYB):
         swapped[j] = jnp.where(first, rhs[2][SWAP[j]], rhs[2][j])
     first = first[:PART]
-    sends = []
     for part in range(2):
         planes = slice(part * PART, (part + 1) * PART)
         for row in range(3):
@@ -283,8 +277,8 @@
             groups = (
                 (t0[:, :LANE], t0[:, LANE:]),
                 (t1[:, :LANE], t1[:, LANE:]),
-                (-d0[:, LANE:], d0[:, :LANE]),
-                (-d1[:, LANE:], d1[:, :LANE]),
+                (d0[:, LANE:], -d0[:, :LANE]),
+                (d1[:, LANE:], -d1[:, :LANE]),
             )
             for j, group in enumerate(groups):
                 for c in range(2):
@@ -292,11 +286,6 @@
                     sums[to, pl.ds(c * NU + at[slot], PART, stride=2 * NU), :] = group[c]
         for j in range(3):
             out[planes, :, j * LANE : (j + 1) * LANE] = sums[j].astype(BF16).reshape(PART, 2 * NU, LANE)
-        send = pltpu.make_async_copy(out.at[planes], out_hbm.at[planes], out_sem.at[part])
-        send.start()
-        sends.append(send)
-    for send in sends:
-        send.wait()
 
 
 def mix(pencil, green, mirror):
@@ -304,18 +293,16 @@
     hbm = pl.BlockSpec(memory_space=pltpu.HBM)
     return pl.pallas_call(
         green_kernel,
-        out_shape=pltpu.HBM((NZ, 2 * NU, WIDE), BF16),
+        out_shape=pltpu.VMEM((NZ, 2 * NU, WIDE), BF16),
         in_specs=[pl.BlockSpec(memory_space=pltpu.SMEM), vmem, hbm, hbm],
-        out_specs=hbm,
+        out_specs=vmem,
         compiler_params=pltpu.CompilerParams(vmem_limit_bytes=36 << 20),
         scratch_shapes=[
             pltpu.VMEM((NU, KYB, NZ, NZ), BF16),
-            pltpu.VMEM((NZ, 2 * NU, WIDE), BF16),
             pltpu.VMEM((NZ * 2 * NU, LANE), F32),
             pltpu.VMEM((3, PART * 2 * NU, LANE), F32),
             pltpu.VMEM((KYB, NZ, 2 * LANE), BF16),
             pltpu.SemaphoreType.DMA((NU,)),
-            pltpu.SemaphoreType.DMA((2,)),
         ]
         + [pltpu.VMEM((KYB, NZ, 2 * LANE), BF16)] * 3,
         name="mix",
@@ -324,9 +311,8 @@
 
 def back_kernel(mixed, x_hbm, y_hbm, out_hbm, along_x, along_y, out, rest, tab_sem, out_sem):
     fetches = [
-        pltpu.make_async_copy(x_hbm.at[pl.ds(0, HALF)], along_x.at[pl.ds(0, HALF)], tab_sem.at[0]),
+        pltpu.make_async_copy(x_hbm, along_x.at[pl.ds(0, HALF)], tab_sem.at[0]),
         pltpu.make_async_copy(y_hbm, along_y, tab_sem.at[1]),
-        pltpu.make_async_copy(x_hbm.at[pl.ds(HALF, HALF)], along_x.at[pl.ds(HALF, HALF)], tab_sem.at[2]),
     ]
     for fetch in fetches:
         fetch.start()
@@ -345,13 +331,17 @@
         rest[:, :, :LANE] = mixed[:, z, :, 2 * LANE :]
         for h in range(2):
             rows = pl.ds(h * HALF, HALF)
-            if z == 0:
-                fetches[2 * h].wait()
+            if z == 0 and h == 0:
+                fetches[0].wait()
+            elif z == 0:
+                place = lax.broadcasted_iota(jnp.int32, (1, 2 * NX), 1)
+                sign = jnp.where(place % NU == jnp.where(place < NX, 2, 0), -1.0, 1.0).astype(BF16)
+                along_x[HALF:, :] = along_x[:HALF, :] * sign
             front = dot(along_x[rows, :], mixed[:, z, :, : 2 * LANE].reshape(2 * NX, 2 * LANE)).astype(BF16)
             tail = dot(along_x[rows, :], rest[...].reshape(2 * NX, 2 * LANE)).astype(BF16)
             if z == 0 and h == 0:
                 fetches[1].wait()
-            out[z, rows, :] = dot(front, along_y[: 2 * LANE, :]) + dot(tail, along_y[2 * LANE :, :])
+            out[z, rows, :] = dot_nt(front, along_y[:, : 2 * LANE]) + dot_nt(tail, along_y[:, 2 * LANE :])
             send = pltpu.make_async_copy(out.at[z, rows], out_hbm.at[z, rows], out_sem.at[2 * z + h])
             send.start()
             sends.append(send)
@@ -373,7 +363,7 @@
             pltpu.VMEM((NY, NY), BF16),
             pltpu.VMEM((ZD, NX, NY), F32),
             pltpu.VMEM((DEV, 2 * NU, 2 * LANE), BF16),
-            pltpu.SemaphoreType.DMA((3,)),
+            pltpu.SemaphoreType.DMA((2,)),
             pltpu.SemaphoreType.DMA((2 * ZD,)),
         ],
         name="back",
@@ -382,13 +372,12 @@
 
 def steps(charges, cells, splines, counts, green):
     forward = tuple(jnp.asarray(t) for t in forward_tables())
-    inverse_x, inverse_y = inverse_tables()
     mirror = lax.ppermute(green[NU - 1], AXES, [(d, DEV - 1 - d) for d in range(DEV)])
     spectrum = front(charges, cells, splines, counts, forward)
     pencil = lax.all_to_all(spectrum, AXES, split_axis=0, concat_axis=0, tiled=True)
     mixed = mix(pencil, green, mirror).reshape(DEV, ZD, 2 * NU, WIDE)
     returned = lax.all_to_all(mixed, AXES, split_axis=0, concat_axis=0, tiled=True)
-    return back(returned, inverse_x, inverse_y)
+    return back(returned, jnp.asarray(inverse_table()), forward[0])
 
 
 def solution(mesh):

time: 144 us -> 143 us (level)
  blocking collectives: 0 us -> 37 us
  waiting for transfers between devices: 69.7 us -> 49.5 us
  other arithmetic: 14.6 us -> 1.46 us
  starting transfers between devices: 23.4 us -> 19.6 us
    all_to_all x0 -> x1, blocking collectives: none -> 37 us  [steps(): lax.all_to_all(mixed, AXES, split_axis=0, concat_axis=0, tiled=True)]
    all_to_all x1 -> x0, waiting for transfers between devices: 20.2 us -> none  [steps(): lax.all_to_all(mixed, AXES, split_axis=0, concat_axis=0, tiled=True)]
    convert_element_type x2 -> x0, other arithmetic: 13.1 us -> none  [inverse_tables(): return (along_x.astype(BF16), along_y.astype(BF16))]
    all_to_all x1 -> x0, starting transfers between devices: 3.79 us -> none  [steps(): lax.all_to_all(mixed, AXES, split_axis=0, concat_axis=0, tiled=True)]
  transfers between devices with their start and end apart: 3 -> 2, of which waited for: 2 -> 1; matrix products, arithmetic and copies ran while one was open for 10% -> 1% of each run, Pallas kernels for 0% -> 0%
where the time goes in v6:
time: 143 us; the launch traced here: 142 us
  waiting for transfers between devices  49.5 us (35%)
  blocking collectives  37 us (26%)
  Pallas kernels  32.7 us (23%)
  starting transfers between devices  19.6 us (14%)
  other arithmetic  1.46 us (1%)
    ppermute x1, waiting for transfers between devices, steps(): lax.ppermute(green[NU - 1], AXES, [(d, DEV - 1 - d) for d in range(DEV)])  49.5 us
    all_to_all x1, blocking collectives, steps(): lax.all_to_all(mixed, AXES, split_axis=0, concat_axis=0, tiled=True)  37 us
    pallas_call x1, Pallas kernels, front(): pl.pallas_call(front_kernel, out_shape=pltpu.HBM((DEV, ZD, 2 * NU, WIDE),...  22.8 us
    all_to_all x1, starting transfers between devices, steps(): lax.all_to_all(spectrum, AXES, split_axis=0, concat_axis=0, tiled=True)  11.5 us
    ppermute x1, starting transfers between devices, steps(): lax.ppermute(green[NU - 1], AXES, [(d, DEV - 1 - d) for d in range(DEV)])  8.05 us
    pallas_call x1, Pallas kernels, back(): pl.pallas_call(back_kernel, out_shape=jax.ShapeDtypeStruct((ZD, NX, NY),...  5.12 us
    pallas_call x1, Pallas kernels, mix(): pl.pallas_call(green_kernel, out_shape=pltpu.VMEM((NZ, 2 * NU, WIDE), BF1...  4.85 us
  transfers between devices with their start and end apart: 2, of which 1 were waited for; matrix products, arithmetic and copies ran while one was open for 1% of the time, Pallas kernels for 0%

profile of v6, /device:TPU:1, one launch (start us, length us, event | category | flops | bytes accessed | tf_op | source)
XLA Modules:
  0.0 142.4 jit_solution(2892792527921081987)
XLA Ops:
  0.0 1.5 %shift-right-logical_bitcast_fusion.rows_hbm = s32[16384]{0:T(1024)} fusion(s32[8,2048]{1,0:T(8,128)} %cells_hbm.1), kind=kLoop, calls=%fused_computation.1 | loop fusion | flops 16384 | bytes 131072 | tf_op jit(solution)/shard_map/reshape | solution.py:215
  2.1 22.8 %front.1 = bf16[128,3,8,384]{3,2,1,0:T(8,128)(2,1)} custom-call(s32[16384]{0:T(1024)} %shift-right-logical_bitcast_fusion.rows_hbm, s32[8,2048]{1,0:T(8,128)} %cells_hbm.1, f32[8,2048]{1,0:T(8,128)} %splines_hbm.1, f32[1,2048]{1,0:T(1,128)} %bitcast.14, s32[1]{0:T(128)S(6)} %copy.13.counts, bf16[512,512]{1,0:T(8,128)(2,1)} %constant.22.clone.yh_hbm.y_hbm, ...), custom_call_target="tpu_custom_call" | custom-call | tf_op jit(solution)/shard_map/front/pallas_call | solution.py:216
  24.9 11.5 %all-to-all-start = ((bf16[128,3,8,384]{3,2,1,0:T(8,128)(2,1)}), bf16[128,3,8,384]{3,2,1,0:T(8,128)(2,1)S(1)}, u32[]{:S(2)}, u32[]{:S(2)}) async-start(bf16[128,3,8,384]{3,2,1,0:T(8,128)(2,1)} %front.1), calls=%async_computation | async-start | bytes 4718592 | tf_op jit(solution)/shard_map/all_to_all | solution.py:377
  36.4 1.4 slice_bitcast_fusion
  37.8 8.1 %collective-permute-start = (bf16[4,384,384]{2,1,0:T(8,128)(2,1)S(1)}, bf16[4,384,384]{2,1,0:T(8,128)(2,1)}, u32[]{:S(2)}, u32[]{:S(2)}) collective-permute-start(bf16[4,384,384]{2,1,0:T(8,128)(2,1)S(1)} %slice_bitcast_fusion), channel_id=1, source_target_pairs={{0,127},{1,126},{2,125},{3,124},{4,123},{5,122},{6,121},{7,120},{8... | collective-permute-start | bytes 3538952 | tf_op jit(solution)/shard_map/ppermute | solution.py:375
  45.9 49.5 %collective-permute-done.mirror_hbm = bf16[4,384,384]{2,1,0:T(8,128)(2,1)} collective-permute-done((bf16[4,384,384]{2,1,0:T(8,128)(2,1)S(1)}, bf16[4,384,384]{2,1,0:T(8,128)(2,1)}, u32[]{:S(2)}, u32[]{:S(2)}) %collective-permute-start) | collective-permute-done | bytes 1179680 | tf_op jit(solution)/shard_map/ppermute | solution.py:375
  95.4 0.0 all-to-all-done
  95.4 4.8 %mix.1 = bf16[384,8,384]{2,1,0:T(8,128)(2,1)S(1)} custom-call(s32[1]{0:T(128)} %bitcast.far, bf16[384,8,384]{2,1,0:T(8,128)(2,1)S(1)} %bitcast.12, bf16[4,4,384,384]{3,2,1,0:T(8,128)(2,1)} %green_hbm.1, bf16[4,384,384]{2,1,0:T(8,128)(2,1)} %collective-permute-done.mirror_hbm), custom_call_target="tpu_custom_call" | custom-call | tf_op jit(solution)/shard_map/mix/pallas_call | solution.py:294
  100.2 37.0 %all_to_all.10.mixed = bf16[128,3,8,384]{3,2,1,0:T(8,128)(2,1)S(1)} all-to-all(bf16[128,3,8,384]{3,2,1,0:T(8,128)(2,1)S(1)} %bitcast.13), channel_id=1, replica_groups=mesh['zg'=2,'xy'=64] {'zg','xy'}, dimensions={0} | all-to-all | bytes 4718592 | tf_op jit(solution)/shard_map/all_to_all | solution.py:379
  137.2 5.1 %back.1 = f32[3,512,512]{2,1,0:T(8,128)} custom-call(bf16[128,3,8,384]{3,2,1,0:T(8,128)(2,1)S(1)} %all_to_all.10.mixed, bf16[256,1024]{1,0:T(8,128)(2,1)} %constant.28.clone.x_hbm, bf16[512,512]{1,0:T(8,128)(2,1)} %constant.22.clone.yh_hbm.y_hbm), custom_call_target="tpu_custom_call" | custom-call | tf_op jit(solution)/shard_map/back/pallas_call | solution.py:355
Async XLA Ops:
  24.9 70.5 %all-to-all-start = ((bf16[128,3,8,384]{3,2,1,0:T(8,128)(2,1)}), bf16[128,3,8,384]{3,2,1,0:T(8,128)(2,1)S(1)}, u32[]{:S(2)}, u32[]{:S(2)}) async-start(bf16[128,3,8,384]{3,2,1,0:T(8,128)(2,1)} %front.1), calls=%async_computation | async-start | bytes 4718592 | tf_op jit(solution)/shard_map/all_to_all | solution.py:377
  37.8 57.6 %collective-permute-start = (bf16[4,384,384]{2,1,0:T(8,128)(2,1)S(1)}, bf16[4,384,384]{2,1,0:T(8,128)(2,1)}, u32[]{:S(2)}, u32[]{:S(2)}) collective-permute-start(bf16[4,384,384]{2,1,0:T(8,128)(2,1)S(1)} %slice_bitcast_fusion), channel_id=1, source_target_pairs={{0,127},{1,126},{2,125},{3,124},{4,123},{5,122},{6,121},{7,120},{8... | collective-permute-start | bytes 3538952 | tf_op jit(solution)/shard_map/ppermute | solution.py:375

commit v7 on v6

--- a/solution.py
+++ b/solution.py
@@ -240,9 +240,13 @@
 PART = NZ // 2
 
 
-def green_kernel(far, spectrum, green_hbm, mirror_hbm, out, green, flat, sums, swapped, green_sem, *rhs):
+def green_kernel(
+    far, spectrum, green_hbm, mirror_hbm, x_hbm, y_hbm, out, x_out, y_out, green, flat, sums, swapped, green_sem, *rhs
+):
     sources = [green_hbm.at[w] for w in WAVE] + [mirror_hbm]
     fetches = [pltpu.make_async_copy(s, green.at[i], green_sem.at[i]) for i, s in enumerate(sources)]
+    fetches.append(pltpu.make_async_copy(x_hbm, x_out, green_sem.at[4]))
+    fetches.append(pltpu.make_async_copy(y_hbm, y_out, green_sem.at[5]))
     for fetch in fetches:
         fetch.start()
     at = [jnp.bitwise_xor(row, 2 * far[0]) for row in range(NU)]
@@ -286,36 +290,32 @@
                     sums[to, pl.ds(c * NU + at[slot], PART, stride=2 * NU), :] = group[c]
         for j in range(3):
             out[planes, :, j * LANE : (j + 1) * LANE] = sums[j].astype(BF16).reshape(PART, 2 * NU, LANE)
-
-
-def mix(pencil, green, mirror):
+    for fetch in fetches[4:]:
+        fetch.wait()
+
+
+def mix(pencil, green, mirror, *tabs):
     vmem = pl.BlockSpec(memory_space=pltpu.VMEM)
     hbm = pl.BlockSpec(memory_space=pltpu.HBM)
     return pl.pallas_call(
         green_kernel,
-        out_shape=pltpu.VMEM((NZ, 2 * NU, WIDE), BF16),
-        in_specs=[pl.BlockSpec(memory_space=pltpu.SMEM), vmem, hbm, hbm],
-        out_specs=vmem,
+        out_shape=(pltpu.VMEM((NZ, 2 * NU, WIDE), BF16), *(pltpu.VMEM(t.shape, BF16) for t in tabs)),
+        in_specs=[pl.BlockSpec(memory_space=pltpu.SMEM), vmem, hbm, hbm, hbm, hbm],
+        out_specs=(vmem, vmem, vmem),
         compiler_params=pltpu.CompilerParams(vmem_limit_bytes=36 << 20),
         scratch_shapes=[
             pltpu.VMEM((NU, KYB, NZ, NZ), BF16),
             pltpu.VMEM((NZ * 2 * NU, LANE), F32),
             pltpu.VMEM((3, PART * 2 * NU, LANE), F32),
             pltpu.VMEM((KYB, NZ, 2 * LANE), BF16),
-            pltpu.SemaphoreType.DMA((NU,)),
+            pltpu.SemaphoreType.DMA((6,)),
         ]
         + [pltpu.VMEM((KYB, NZ, 2 * LANE), BF16)] * 3,
         name="mix",
-    )(lax.axis_index("zg").astype(jnp.int32).reshape(1), pencil.reshape(NZ, 2 * NU, WIDE), *in_hbm(green, mirror))
-
-
-def back_kernel(mixed, x_hbm, y_hbm, out_hbm, along_x, along_y, out, rest, tab_sem, out_sem):
-    fetches = [
-        pltpu.make_async_copy(x_hbm, along_x.at[pl.ds(0, HALF)], tab_sem.at[0]),
-        pltpu.make_async_copy(y_hbm, along_y, tab_sem.at[1]),
-    ]
-    for fetch in fetches:
-        fetch.start()
+    )(lax.axis_index("zg").astype(jnp.int32).reshape(1), pencil.reshape(NZ, 2 * NU, WIDE), *in_hbm(green, mirror, *tabs))
+
+
+def back_kernel(mixed, half_x, along_y, out_hbm, far_x, out, rest, out_sem):
     row_of_tile = lax.broadcasted_iota(jnp.int32, (DEV // 2, 2 * NU, LANE), 1) % NU
     sends = []
     for z in range(ZD):
@@ -331,16 +331,13 @@
         rest[:, :, :LANE] = mixed[:, z, :, 2 * LANE :]
         for h in range(2):
             rows = pl.ds(h * HALF, HALF)
-            if z == 0 and h == 0:
-                fetches[0].wait()
-            elif z == 0:
+            if z == 0 and h == 1:
                 place = lax.broadcasted_iota(jnp.int32, (1, 2 * NX), 1)
                 sign = jnp.where(place % NU == jnp.where(place < NX, 2, 0), -1.0, 1.0).astype(BF16)
-                along_x[HALF:, :] = along_x[:HALF, :] * sign
-            front = dot(along_x[rows, :], mixed[:, z, :, : 2 * LANE].reshape(2 * NX, 2 * LANE)).astype(BF16)
-            tail = dot(along_x[rows, :], rest[...].reshape(2 * NX, 2 * LANE)).astype(BF16)
-            if z == 0 and h == 0:
-                fetches[1].wait()
+                far_x[...] = half_x[...] * sign
+            along_x = (half_x, far_x)[h]
+            front = dot(along_x[...], mixed[:, z, :, : 2 * LANE].reshape(2 * NX, 2 * LANE)).astype(BF16)
+            tail = dot(along_x[...], rest[...].reshape(2 * NX, 2 * LANE)).astype(BF16)
             out[z, rows, :] = dot_nt(front, along_y[:, : 2 * LANE]) + dot_nt(tail, along_y[:, 2 * LANE :])
             send = pltpu.make_async_copy(out.at[z, rows], out_hbm.at[z, rows], out_sem.at[2 * z + h])
             send.start()
@@ -355,19 +352,17 @@
     return pl.pallas_call(
         back_kernel,
         out_shape=jax.ShapeDtypeStruct((ZD, NX, NY), F32),
-        in_specs=[vmem, hbm, hbm],
+        in_specs=[vmem, vmem, vmem],
         out_specs=hbm,
         compiler_params=pltpu.CompilerParams(vmem_limit_bytes=24 << 20),
         scratch_shapes=[
-            pltpu.VMEM((NX, 2 * NX), BF16),
-            pltpu.VMEM((NY, NY), BF16),
+            pltpu.VMEM((NX // 2, 2 * NX), BF16),
             pltpu.VMEM((ZD, NX, NY), F32),
             pltpu.VMEM((DEV, 2 * NU, 2 * LANE), BF16),
-            pltpu.SemaphoreType.DMA((2,)),
             pltpu.SemaphoreType.DMA((2 * ZD,)),
         ],
         name="back",
-    )(returned, *in_hbm(inverse_x, inverse_y))
+    )(returned, inverse_x, inverse_y)
 
 
 def steps(charges, cells, splines, counts, green):
@@ -375,9 +370,10 @@
     mirror = lax.ppermute(green[NU - 1], AXES, [(d, DEV - 1 - d) for d in range(DEV)])
     spectrum = front(charges, cells, splines, counts, forward)
     pencil = lax.all_to_all(spectrum, AXES, split_axis=0, concat_axis=0, tiled=True)
-    mixed = mix(pencil, green, mirror).reshape(DEV, ZD, 2 * NU, WIDE)
+    mixed, *along = mix(pencil, green, mirror, jnp.asarray(inverse_table()), forward[0])
+    mixed = mixed.reshape(DEV, ZD, 2 * NU, WIDE)
     returned = lax.all_to_all(mixed, AXES, split_axis=0, concat_axis=0, tiled=True)
-    return back(returned, jnp.asarray(inverse_table()), forward[0])
+    return back(returned, *along)
 
 
 def solution(mesh):

time: 143 us -> 142 us (level)
  local copies, waits for them, and re-layouts: 1.39 us -> 3.43 us
  transfers between devices with their start and end apart: 2 -> 2, of which waited for: 1 -> 1; matrix products, arithmetic and copies ran while one was open for 1% -> 2% of each run, Pallas kernels for 0% -> 0%
where the time goes in v7:
time: 142 us
  waiting for transfers between devices  48.5 us (34%)
  blocking collectives  36.7 us (26%)
  Pallas kernels  31.5 us (22%)
  starting transfers between devices  19.5 us (14%)
  local copies, waits for them, and re-layouts  3.43 us (2%)
  other arithmetic  1.47 us (1%)
    ppermute x1, waiting for transfers between devices, steps(): lax.ppermute(green[NU - 1], AXES, [(d, DEV - 1 - d) for d in range(DEV)])  48.5 us
    all_to_all x1, blocking collectives, steps(): lax.all_to_all(mixed, AXES, split_axis=0, concat_axis=0, tiled=True)  36.7 us
    pallas_call x1, Pallas kernels, front(): pl.pallas_call(front_kernel, out_shape=pltpu.HBM((DEV, ZD, 2 * NU, WIDE),...  22.7 us
    all_to_all x1, starting transfers between devices, steps(): lax.all_to_all(spectrum, AXES, split_axis=0, concat_axis=0, tiled=True)  11.5 us
    ppermute x1, starting transfers between devices, steps(): lax.ppermute(green[NU - 1], AXES, [(d, DEV - 1 - d) for d in range(DEV)])  7.97 us
    pallas_call x1, Pallas kernels, mix(): pl.pallas_call(green_kernel, out_shape=(pltpu.VMEM((NZ, 2 * NU, WIDE), BF...  4.85 us
    pallas_call x1, Pallas kernels, back(): pl.pallas_call(back_kernel, out_shape=jax.ShapeDtypeStruct((ZD, NX, NY),...  3.96 us
  transfers between devices with their start and end apart: 2, of which 1 were waited for; matrix products, arithmetic and copies ran while one was open for 2% of the time, Pallas kernels for 0%

profile of v7, /device:TPU:1, one launch (start us, length us, event | category | flops | bytes accessed | tf_op | source)
XLA Modules:
  0.0 141.8 jit_solution(7765612981877580421)
XLA Ops:
  0.7 1.5 %shift-right-logical_bitcast_fusion.rows_hbm = s32[16384]{0:T(1024)} fusion(s32[8,2048]{1,0:T(8,128)} %cells_hbm.1), kind=kLoop, calls=%fused_computation.1 | loop fusion | flops 16384 | bytes 131072 | tf_op jit(solution)/shard_map/reshape | solution.py:215
  2.1 22.7 %front.1 = bf16[128,3,8,384]{3,2,1,0:T(8,128)(2,1)} custom-call(s32[16384]{0:T(1024)} %shift-right-logical_bitcast_fusion.rows_hbm, s32[8,2048]{1,0:T(8,128)} %cells_hbm.1, f32[8,2048]{1,0:T(8,128)} %splines_hbm.1, f32[1,2048]{1,0:T(1,128)} %bitcast.14, s32[1]{0:T(128)S(6)} %copy.13.counts, bf16[512,512]{1,0:T(8,128)(2,1)} %constant.22.clone.yh_hbm.y_hbm, ...), custom_call_target="tpu_custom_call" | custom-call | tf_op jit(solution)/shard_map/front/pallas_call | solution.py:216
  24.9 11.5 %all-to-all-start = ((bf16[128,3,8,384]{3,2,1,0:T(8,128)(2,1)}), bf16[128,3,8,384]{3,2,1,0:T(8,128)(2,1)S(1)}, u32[]{:S(2)}, u32[]{:S(2)}) async-start(bf16[128,3,8,384]{3,2,1,0:T(8,128)(2,1)} %front.1), calls=%async_computation | async-start | bytes 4718592 | tf_op jit(solution)/shard_map/all_to_all | solution.py:372
  36.4 2.4 %slice_bitcast_fusion = bf16[4,384,384]{2,1,0:T(8,128)(2,1)} fusion(bf16[4,4,384,384]{3,2,1,0:T(8,128)(2,1)} %green_hbm.1), kind=kLoop, calls=%fused_computation | loop fusion | bytes 2359296 | tf_op jit(solution)/shard_map/squeeze | solution.py:370
  38.8 8.0 %collective-permute-start = (bf16[4,384,384]{2,1,0:T(8,128)(2,1)}, bf16[4,384,384]{2,1,0:T(8,128)(2,1)S(1)}, u32[]{:S(2)}, u32[]{:S(2)}) collective-permute-start(bf16[4,384,384]{2,1,0:T(8,128)(2,1)} %slice_bitcast_fusion), channel_id=1, source_target_pairs={{0,127},{1,126},{2,125},{3,124},{4,123},{5,122},{6,121},{7,120},{8... | collective-permute-start | bytes 3538952 | tf_op jit(solution)/shard_map/ppermute | solution.py:370
  46.8 48.5 %collective-permute-done.mirror_hbm = bf16[4,384,384]{2,1,0:T(8,128)(2,1)S(1)} collective-permute-done((bf16[4,384,384]{2,1,0:T(8,128)(2,1)}, bf16[4,384,384]{2,1,0:T(8,128)(2,1)S(1)}, u32[]{:S(2)}, u32[]{:S(2)}) %collective-permute-start) | collective-permute-done | bytes 1179680 | tf_op jit(solution)/shard_map/ppermute | solution.py:370
  95.2 0.0 copy-start
  95.2 0.0 all-to-all-done
  95.3 1.0 copy-done
  96.3 4.8 %mix.1 = (bf16[384,8,384]{2,1,0:T(8,128)(2,1)S(1)}, bf16[256,1024]{1,0:T(8,128)(2,1)S(1)}, bf16[512,512]{1,0:T(8,128)(2,1)S(1)}) custom-call(s32[1]{0:T(128)} %bitcast.far, bf16[384,8,384]{2,1,0:T(8,128)(2,1)S(1)} %bitcast.12, bf16[4,4,384,384]{3,2,1,0:T(8,128)(2,1)} %green_hbm.1, bf16[4,384,384]{2,1,0:T(8,128)(2,1)} %copy-done, ...), custom_call_target="tpu_custom_call" | custom-call | tf_op jit(solution)/shard_map/mix/pallas_call | solution.py:300
  101.1 36.7 %all_to_all.10.mixed = bf16[128,3,8,384]{3,2,1,0:T(8,128)(2,1)S(1)} all-to-all(bf16[128,3,8,384]{3,2,1,0:T(8,128)(2,1)S(1)} %bitcast.13), channel_id=1, replica_groups=mesh['zg'=2,'xy'=64] {'zg','xy'}, dimensions={0} | all-to-all | bytes 4718592 | tf_op jit(solution)/shard_map/all_to_all | solution.py:375
  137.8 4.0 %back.1 = f32[3,512,512]{2,1,0:T(8,128)} custom-call(bf16[128,3,8,384]{3,2,1,0:T(8,128)(2,1)S(1)} %all_to_all.10.mixed, bf16[256,1024]{1,0:T(8,128)(2,1)S(1)} %get-tuple-element.9.half_x, bf16[512,512]{1,0:T(8,128)(2,1)S(1)} %get-tuple-element.10.along_y), custom_call_target="tpu_custom_call" | custom-call | tf_op jit(solution)/shard_map/back/pallas_call | solution.py:352
Async XLA Ops:
  24.9 70.4 %all-to-all-start = ((bf16[128,3,8,384]{3,2,1,0:T(8,128)(2,1)}), bf16[128,3,8,384]{3,2,1,0:T(8,128)(2,1)S(1)}, u32[]{:S(2)}, u32[]{:S(2)}) async-start(bf16[128,3,8,384]{3,2,1,0:T(8,128)(2,1)} %front.1), calls=%async_computation | async-start | bytes 4718592 | tf_op jit(solution)/shard_map/all_to_all | solution.py:372
  38.8 56.4 %collective-permute-start = (bf16[4,384,384]{2,1,0:T(8,128)(2,1)}, bf16[4,384,384]{2,1,0:T(8,128)(2,1)S(1)}, u32[]{:S(2)}, u32[]{:S(2)}) collective-permute-start(bf16[4,384,384]{2,1,0:T(8,128)(2,1)} %slice_bitcast_fusion), channel_id=1, source_target_pairs={{0,127},{1,126},{2,125},{3,124},{4,123},{5,122},{6,121},{7,120},{8... | collective-permute-start | bytes 3538952 | tf_op jit(solution)/shard_map/ppermute | solution.py:370
  95.2 1.0 copy-start

commit v8 on v7

--- a/solution.py
+++ b/solution.py
@@ -82,7 +82,7 @@
 
 
 def front_kernel(
-    rows_hbm, cells_hbm, splines_hbm, charges_hbm, counts, yh_hbm, yl_hbm, eh_hbm, el_hbm, oh_hbm, ol_hbm, out_hbm, *scratch
+    row_table, cells_hbm, splines_hbm, charges_hbm, counts, yh_hbm, yl_hbm, eh_hbm, el_hbm, oh_hbm, ol_hbm, out_hbm, *scratch
 ):
     bins = scratch[:SPREAD]
     spikes = scratch[8:10]
@@ -96,9 +96,7 @@
     ]
     for copy in slot_copies:
         copy.start()
-    row_copies = [
-        pltpu.make_async_copy(rows_hbm.at[pl.ds(t * 1024, 1024)], row_of[t], row_sem.at[t]) for t in range(TILES)
-    ]
+    row_copies = [pltpu.make_async_copy(row_table.at[t], row_of[t], row_sem.at[t]) for t in range(TILES)]
     for copy in row_copies:
         copy.start()
     sources = (yh_hbm, yl_hbm, eh_hbm, el_hbm, oh_hbm, ol_hbm)
@@ -133,7 +131,7 @@
 
     def apply(spike, g):
         for t in range(TILES):
-            rows = [row_of[t][g + k * LANE] for k in range(SPREAD)]
+            rows = [row_of[t][k, g] for k in range(SPREAD)]
             sums = [bins[k][pl.ds(rows[k], 1), :] + spike[pl.ds(t * SPREAD + k, 1), :] for k in range(SPREAD)]
             for k in range(SPREAD):
                 bins[k][pl.ds(rows[k], 1), :] = sums[k]
@@ -209,14 +207,40 @@
         pltpu.make_async_copy(out.at[z], out_hbm.at[:, z], out_sem.at[z]).wait()
 
 
-def front(charges, cells, splines, counts, tabs):
+def prepare_kernel(green_hbm, cells_hbm, piece, rows, cells, sem):
+    copies = [
+        pltpu.make_async_copy(cells_hbm, cells, sem.at[0]),
+        pltpu.make_async_copy(green_hbm.at[NU - 1], piece, sem.at[1]),
+    ]
+    for copy in copies:
+        copy.start()
+    copies[0].wait()
+    for t in range(TILES):
+        rows[t] = lax.shift_right_logical(cells[:, t * LANE : (t + 1) * LANE], 7)
+    copies[1].wait()
+
+
+def prepare(green, cells):
+    hbm = pl.BlockSpec(memory_space=pltpu.HBM)
+    vmem = pl.BlockSpec(memory_space=pltpu.VMEM)
+    return pl.pallas_call(
+        prepare_kernel,
+        out_shape=(pltpu.VMEM(green.shape[1:], BF16), pltpu.VMEM((TILES, SPREAD, LANE), jnp.int32)),
+        in_specs=[hbm, hbm],
+        out_specs=(vmem, vmem),
+        scratch_shapes=[pltpu.VMEM((SPREAD, SLOTS), jnp.int32), pltpu.SemaphoreType.DMA((2,))],
+        compiler_params=pltpu.CompilerParams(vmem_limit_bytes=8 << 20),
+        name="prepare",
+    )(*in_hbm(green, cells))
+
+
+def front(rows, charges, cells, splines, counts, tabs):
     smem = pl.BlockSpec(memory_space=pltpu.SMEM)
     hbm = pl.BlockSpec(memory_space=pltpu.HBM)
-    rows = lax.shift_right_logical(cells, 7).reshape(SPREAD, TILES, LANE).transpose(1, 0, 2).reshape(-1)
     return pl.pallas_call(
         front_kernel,
         out_shape=pltpu.HBM((DEV, ZD, 2 * NU, WIDE), BF16),
-        in_specs=[hbm] * 4 + [smem] + [hbm] * 6,
+        in_specs=[pl.BlockSpec(memory_space=pltpu.VMEM)] + [hbm] * 3 + [smem] + [hbm] * 6,
         out_specs=hbm,
         scratch_shapes=[pltpu.VMEM((ROWS, LANE), F32)] * SPREAD
         + [pltpu.VMEM((LANE, LANE), F32)] * 2
@@ -227,10 +251,10 @@
         + [pltpu.VMEM((ZD, DEV, 2 * NU, WIDE), BF16)]
         + [pltpu.VMEM((SPREAD, SLOTS), jnp.int32), pltpu.VMEM((SPREAD, SLOTS), F32), pltpu.VMEM((1, SLOTS), F32)]
         + [pltpu.SemaphoreType.DMA((n,)) for n in (TILES, 6, ZD, 3)]
-        + [pltpu.SMEM((SPREAD * LANE,), jnp.int32)] * TILES,
+        + [pltpu.SMEM((SPREAD, LANE), jnp.int32)] * TILES,
         compiler_params=pltpu.CompilerParams(vmem_limit_bytes=44 << 20),
         name="front",
-    )(*in_hbm(rows, cells, splines, charges.reshape(1, SLOTS)), counts, *in_hbm(*tabs))
+    )(rows, *in_hbm(cells, splines, charges.reshape(1, SLOTS)), counts, *in_hbm(*tabs))
 
 
 WAVE = (0, 2, 1)
@@ -367,8 +391,9 @@
 
 def steps(charges, cells, splines, counts, green):
     forward = tuple(jnp.asarray(t) for t in forward_tables())
-    mirror = lax.ppermute(green[NU - 1], AXES, [(d, DEV - 1 - d) for d in range(DEV)])
-    spectrum = front(charges, cells, splines, counts, forward)
+    piece, rows = prepare(green, cells)
+    mirror = lax.ppermute(piece, AXES, [(d, DEV - 1 - d) for d in range(DEV)])
+    spectrum = front(rows, charges, cells, splines, counts, forward)
     pencil = lax.all_to_all(spectrum, AXES, split_axis=0, concat_axis=0, tiled=True)
     mixed, *along = mix(pencil, green, mirror, jnp.asarray(inverse_table()), forward[0])
     mixed = mixed.reshape(DEV, ZD, 2 * NU, WIDE)

time: 142 us -> 142 us (level)
  local copies, waits for them, and re-layouts: 3.43 us -> 0 us
  waiting for transfers between devices: 48.5 us -> 50.9 us
  Pallas kernels: 31.5 us -> 33.5 us
  other arithmetic: 1.47 us -> 0 us
    ppermute x1, waiting for transfers between devices: 48.5 us -> 50.9 us  [steps(): mirror = lax.ppermute(piece, AXES, [(d, DEV - 1 - d) for d in range(DEV)])]
    squeeze x1 -> x0, local copies, waits for them, and re-layouts: 2.41 us -> none  [steps(): green[NU - 1]]
    reshape x1 -> x0, other arithmetic: 1.47 us -> none  [front(): lax.shift_right_logical(cells, 7).reshape(SPREAD, TILES, LANE)]
  transfers between devices with their start and end apart: 2 -> 2, of which waited for: 1 -> 1; matrix products, arithmetic and copies ran while one was open for 2% -> 0% of each run, Pallas kernels for 0% -> 0%
where the time goes in v8:
time: 142 us
  waiting for transfers between devices  50.9 us (36%)
  blocking collectives  37 us (26%)
  Pallas kernels  33.5 us (24%)
  starting transfers between devices  19.5 us (14%)
    ppermute x1, waiting for transfers between devices, steps(): mirror = lax.ppermute(piece, AXES, [(d, DEV - 1 - d) for d in range(DEV)])  50.9 us
    all_to_all x1, blocking collectives, steps(): lax.all_to_all(mixed, AXES, split_axis=0, concat_axis=0, tiled=True)  37 us
    pallas_call x1, Pallas kernels, front(): pl.pallas_call(front_kernel, out_shape=pltpu.HBM((DEV, ZD, 2 * NU, WIDE),...  23.3 us
    all_to_all x1, starting transfers between devices, steps(): lax.all_to_all(spectrum, AXES, split_axis=0, concat_axis=0, tiled=True)  11.5 us
    ppermute x1, starting transfers between devices, steps(): mirror = lax.ppermute(piece, AXES, [(d, DEV - 1 - d) for d in range(DEV)])  8.05 us
    pallas_call x1, Pallas kernels, mix(): pl.pallas_call(green_kernel, out_shape=(pltpu.VMEM((NZ, 2 * NU, WIDE), BF...  4.87 us
    pallas_call x1, Pallas kernels, back(): pl.pallas_call(back_kernel, out_shape=jax.ShapeDtypeStruct((ZD, NX, NY),...  3.96 us
  transfers between devices with their start and end apart: 2, of which 1 were waited for; matrix products, arithmetic and copies ran while one was open for 0% of the time, Pallas kernels for 0%

profile of v8, /device:TPU:1, one launch (start us, length us, event | category | flops | bytes accessed | tf_op | source)
XLA Modules:
  0.0 141.6 jit_solution(16771736718131986351)
XLA Ops:
  0.7 1.3 prepare.1
  2.0 23.3 %front.1 = bf16[128,3,8,384]{3,2,1,0:T(8,128)(2,1)} custom-call(s32[16,8,128]{2,1,0:T(8,128)S(1)} %get-tuple-element.10.row_table, s32[8,2048]{1,0:T(8,128)} %cells_hbm.3, f32[8,2048]{1,0:T(8,128)} %splines_hbm.1, f32[1,2048]{1,0:T(1,128)} %bitcast.6, s32[1]{0:T(128)S(6)} %copy.13.counts, bf16[512,512]{1,0:T(8,128)(2,1)} %constant.20.clone.yh_hbm.y_hbm, ...), custom_call_target="tpu_custom_call" | custom-call | tf_op jit(solution)/shard_map/front/pallas_call | solution.py:240
  25.3 11.5 %all-to-all-start = ((bf16[128,3,8,384]{3,2,1,0:T(8,128)(2,1)}), bf16[128,3,8,384]{3,2,1,0:T(8,128)(2,1)S(1)}, u32[]{:S(2)}, u32[]{:S(2)}) async-start(bf16[128,3,8,384]{3,2,1,0:T(8,128)(2,1)} %front.1), calls=%async_computation | async-start | bytes 4718592 | tf_op jit(solution)/shard_map/all_to_all | solution.py:397
  36.8 8.1 %collective-permute-start = (bf16[4,384,384]{2,1,0:T(8,128)(2,1)S(1)}, bf16[4,384,384]{2,1,0:T(8,128)(2,1)}, u32[]{:S(2)}, u32[]{:S(2)}) collective-permute-start(bf16[4,384,384]{2,1,0:T(8,128)(2,1)S(1)} %get-tuple-element.11), channel_id=1, source_target_pairs={{0,127},{1,126},{2,125},{3,124},{4,123},{5,122},{6,121},{7,120},{8... | collective-permute-start | bytes 3538952 | tf_op jit(solution)/shard_map/ppermute | solution.py:395
  44.9 50.9 %collective-permute-done.mirror_hbm = bf16[4,384,384]{2,1,0:T(8,128)(2,1)} collective-permute-done((bf16[4,384,384]{2,1,0:T(8,128)(2,1)S(1)}, bf16[4,384,384]{2,1,0:T(8,128)(2,1)}, u32[]{:S(2)}, u32[]{:S(2)}) %collective-permute-start) | collective-permute-done | bytes 1179680 | tf_op jit(solution)/shard_map/ppermute | solution.py:395
  95.8 0.0 all-to-all-done
  95.8 4.9 %mix.1 = (bf16[384,8,384]{2,1,0:T(8,128)(2,1)S(1)}, bf16[256,1024]{1,0:T(8,128)(2,1)S(1)}, bf16[512,512]{1,0:T(8,128)(2,1)S(1)}) custom-call(s32[1]{0:T(128)} %bitcast.far, bf16[384,8,384]{2,1,0:T(8,128)(2,1)S(1)} %bitcast.4, bf16[4,4,384,384]{3,2,1,0:T(8,128)(2,1)} %green_hbm.3, bf16[4,384,384]{2,1,0:T(8,128)(2,1)} %collective-permute-done.mirror_hbm, ...), custom_call_target="tpu_custom_call" | custom-call | tf_op jit(solution)/shard_map/mix/pallas_call | solution.py:324
  100.6 37.0 %all_to_all.10.mixed = bf16[128,3,8,384]{3,2,1,0:T(8,128)(2,1)S(1)} all-to-all(bf16[128,3,8,384]{3,2,1,0:T(8,128)(2,1)S(1)} %bitcast.5), channel_id=1, replica_groups=mesh['zg'=2,'xy'=64] {'zg','xy'}, dimensions={0} | all-to-all | bytes 4718592 | tf_op jit(solution)/shard_map/all_to_all | solution.py:400
  137.6 4.0 %back.1 = f32[3,512,512]{2,1,0:T(8,128)} custom-call(bf16[128,3,8,384]{3,2,1,0:T(8,128)(2,1)S(1)} %all_to_all.10.mixed, bf16[256,1024]{1,0:T(8,128)(2,1)S(1)} %get-tuple-element.13.half_x, bf16[512,512]{1,0:T(8,128)(2,1)S(1)} %get-tuple-element.14.along_y), custom_call_target="tpu_custom_call" | custom-call | tf_op jit(solution)/shard_map/back/pallas_call | solution.py:376
Async XLA Ops:
  25.3 70.4 %all-to-all-start = ((bf16[128,3,8,384]{3,2,1,0:T(8,128)(2,1)}), bf16[128,3,8,384]{3,2,1,0:T(8,128)(2,1)S(1)}, u32[]{:S(2)}, u32[]{:S(2)}) async-start(bf16[128,3,8,384]{3,2,1,0:T(8,128)(2,1)} %front.1), calls=%async_computation | async-start | bytes 4718592 | tf_op jit(solution)/shard_map/all_to_all | solution.py:397
  36.8 59.0 %collective-permute-start = (bf16[4,384,384]{2,1,0:T(8,128)(2,1)S(1)}, bf16[4,384,384]{2,1,0:T(8,128)(2,1)}, u32[]{:S(2)}, u32[]{:S(2)}) collective-permute-start(bf16[4,384,384]{2,1,0:T(8,128)(2,1)S(1)} %get-tuple-element.11), channel_id=1, source_target_pairs={{0,127},{1,126},{2,125},{3,124},{4,123},{5,122},{6,121},{7,120},{8... | collective-permute-start | bytes 3538952 | tf_op jit(solution)/shard_map/ppermute | solution.py:395

commit v9 on v8

--- a/solution.py
+++ b/solution.py
@@ -158,7 +158,7 @@
     def plane(z, carry):
         for j in range(NY // LANE):
             for q in range(4):
-                at = pl.ds(z * (NX * 4) + q * 512 + j, 128, stride=4)
+                at = pl.ds(j * (ROWS // 4) + z * NX + q * 128, 128)
                 total = bins[0][at, :]
                 for b in bins[1:]:
                     total = total + b[at, :]
@@ -216,7 +216,8 @@
         copy.start()
     copies[0].wait()
     for t in range(TILES):
-        rows[t] = lax.shift_right_logical(cells[:, t * LANE : (t + 1) * LANE], 7)
+        row = lax.shift_right_logical(cells[:, t * LANE : (t + 1) * LANE], 7)
+        rows[t] = (row & 3) * (ROWS // 4) + lax.shift_right_logical(row, 2)
     copies[1].wait()
 
 

time: 142 us -> 142 us (level)
  no operation moved by 1% of the time
where the time goes in v9:
time: 142 us; the launch traced here: 141 us
  waiting for transfers between devices  50.9 us (36%)
  blocking collectives  37 us (26%)
  Pallas kernels  33.2 us (23%)
  starting transfers between devices  19.6 us (14%)
    ppermute x1, waiting for transfers between devices, steps(): mirror = lax.ppermute(piece, AXES, [(d, DEV - 1 - d) for d in range(DEV)])  50.9 us
    all_to_all x1, blocking collectives, steps(): lax.all_to_all(mixed, AXES, split_axis=0, concat_axis=0, tiled=True)  37 us
    pallas_call x1, Pallas kernels, front(): pl.pallas_call(front_kernel, out_shape=pltpu.HBM((DEV, ZD, 2 * NU, WIDE),...  23 us
    all_to_all x1, starting transfers between devices, steps(): lax.all_to_all(spectrum, AXES, split_axis=0, concat_axis=0, tiled=True)  11.5 us
    ppermute x1, starting transfers between devices, steps(): mirror = lax.ppermute(piece, AXES, [(d, DEV - 1 - d) for d in range(DEV)])  8.05 us
    pallas_call x1, Pallas kernels, mix(): pl.pallas_call(green_kernel, out_shape=(pltpu.VMEM((NZ, 2 * NU, WIDE), BF...  4.86 us
    pallas_call x1, Pallas kernels, back(): pl.pallas_call(back_kernel, out_shape=jax.ShapeDtypeStruct((ZD, NX, NY),...  3.96 us
  transfers between devices with their start and end apart: 2, of which 1 were waited for; matrix products, arithmetic and copies ran while one was open for 0% of the time, Pallas kernels for 0%

profile of v9, /device:TPU:1, one launch (start us, length us, event | category | flops | bytes accessed | tf_op | source)
XLA Modules:
  0.0 141.3 jit_solution(13588016285782701655)
XLA Ops:
  0.7 1.3 prepare.1
  2.0 23.0 %front.1 = bf16[128,3,8,384]{3,2,1,0:T(8,128)(2,1)} custom-call(s32[16,8,128]{2,1,0:T(8,128)S(1)} %get-tuple-element.10.row_table, s32[8,2048]{1,0:T(8,128)} %cells_hbm.3, f32[8,2048]{1,0:T(8,128)} %splines_hbm.1, f32[1,2048]{1,0:T(1,128)} %bitcast.6, s32[1]{0:T(128)S(6)} %copy.13.counts, bf16[512,512]{1,0:T(8,128)(2,1)} %constant.20.clone.yh_hbm.y_hbm, ...), custom_call_target="tpu_custom_call" | custom-call | tf_op jit(solution)/shard_map/front/pallas_call | solution.py:241
  25.0 11.5 %all-to-all-start = ((bf16[128,3,8,384]{3,2,1,0:T(8,128)(2,1)}), bf16[128,3,8,384]{3,2,1,0:T(8,128)(2,1)S(1)}, u32[]{:S(2)}, u32[]{:S(2)}) async-start(bf16[128,3,8,384]{3,2,1,0:T(8,128)(2,1)} %front.1), calls=%async_computation | async-start | bytes 4718592 | tf_op jit(solution)/shard_map/all_to_all | solution.py:398
  36.6 8.1 %collective-permute-start = (bf16[4,384,384]{2,1,0:T(8,128)(2,1)S(1)}, bf16[4,384,384]{2,1,0:T(8,128)(2,1)}, u32[]{:S(2)}, u32[]{:S(2)}) collective-permute-start(bf16[4,384,384]{2,1,0:T(8,128)(2,1)S(1)} %get-tuple-element.11), channel_id=1, source_target_pairs={{0,127},{1,126},{2,125},{3,124},{4,123},{5,122},{6,121},{7,120},{8... | collective-permute-start | bytes 3538952 | tf_op jit(solution)/shard_map/ppermute | solution.py:396
  44.6 50.9 %collective-permute-done.mirror_hbm = bf16[4,384,384]{2,1,0:T(8,128)(2,1)} collective-permute-done((bf16[4,384,384]{2,1,0:T(8,128)(2,1)S(1)}, bf16[4,384,384]{2,1,0:T(8,128)(2,1)}, u32[]{:S(2)}, u32[]{:S(2)}) %collective-permute-start) | collective-permute-done | bytes 1179680 | tf_op jit(solution)/shard_map/ppermute | solution.py:396
  95.5 0.0 all-to-all-done
  95.5 4.9 %mix.1 = (bf16[384,8,384]{2,1,0:T(8,128)(2,1)S(1)}, bf16[256,1024]{1,0:T(8,128)(2,1)S(1)}, bf16[512,512]{1,0:T(8,128)(2,1)S(1)}) custom-call(s32[1]{0:T(128)} %bitcast.far, bf16[384,8,384]{2,1,0:T(8,128)(2,1)S(1)} %bitcast.4, bf16[4,4,384,384]{3,2,1,0:T(8,128)(2,1)} %green_hbm.3, bf16[4,384,384]{2,1,0:T(8,128)(2,1)} %collective-permute-done.mirror_hbm, ...), custom_call_target="tpu_custom_call" | custom-call | tf_op jit(solution)/shard_map/mix/pallas_call | solution.py:325
  100.4 37.0 %all_to_all.10.mixed = bf16[128,3,8,384]{3,2,1,0:T(8,128)(2,1)S(1)} all-to-all(bf16[128,3,8,384]{3,2,1,0:T(8,128)(2,1)S(1)} %bitcast.5), channel_id=1, replica_groups=mesh['zg'=2,'xy'=64] {'zg','xy'}, dimensions={0} | all-to-all | bytes 4718592 | tf_op jit(solution)/shard_map/all_to_all | solution.py:401
  137.4 4.0 %back.1 = f32[3,512,512]{2,1,0:T(8,128)} custom-call(bf16[128,3,8,384]{3,2,1,0:T(8,128)(2,1)S(1)} %all_to_all.10.mixed, bf16[256,1024]{1,0:T(8,128)(2,1)S(1)} %get-tuple-element.13.half_x, bf16[512,512]{1,0:T(8,128)(2,1)S(1)} %get-tuple-element.14.along_y), custom_call_target="tpu_custom_call" | custom-call | tf_op jit(solution)/shard_map/back/pallas_call | solution.py:377
Async XLA Ops:
  25.0 70.5 %all-to-all-start = ((bf16[128,3,8,384]{3,2,1,0:T(8,128)(2,1)}), bf16[128,3,8,384]{3,2,1,0:T(8,128)(2,1)S(1)}, u32[]{:S(2)}, u32[]{:S(2)}) async-start(bf16[128,3,8,384]{3,2,1,0:T(8,128)(2,1)} %front.1), calls=%async_computation | async-start | bytes 4718592 | tf_op jit(solution)/shard_map/all_to_all | solution.py:398
  36.6 59.0 %collective-permute-start = (bf16[4,384,384]{2,1,0:T(8,128)(2,1)S(1)}, bf16[4,384,384]{2,1,0:T(8,128)(2,1)}, u32[]{:S(2)}, u32[]{:S(2)}) collective-permute-start(bf16[4,384,384]{2,1,0:T(8,128)(2,1)S(1)} %get-tuple-element.11), channel_id=1, source_target_pairs={{0,127},{1,126},{2,125},{3,124},{4,123},{5,122},{6,121},{7,120},{8... | collective-permute-start | bytes 3538952 | tf_op jit(solution)/shard_map/ppermute | solution.py:396

commit v10 on v9

--- a/solution.py
+++ b/solution.py
@@ -266,7 +266,7 @@
 
 
 def green_kernel(
-    far, spectrum, green_hbm, mirror_hbm, x_hbm, y_hbm, out, x_out, y_out, green, flat, sums, swapped, green_sem, *rhs
+    spectrum, green_hbm, mirror_hbm, x_hbm, y_hbm, out, x_out, y_out, green, flat, sums, swapped, green_sem, *rhs
 ):
     sources = [green_hbm.at[w] for w in WAVE] + [mirror_hbm]
     fetches = [pltpu.make_async_copy(s, green.at[i], green_sem.at[i]) for i, s in enumerate(sources)]
@@ -274,7 +274,8 @@
     fetches.append(pltpu.make_async_copy(y_hbm, y_out, green_sem.at[5]))
     for fetch in fetches:
         fetch.start()
-    at = [jnp.bitwise_xor(row, 2 * far[0]) for row in range(NU)]
+    far = lax.axis_index("zg")
+    at = [jnp.bitwise_xor(row, 2 * far) for row in range(NU)]
     for j in range(3):
         flat[...] = spectrum[:, :, j * LANE : (j + 1) * LANE].astype(F32).reshape(NZ * 2 * NU, LANE)
         for row in range(NU):
@@ -325,7 +326,7 @@
     return pl.pallas_call(
         green_kernel,
         out_shape=(pltpu.VMEM((NZ, 2 * NU, WIDE), BF16), *(pltpu.VMEM(t.shape, BF16) for t in tabs)),
-        in_specs=[pl.BlockSpec(memory_space=pltpu.SMEM), vmem, hbm, hbm, hbm, hbm],
+        in_specs=[vmem, hbm, hbm, hbm, hbm],
         out_specs=(vmem, vmem, vmem),
         compiler_params=pltpu.CompilerParams(vmem_limit_bytes=36 << 20),
         scratch_shapes=[
@@ -337,7 +338,7 @@
         ]
         + [pltpu.VMEM((KYB, NZ, 2 * LANE), BF16)] * 3,
         name="mix",
-    )(lax.axis_index("zg").astype(jnp.int32).reshape(1), pencil.reshape(NZ, 2 * NU, WIDE), *in_hbm(green, mirror, *tabs))
+    )(pencil.reshape(NZ, 2 * NU, WIDE), *in_hbm(green, mirror, *tabs))
 
 
 def back_kernel(mixed, half_x, along_y, out_hbm, far_x, out, rest, out_sem):

time: 142 us -> 142 us (level)
  no operation moved by 1% of the time
where the time goes in v10:
time: 142 us; the launch traced here: 141 us
  waiting for transfers between devices  50.9 us (36%)
  blocking collectives  37 us (26%)
  Pallas kernels  33.2 us (23%)
  starting transfers between devices  19.6 us (14%)
    ppermute x1, waiting for transfers between devices, steps(): mirror = lax.ppermute(piece, AXES, [(d, DEV - 1 - d) for d in range(DEV)])  50.9 us
    all_to_all x1, blocking collectives, steps(): lax.all_to_all(mixed, AXES, split_axis=0, concat_axis=0, tiled=True)  37 us
    pallas_call x1, Pallas kernels, front(): pl.pallas_call(front_kernel, out_shape=pltpu.HBM((DEV, ZD, 2 * NU, WIDE),...  23 us
    all_to_all x1, starting transfers between devices, steps(): lax.all_to_all(spectrum, AXES, split_axis=0, concat_axis=0, tiled=True)  11.5 us
    ppermute x1, starting transfers between devices, steps(): mirror = lax.ppermute(piece, AXES, [(d, DEV - 1 - d) for d in range(DEV)])  8.05 us
    pallas_call x1, Pallas kernels, mix(): pl.pallas_call(green_kernel, out_shape=(pltpu.VMEM((NZ, 2 * NU, WIDE), BF...  4.87 us
    pallas_call x1, Pallas kernels, back(): pl.pallas_call(back_kernel, out_shape=jax.ShapeDtypeStruct((ZD, NX, NY),...  3.96 us
  transfers between devices with their start and end apart: 2, of which 1 were waited for; matrix products, arithmetic and copies ran while one was open for 0% of the time, Pallas kernels for 0%

profile of v10, /device:TPU:1, one launch (start us, length us, event | category | flops | bytes accessed | tf_op | source)
XLA Modules:
  0.0 141.3 jit_solution(15673293800925690355)
XLA Ops:
  0.7 1.3 prepare.1
  2.0 23.0 %front.1 = bf16[128,3,8,384]{3,2,1,0:T(8,128)(2,1)} custom-call(s32[16,8,128]{2,1,0:T(8,128)S(1)} %get-tuple-element.10.row_table, s32[8,2048]{1,0:T(8,128)} %cells_hbm.3, f32[8,2048]{1,0:T(8,128)} %splines_hbm.1, f32[1,2048]{1,0:T(1,128)} %bitcast.5, s32[1]{0:T(128)S(6)} %copy.13.counts, bf16[512,512]{1,0:T(8,128)(2,1)} %constant.14.clone.yh_hbm.y_hbm, ...), custom_call_target="tpu_custom_call" | custom-call | tf_op jit(solution)/shard_map/front/pallas_call | solution.py:241
  25.0 11.5 %all-to-all-start = ((bf16[128,3,8,384]{3,2,1,0:T(8,128)(2,1)}), bf16[128,3,8,384]{3,2,1,0:T(8,128)(2,1)S(1)}, u32[]{:S(2)}, u32[]{:S(2)}) async-start(bf16[128,3,8,384]{3,2,1,0:T(8,128)(2,1)} %front.1), calls=%async_computation | async-start | bytes 4718592 | tf_op jit(solution)/shard_map/all_to_all | solution.py:399
  36.6 8.1 %collective-permute-start = (bf16[4,384,384]{2,1,0:T(8,128)(2,1)S(1)}, bf16[4,384,384]{2,1,0:T(8,128)(2,1)}, u32[]{:S(2)}, u32[]{:S(2)}) collective-permute-start(bf16[4,384,384]{2,1,0:T(8,128)(2,1)S(1)} %get-tuple-element.11), channel_id=1, source_target_pairs={{0,127},{1,126},{2,125},{3,124},{4,123},{5,122},{6,121},{7,120},{8... | collective-permute-start | bytes 3538952 | tf_op jit(solution)/shard_map/ppermute | solution.py:397
  44.6 50.9 %collective-permute-done.mirror_hbm = bf16[4,384,384]{2,1,0:T(8,128)(2,1)} collective-permute-done((bf16[4,384,384]{2,1,0:T(8,128)(2,1)S(1)}, bf16[4,384,384]{2,1,0:T(8,128)(2,1)}, u32[]{:S(2)}, u32[]{:S(2)}) %collective-permute-start) | collective-permute-done | bytes 1179680 | tf_op jit(solution)/shard_map/ppermute | solution.py:397
  95.5 0.0 all-to-all-done
  95.5 4.9 %mix.1 = (bf16[384,8,384]{2,1,0:T(8,128)(2,1)S(1)}, bf16[256,1024]{1,0:T(8,128)(2,1)S(1)}, bf16[512,512]{1,0:T(8,128)(2,1)S(1)}) custom-call(bf16[384,8,384]{2,1,0:T(8,128)(2,1)S(1)} %bitcast.3, bf16[4,4,384,384]{3,2,1,0:T(8,128)(2,1)} %green_hbm.3, bf16[4,384,384]{2,1,0:T(8,128)(2,1)} %collective-permute-done.mirror_hbm, ...), custom_call_target="tpu_custom_call" | custom-call | tf_op jit(solution)/shard_map/mix/pallas_call | solution.py:326
  100.4 37.0 %all_to_all.10.mixed = bf16[128,3,8,384]{3,2,1,0:T(8,128)(2,1)S(1)} all-to-all(bf16[128,3,8,384]{3,2,1,0:T(8,128)(2,1)S(1)} %bitcast.4), channel_id=1, replica_groups=mesh['zg'=2,'xy'=64] {'zg','xy'}, dimensions={0} | all-to-all | bytes 4718592 | tf_op jit(solution)/shard_map/all_to_all | solution.py:402
  137.4 4.0 %back.1 = f32[3,512,512]{2,1,0:T(8,128)} custom-call(bf16[128,3,8,384]{3,2,1,0:T(8,128)(2,1)S(1)} %all_to_all.10.mixed, bf16[256,1024]{1,0:T(8,128)(2,1)S(1)} %get-tuple-element.13.half_x, bf16[512,512]{1,0:T(8,128)(2,1)S(1)} %get-tuple-element.14.along_y), custom_call_target="tpu_custom_call" | custom-call | tf_op jit(solution)/shard_map/back/pallas_call | solution.py:378
Async XLA Ops:
  25.0 70.5 %all-to-all-start = ((bf16[128,3,8,384]{3,2,1,0:T(8,128)(2,1)}), bf16[128,3,8,384]{3,2,1,0:T(8,128)(2,1)S(1)}, u32[]{:S(2)}, u32[]{:S(2)}) async-start(bf16[128,3,8,384]{3,2,1,0:T(8,128)(2,1)} %front.1), calls=%async_computation | async-start | bytes 4718592 | tf_op jit(solution)/shard_map/all_to_all | solution.py:399
  36.6 59.0 %collective-permute-start = (bf16[4,384,384]{2,1,0:T(8,128)(2,1)S(1)}, bf16[4,384,384]{2,1,0:T(8,128)(2,1)}, u32[]{:S(2)}, u32[]{:S(2)}) collective-permute-start(bf16[4,384,384]{2,1,0:T(8,128)(2,1)S(1)} %get-tuple-element.11), channel_id=1, source_target_pairs={{0,127},{1,126},{2,125},{3,124},{4,123},{5,122},{6,121},{7,120},{8... | collective-permute-start | bytes 3538952 | tf_op jit(solution)/shard_map/ppermute | solution.py:397

commit v11 on v10

--- a/solution.py
+++ b/solution.py
@@ -154,6 +154,10 @@
     first = lax.broadcasted_iota(jnp.int32, (NX, LANE), 1) == 0
     lower = lax.broadcasted_iota(jnp.int32, (NX, LANE), 0) % NU < 2
     row_of_tile = lax.broadcasted_iota(jnp.int32, (DEV // 2, 2 * NU, LANE), 1) % NU
+
+    def send(z, side):
+        devices = pl.ds(side * (DEV // 2), DEV // 2)
+        return pltpu.make_async_copy(out.at[z, devices], out_hbm.at[devices, z], out_sem.at[2 * z + side])
 
     def plane(z, carry):
         for j in range(NY // LANE):
@@ -199,12 +203,13 @@
                 out[z, side * (DEV // 2) : (side + 1) * (DEV // 2), :, j * LANE : (j + 1) * LANE] = jnp.where(
                     row_of_tile == spare, moved, groups[j].reshape(shape)
                 ).astype(BF16)
-        pltpu.make_async_copy(out.at[z], out_hbm.at[:, z], out_sem.at[z]).start()
+            send(z, side).start()
         return carry
 
     lax.fori_loop(0, ZD, plane, 0)
     for z in range(ZD):
-        pltpu.make_async_copy(out.at[z], out_hbm.at[:, z], out_sem.at[z]).wait()
+        for side in range(2):
+            send(z, side).wait()
 
 
 def prepare_kernel(green_hbm, cells_hbm, piece, rows, cells, sem):
@@ -251,7 +256,7 @@
         + [pltpu.VMEM(t.shape, BF16) for t in tabs]
         + [pltpu.VMEM((ZD, DEV, 2 * NU, WIDE), BF16)]
         + [pltpu.VMEM((SPREAD, SLOTS), jnp.int32), pltpu.VMEM((SPREAD, SLOTS), F32), pltpu.VMEM((1, SLOTS), F32)]
-        + [pltpu.SemaphoreType.DMA((n,)) for n in (TILES, 6, ZD, 3)]
+        + [pltpu.SemaphoreType.DMA((n,)) for n in (TILES, 6, 2 * ZD, 3)]
         + [pltpu.SMEM((SPREAD, LANE), jnp.int32)] * TILES,
         compiler_params=pltpu.CompilerParams(vmem_limit_bytes=44 << 20),
         name="front",

time: 142 us -> 142 us (level)
  no operation moved by 1% of the time
where the time goes in v11:
time: 142 us; the launch traced here: 141 us
  waiting for transfers between devices  50.9 us (36%)
  blocking collectives  37 us (26%)
  Pallas kernels  33.2 us (23%)
  starting transfers between devices  19.6 us (14%)
    ppermute x1, waiting for transfers between devices, steps(): mirror = lax.ppermute(piece, AXES, [(d, DEV - 1 - d) for d in range(DEV)])  50.9 us
    all_to_all x1, blocking collectives, steps(): lax.all_to_all(mixed, AXES, split_axis=0, concat_axis=0, tiled=True)  37 us
    pallas_call x1, Pallas kernels, front(): pl.pallas_call(front_kernel, out_shape=pltpu.HBM((DEV, ZD, 2 * NU, WIDE),...  23.1 us
    all_to_all x1, starting transfers between devices, steps(): lax.all_to_all(spectrum, AXES, split_axis=0, concat_axis=0, tiled=True)  11.5 us
    ppermute x1, starting transfers between devices, steps(): mirror = lax.ppermute(piece, AXES, [(d, DEV - 1 - d) for d in range(DEV)])  8.05 us
    pallas_call x1, Pallas kernels, mix(): pl.pallas_call(green_kernel, out_shape=(pltpu.VMEM((NZ, 2 * NU, WIDE), BF...  4.87 us
    pallas_call x1, Pallas kernels, back(): pl.pallas_call(back_kernel, out_shape=jax.ShapeDtypeStruct((ZD, NX, NY),...  3.96 us
  transfers between devices with their start and end apart: 2, of which 1 were waited for; matrix products, arithmetic and copies ran while one was open for 0% of the time, Pallas kernels for 0%

profile of v11, /device:TPU:1, one launch (start us, length us, event | category | flops | bytes accessed | tf_op | source)
XLA Modules:
  0.0 141.4 jit_solution(16893764459259784581)
XLA Ops:
  0.7 1.3 prepare.1
  2.0 23.1 %front.1 = bf16[128,3,8,384]{3,2,1,0:T(8,128)(2,1)} custom-call(s32[16,8,128]{2,1,0:T(8,128)S(1)} %get-tuple-element.10.row_table, s32[8,2048]{1,0:T(8,128)} %cells_hbm.3, f32[8,2048]{1,0:T(8,128)} %splines_hbm.1, f32[1,2048]{1,0:T(1,128)} %bitcast.5, s32[1]{0:T(128)S(6)} %copy.13.counts, bf16[512,512]{1,0:T(8,128)(2,1)} %constant.14.clone.yh_hbm.y_hbm, ...), custom_call_target="tpu_custom_call" | custom-call | tf_op jit(solution)/shard_map/front/pallas_call | solution.py:246
  25.1 11.5 %all-to-all-start = ((bf16[128,3,8,384]{3,2,1,0:T(8,128)(2,1)}), bf16[128,3,8,384]{3,2,1,0:T(8,128)(2,1)S(1)}, u32[]{:S(2)}, u32[]{:S(2)}) async-start(bf16[128,3,8,384]{3,2,1,0:T(8,128)(2,1)} %front.1), calls=%async_computation | async-start | bytes 4718592 | tf_op jit(solution)/shard_map/all_to_all | solution.py:404
  36.6 8.1 %collective-permute-start = (bf16[4,384,384]{2,1,0:T(8,128)(2,1)S(1)}, bf16[4,384,384]{2,1,0:T(8,128)(2,1)}, u32[]{:S(2)}, u32[]{:S(2)}) collective-permute-start(bf16[4,384,384]{2,1,0:T(8,128)(2,1)S(1)} %get-tuple-element.11), channel_id=1, source_target_pairs={{0,127},{1,126},{2,125},{3,124},{4,123},{5,122},{6,121},{7,120},{8... | collective-permute-start | bytes 3538952 | tf_op jit(solution)/shard_map/ppermute | solution.py:402
  44.6 50.9 %collective-permute-done.mirror_hbm = bf16[4,384,384]{2,1,0:T(8,128)(2,1)} collective-permute-done((bf16[4,384,384]{2,1,0:T(8,128)(2,1)S(1)}, bf16[4,384,384]{2,1,0:T(8,128)(2,1)}, u32[]{:S(2)}, u32[]{:S(2)}) %collective-permute-start) | collective-permute-done | bytes 1179680 | tf_op jit(solution)/shard_map/ppermute | solution.py:402
  95.5 0.0 all-to-all-done
  95.5 4.9 %mix.1 = (bf16[384,8,384]{2,1,0:T(8,128)(2,1)S(1)}, bf16[256,1024]{1,0:T(8,128)(2,1)S(1)}, bf16[512,512]{1,0:T(8,128)(2,1)S(1)}) custom-call(bf16[384,8,384]{2,1,0:T(8,128)(2,1)S(1)} %bitcast.3, bf16[4,4,384,384]{3,2,1,0:T(8,128)(2,1)} %green_hbm.3, bf16[4,384,384]{2,1,0:T(8,128)(2,1)} %collective-permute-done.mirror_hbm, ...), custom_call_target="tpu_custom_call" | custom-call | tf_op jit(solution)/shard_map/mix/pallas_call | solution.py:331
  100.4 37.0 %all_to_all.10.mixed = bf16[128,3,8,384]{3,2,1,0:T(8,128)(2,1)S(1)} all-to-all(bf16[128,3,8,384]{3,2,1,0:T(8,128)(2,1)S(1)} %bitcast.4), channel_id=1, replica_groups=mesh['zg'=2,'xy'=64] {'zg','xy'}, dimensions={0} | all-to-all | bytes 4718592 | tf_op jit(solution)/shard_map/all_to_all | solution.py:407
  137.4 4.0 %back.1 = f32[3,512,512]{2,1,0:T(8,128)} custom-call(bf16[128,3,8,384]{3,2,1,0:T(8,128)(2,1)S(1)} %all_to_all.10.mixed, bf16[256,1024]{1,0:T(8,128)(2,1)S(1)} %get-tuple-element.13.half_x, bf16[512,512]{1,0:T(8,128)(2,1)S(1)} %get-tuple-element.14.along_y), custom_call_target="tpu_custom_call" | custom-call | tf_op jit(solution)/shard_map/back/pallas_call | solution.py:383
Async XLA Ops:
  25.1 70.5 %all-to-all-start = ((bf16[128,3,8,384]{3,2,1,0:T(8,128)(2,1)}), bf16[128,3,8,384]{3,2,1,0:T(8,128)(2,1)S(1)}, u32[]{:S(2)}, u32[]{:S(2)}) async-start(bf16[128,3,8,384]{3,2,1,0:T(8,128)(2,1)} %front.1), calls=%async_computation | async-start | bytes 4718592 | tf_op jit(solution)/shard_map/all_to_all | solution.py:404
  36.6 59.0 %collective-permute-start = (bf16[4,384,384]{2,1,0:T(8,128)(2,1)S(1)}, bf16[4,384,384]{2,1,0:T(8,128)(2,1)}, u32[]{:S(2)}, u32[]{:S(2)}) collective-permute-start(bf16[4,384,384]{2,1,0:T(8,128)(2,1)S(1)} %get-tuple-element.11), channel_id=1, source_target_pairs={{0,127},{1,126},{2,125},{3,124},{4,123},{5,122},{6,121},{7,120},{8... | collective-permute-start | bytes 3538952 | tf_op jit(solution)/shard_map/ppermute | solution.py:402
